TPU v7x, 32 devices: a whole 2x2x4 slice. The times are simulated.
32 devices in a mesh: rows: 4 (over y, x), wide: 8 (over z, core).
Axes of the slice: x: 2, y: 2, z: 4, core: 2. Of those that a mesh axis runs over, the one named last changes fastest.
Arguments:
- tokens: bfloat16 [16, 1024, 1024], P('rows', 'wide'), may hold values from -6 to 6
- segments: int32 [16, 1024], P('rows'), may hold values from 0 to 15, never falling along the last dimension, each value on 1 to 128 neighbouring positions
- w_qkv: bfloat16 [2, 1024, 3072], replicated, may hold values from -0.1875 to 0.1875
- b_qkv: float32 [2, 3072], replicated, may hold values from -3 to 3
- w_out: bfloat16 [2, 1024, 1024], replicated, may hold values from -1 to 1
- b_out: float32 [2, 1024], replicated, may hold values from -3 to 3
- norm_gain: float32 [2, 2, 1024], replicated, may hold values from 0.5 to 1.5
- norm_bias: float32 [2, 2, 1024], replicated, may hold values from -2 to 2
- w_up: bfloat16 [2, 4096, 1024], P(None, 'wide'), may hold values from -0.1875 to 0.1875
- b_up: bfloat16 [2, 4096], P(None, 'wide'), may hold values from -3 to 3
- w_down: bfloat16 [2, 4096, 1024], P(None, 'wide'), may hold values from -0.09375 to 0.09375
- b_down: float32 [2, 1024], replicated, may hold values from -2 to 2
- prefix: bfloat16 [2, 2, 64, 1024], replicated, may hold values from -6 to 6
- cotangent: bfloat16 [16, 1024, 1024], P('rows', 'wide'), may hold values from -6 to 6
Outputs:
- output: bfloat16 [16, 1024, 1024], P('rows', 'wide')
- grad_tokens: float32 [16, 1024, 1024], P('rows', 'wide')
- grad_prefix: float32 [2, 2, 64, 1024], replicated
Inputs may be any that keep to these rules, and one draw needn't show every extreme that they name: `segments`: along each row the pair ids never fall, each pair covers 1 to 128 consecutive positions, and some pair covers exactly 128.
All inputs are finite; a program needn't handle non-finite values.
Results may differ from a plain program's by a relative error of at most 0.02.
Values may be sent and summed in bfloat16 or wider, within the bound.
A program may use at most 320 MiB of HBM per device.

v0:
```python
import math

import jax
import jax.numpy as jnp
from jax import lax
from jax.sharding import PartitionSpec as P

HEADS = 16
PAIR_MAX = 128
LAYERS = 2


def extended(block, sides, width):
    for axis, dim in sides:
        count = lax.axis_size(axis)
        forward = [(i, i + 1) for i in range(count - 1)]
        backward = [(target, source) for source, target in forward]
        low = lax.ppermute(
            lax.slice_in_dim(block, block.shape[dim] - width, None, axis=dim), axis, forward
        )
        high = lax.ppermute(lax.slice_in_dim(block, 0, width, axis=dim), axis, backward)
        block = jnp.concatenate([low, block, high], axis=dim)
    return block


def normalize(values, gain, shift):
    center = values - jnp.mean(values, axis=-1, keepdims=True)
    spread = jnp.mean(center * center, axis=-1, keepdims=True)
    return center * lax.rsqrt(spread + 1e-05) * gain + shift


def gelu_exact(values):
    return jax.nn.gelu(values, approximate=False)


def gelu_back(pre_values, grad_values):
    return jax.vjp(gelu_exact, pre_values)[1](grad_values)[0]


def norm_grad(values, gain, shift, grad_values):
    return jax.vjp(lambda inner: normalize(inner, gain, shift), values)[1](grad_values)[0]


def multiply(left, right):
    return jnp.dot(left, right, preferred_element_type=jnp.float32)


def multiply_back(left, right):
    return lax.dot_general(
        left, right, (((1,), (1,)), ((), ())), preferred_element_type=jnp.float32
    )


def local(
    tokens,
    segments,
    w_qkv,
    b_qkv,
    w_out,
    b_out,
    norm_gain,
    norm_bias,
    w_up,
    b_up,
    w_down,
    b_down,
    prefix,
    cotangent,
):
    seqs_here, tok_here, model_width = tokens.shape
    rows_here = seqs_here * tok_here
    head_count = HEADS
    head_size = model_width // head_count
    score_scale = 1.0 / math.sqrt(head_size)
    rim_rows = PAIR_MAX
    prefix_len = prefix.shape[2]
    position = lax.axis_index("wide") * tok_here
    padded_ids = jnp.pad(segments, ((0, 0), (rim_rows, rim_rows)), constant_values=-1)
    query_ids = lax.dynamic_slice_in_dim(segments, position, tok_here, 1)
    window_ids = lax.dynamic_slice_in_dim(padded_ids, position, tok_here + 2 * rim_rows, 1)
    prefix_mask = jnp.ones((seqs_here, prefix_len, tok_here), dtype=bool)
    visible = jnp.concatenate(
        [prefix_mask, window_ids[:, :, None] == query_ids[:, None, :]], axis=1
    )[:, None]

    def split_heads(values):
        return values.reshape(seqs_here, values.shape[1], head_count, head_size)

    def with_prefix(layer_index, member, window_part):
        fixed_rows = jnp.broadcast_to(
            prefix[layer_index, member][None], (seqs_here, prefix_len, model_width)
        )
        return split_heads(jnp.concatenate([fixed_rows, window_part], axis=1))

    def score_block(queries, key_all):
        scores = (
            jnp.einsum("sqhe,skhe->shkq", queries, key_all, preferred_element_type=jnp.float32)
            * score_scale
        )
        return jnp.where(visible, scores, -1e30)

    hidden = tokens.astype(jnp.float32).reshape(rows_here, model_width)
    stored = []
    for layer_index in range(LAYERS):
        qkv_all = multiply(hidden.astype(jnp.bfloat16), w_qkv[layer_index]) + b_qkv[layer_index]
        qkv_low = qkv_all.astype(jnp.bfloat16).reshape(seqs_here, tok_here, 3 * model_width)
        queries = split_heads(qkv_low[:, :, :model_width])
        window = extended(qkv_low[:, :, model_width:], (("wide", 1),), rim_rows)
        key_all = with_prefix(layer_index, 0, window[:, :, :model_width])
        value_all = with_prefix(layer_index, 1, window[:, :, model_width:])
        scores = score_block(queries, key_all)
        top_score = jnp.max(scores, axis=2, keepdims=True)
        exp_scores = jnp.exp(scores - top_score)
        denominator = jnp.sum(exp_scores, axis=2, keepdims=True)
        probs_low = (exp_scores / denominator).astype(jnp.bfloat16)
        log_total = top_score + jnp.log(denominator)
        context = jnp.einsum(
            "shkq,skhe->sqhe", probs_low, value_all, preferred_element_type=jnp.float32
        )
        context_low = context.astype(jnp.bfloat16).reshape(rows_here, model_width)
        attention = multiply(context_low, w_out[layer_index]) + b_out[layer_index]
        pre_norm = hidden + attention
        normed = normalize(pre_norm, norm_gain[layer_index, 0], norm_bias[layer_index, 0])
        normed_low = normed.astype(jnp.bfloat16)
        up_rows = lax.all_gather(w_up[layer_index], "wide", axis=0, tiled=True)
        down_rows = lax.all_gather(w_down[layer_index], "wide", axis=0, tiled=True)
        bias_rows = lax.all_gather(b_up[layer_index], "wide", axis=0, tiled=True)
        pre_rows = multiply_back(normed_low, up_rows) + bias_rows.astype(jnp.float32)
        ffn_out = multiply(gelu_exact(pre_rows).astype(jnp.bfloat16), down_rows)
        kept_ffn = ()
        second_in = normed + ffn_out + b_down[layer_index]
        stored.append(
            (queries, key_all, value_all, log_total, pre_norm, normed_low, second_in, kept_ffn)
        )
        hidden = normalize(second_in, norm_gain[layer_index, 1], norm_bias[layer_index, 1])
    output = hidden.astype(jnp.bfloat16).reshape(seqs_here, tok_here, model_width)
    grad_hidden = cotangent.astype(jnp.float32).reshape(rows_here, model_width)
    prefix_grads = [None] * LAYERS
    for layer_index in reversed(range(LAYERS)):
        queries, key_all, value_all, log_total, pre_norm, normed_low, second_in, kept_ffn = stored[
            layer_index
        ]
        grad_sum2 = norm_grad(
            second_in, norm_gain[layer_index, 1], norm_bias[layer_index, 1], grad_hidden
        )
        grad_ffn_low = grad_sum2.astype(jnp.bfloat16)
        back_up_rows = lax.all_gather(w_up[layer_index], "wide", axis=0, tiled=True)
        back_down_rows = lax.all_gather(w_down[layer_index], "wide", axis=0, tiled=True)
        back_bias_rows = lax.all_gather(b_up[layer_index], "wide", axis=0, tiled=True)
        back_pre_rows = multiply_back(normed_low, back_up_rows) + back_bias_rows.astype(jnp.float32)
        grad_rows = gelu_back(back_pre_rows, multiply_back(grad_ffn_low, back_down_rows)).astype(
            jnp.bfloat16
        )
        grad_from_ffn = multiply(grad_rows, back_up_rows)
        grad_normed = grad_sum2 + grad_from_ffn
        grad_sum1 = norm_grad(
            pre_norm, norm_gain[layer_index, 0], norm_bias[layer_index, 0], grad_normed
        )
        grad_attn_low = grad_sum1.astype(jnp.bfloat16)
        grad_context = multiply_back(grad_attn_low, w_out[layer_index]).astype(jnp.bfloat16)
        grad_context = split_heads(grad_context.reshape(seqs_here, tok_here, model_width))
        scores = score_block(queries, key_all)
        probs = jnp.exp(scores - log_total)
        probs_low = probs.astype(jnp.bfloat16)
        grad_probs = jnp.einsum(
            "sqhe,skhe->shkq", grad_context, value_all, preferred_element_type=jnp.float32
        )
        row_dot = jnp.sum(probs * grad_probs, axis=2, keepdims=True)
        grad_scores = (probs * (grad_probs - row_dot)).astype(jnp.bfloat16)
        grad_queries = (
            jnp.einsum("shkq,skhe->sqhe", grad_scores, key_all, preferred_element_type=jnp.float32)
            * score_scale
        )
        grad_keys = (
            jnp.einsum("shkq,sqhe->skhe", grad_scores, queries, preferred_element_type=jnp.float32)
            * score_scale
        )
        grad_values = jnp.einsum(
            "shkq,sqhe->skhe", probs_low, grad_context, preferred_element_type=jnp.float32
        )
        key_count = grad_keys.shape[1]
        grad_keys = grad_keys.reshape(seqs_here, key_count, model_width)
        grad_values = grad_values.reshape(seqs_here, key_count, model_width)
        prefix_grads[layer_index] = jnp.stack(
            [
                jnp.sum(grad_keys[:, :prefix_len], axis=0),
                jnp.sum(grad_values[:, :prefix_len], axis=0),
            ],
            axis=0,
        )
        grad_window = jnp.concatenate(
            [grad_keys[:, prefix_len:], grad_values[:, prefix_len:]], axis=2
        )
        grad_kv = grad_window[:, rim_rows : rim_rows + tok_here]
        rim_grads = jnp.concatenate(
            [grad_window[:, :rim_rows], grad_window[:, rim_rows + tok_here :]], axis=1
        )
        returned = extended(rim_grads.astype(jnp.bfloat16), (("wide", 1),), rim_rows).astype(
            rim_grads.dtype
        )
        grad_kv = grad_kv + returned[:, :rim_rows]
        grad_kv = grad_kv + returned[:, 3 * rim_rows :]
        grad_qkv = jnp.concatenate(
            [grad_queries.reshape(seqs_here, tok_here, model_width), grad_kv], axis=2
        )
        grad_qkv = grad_qkv.astype(jnp.bfloat16).reshape(rows_here, 3 * model_width)
        grad_hidden = grad_sum1 + multiply_back(grad_qkv, w_qkv[layer_index])
    grad_prefix = lax.psum(jnp.stack(prefix_grads, axis=0), ("rows", "wide"))
    return (output, grad_hidden.reshape(seqs_here, tok_here, model_width), grad_prefix)


def solution(mesh):
    return jax.shard_map(
        local,
        mesh=mesh,
        in_specs=(
            P("rows", "wide", None),
            P("rows", None),
            P(),
            P(),
            P(),
            P(),
            P(),
            P(),
            P(None, "wide", None),
            P(None, "wide"),
            P(None, "wide", None),
            P(),
            P(),
            P("rows", "wide", None),
        ),
        out_specs=(P("rows", "wide", None), P("rows", "wide", None), P()),
        check_vma=False,
    )
```

profile of v0, /device:TPU:9, one launch (start us, length us, event | category | flops | bytes accessed | tf_op | source)
XLA Modules:
  0.0 837.8 jit_solution(1946470250862313874)
XLA Ops:
  28.3 90.1 %all-gather.1 = bf16[1,4096]{1,0:T(2,128)(2,1)S(1)} all-gather(bf16[1,512]{1,0:T(2,128)(2,1)S(1)} %get-tuple-element.50), channel_id=3, replica_groups=mesh['rows'=4,'wide'=8] {'wide'}, dimensions={1}, use_global_device_ids=true | all-gather | bytes 9216 | tf_op jit(solution)/shard_map/all_gather | solution.py:127
  145.4 10.5 %fusion.193 = (f32[4,16,128]{2,1,0:T(8,128)S(1)}, f32[4,16,448,128]{3,2,1,0:T(8,128)}) fusion(bf16[4,448,16,64]{1,3,2,0:T(8,128)(2,1)} %bitcast.215, bf16[4,128,16,64]{1,3,2,0:T(8,128)(2,1)S(1)} %bitcast.223, pred[4,448,128]{2,1,0:T(8,128)(4,1)S(1)} %concatenate.59), kind=kOutput, calls=%fused_computation.264 | convolution fusion | flops 480763904 | bytes 19660800 | tf_op jit(solution)/shard_map/sqhe,skhe->shkq/dot_general | solution.py:97
  155.9 8.9 %fusion = f32[4,16,128]{2,1,0:T(8,128)S(1)} fusion(f32[4,16,448,128]{3,2,1,0:T(8,128)} %get-tuple-element.52, f32[4,16,128]{2,1,0:T(8,128)S(1)} %get-tuple-element.51), kind=kLoop, calls=%fused_computation.18 | loop fusion | flops 7331840 | bytes 14745600 | tf_op jit(solution)/shard_map/reduce_sum | solution.py:114
  164.9 8.6 %fusion.134 = bf16[4,128,16,64]{1,3,2,0:T(8,128)(2,1)S(1)} fusion(bf16[4,448,16,64]{1,3,2,0:T(8,128)(2,1)S(1)} %bitcast.227, f32[4,16,448,128]{3,2,1,0:T(8,128)} %get-tuple-element.52, f32[4,16,128]{2,1,0:T(8,128)S(1)} %fusion, f32[4,16,128]{2,1,0:T(8,128)S(1)} %get-tuple-element.51), kind=kOutput, calls=%fused_computation.183 | convolution fusion | flops 481296384 | bytes 19464192 | tf_op jit(solution)/shard_map/shkq,skhe->sqhe/dot_general | solution.py:117
  176.3 27.1 %fusion.6 = (f32[512,4096]{1,0:T(8,128)}, f32[512,4096]{1,0:T(8,128)}) fusion(f32[4096]{0:T(1024)S(1)} %bitcast.247, bf16[1,4096,1024]{2,1,0:T(8,128)(2,1)} %all-gather.11.cloned.1.call-done, f32[512,1024]{1,0:T(8,128)S(1)} %get-tuple-element.54, f32[1024]{0:T(1024)} %bitcast.272, f32[1024]{0:T(1024)S(1)} %bitcast.259, f32[512]{0:T(512)S(1)} %fusion.163, ...), kind=kOutput, calls=%fused_computation.26 | convolution fusion | flops 4429709312 | bytes 27291648 | tf_op jit(solution)/shard_map/dot_general | solution.py:49
  203.5 12.3 %fusion.195 = (f32[512]{0:T(512)S(1)}, f32[512,1024]{1,0:T(8,128)S(1)}) fusion(f32[1024]{0:T(1024)S(1)} %bitcast.257, bf16[1,4096,1024]{2,1,0:T(8,128)(2,1)} %all-gather.13.cloned.1.call-done, f32[512,4096]{1,0:T(8,128)} %get-tuple-element.55, f32[512,4096]{1,0:T(8,128)} %get-tuple-element.56, f32[4096]{0:T(1024)S(1)} %bitcast.248, ...), kind=kOutput, calls=%fused_computation.266 | convolution fusion | flops 4307025408 | bytes 29394944 | tf_op jit(solution)/shard_map/dot_general | solution.py:45
  216.2 7.0 add_convert_fusion.2
  230.5 74.9 %all-gather.4 = bf16[1,4096]{1,0:T(2,128)(2,1)S(1)} all-gather(bf16[1,512]{1,0:T(2,128)(2,1)S(1)} %get-tuple-element.49), channel_id=6, replica_groups=mesh['rows'=4,'wide'=8] {'wide'}, dimensions={1}, use_global_device_ids=true | all-gather | bytes 9216 | tf_op jit(solution)/shard_map/all_gather | solution.py:127
  334.5 10.5 %fusion.196 = (f32[4,16,128]{2,1,0:T(8,128)S(1)}, f32[4,16,448,128]{3,2,1,0:T(8,128)}) fusion(bf16[4,448,16,64]{1,3,2,0:T(8,128)(2,1)} %bitcast.217, bf16[4,128,16,64]{1,3,2,0:T(8,128)(2,1)S(1)} %bitcast.225, pred[4,448,128]{2,1,0:T(8,128)(4,1)S(1)} %concatenate.59), kind=kOutput, calls=%fused_computation.267 | convolution fusion | flops 480763904 | bytes 19660800 | tf_op jit(solution)/shard_map/sqhe,skhe->shkq/dot_general | solution.py:97
  345.1 9.1 %fusion.1 = f32[4,16,128]{2,1,0:T(8,128)S(1)} fusion(f32[4,16,448,128]{3,2,1,0:T(8,128)} %get-tuple-element.60, f32[4,16,128]{2,1,0:T(8,128)S(1)} %get-tuple-element.59), kind=kLoop, calls=%fused_computation.19 | loop fusion | flops 7331840 | bytes 14745600 | tf_op jit(solution)/shard_map/reduce_sum | solution.py:114
  354.2 8.5 %fusion.135 = bf16[4,128,16,64]{1,3,2,0:T(8,128)(2,1)S(1)} fusion(bf16[4,448,16,64]{1,3,2,0:T(8,128)(2,1)S(1)} %bitcast.229, f32[4,16,448,128]{3,2,1,0:T(8,128)} %get-tuple-element.60, f32[4,16,128]{2,1,0:T(8,128)S(1)} %fusion.1, f32[4,16,128]{2,1,0:T(8,128)S(1)} %get-tuple-element.59), kind=kOutput, calls=%fused_computation.184 | convolution fusion | flops 481296384 | bytes 19464192 | tf_op jit(solution)/shard_map/shkq,skhe->sqhe/dot_general | solution.py:117
  365.9 26.7 %fusion.7 = (f32[512,4096]{1,0:T(8,128)}, f32[512,4096]{1,0:T(8,128)}) fusion(f32[4096]{0:T(1024)S(1)} %bitcast.250, bf16[1,4096,1024]{2,1,0:T(8,128)(2,1)} %all-gather.15.cloned.1.call-done, f32[512,1024]{1,0:T(8,128)S(1)} %get-tuple-element.62, f32[1024]{0:T(1024)S(1)} %bitcast.268, f32[1024]{0:T(1024)S(1)} %bitcast.265, f32[512]{0:T(512)S(1)} %fusion.165, ...), kind=kOutput, calls=%fused_computation.27 | convolution fusion | flops 4429709312 | bytes 27291648 | tf_op jit(solution)/shard_map/dot_general | solution.py:49
  392.6 11.0 %fusion.198 = (f32[512]{0:T(512)S(1)}, f32[512,1024]{1,0:T(8,128)S(1)}) fusion(f32[1024]{0:T(1024)S(1)} %bitcast.255, bf16[1,4096,1024]{2,1,0:T(8,128)(2,1)} %all-gather.17.cloned.1.call-done, f32[512,4096]{1,0:T(8,128)} %get-tuple-element.63, f32[512,4096]{1,0:T(8,128)} %get-tuple-element.64, f32[4096]{0:T(1024)S(1)} %bitcast.251, ...), kind=kOutput, calls=%fused_computation.269 | convolution fusion | flops 4307025408 | bytes 29394944 | tf_op jit(solution)/shard_map/dot_general | solution.py:45
  406.8 23.7 %multiply_reduce_fusion.4 = (f32[512]{0:T(512)S(1)}, f32[512,1024]{1,0:T(8,128)}) fusion(f32[512,1024]{1,0:T(8,128)S(1)} %get-tuple-element.62, f32[512]{0:T(512)S(1)} %broadcast_multiply_fusion.3, f32[1024]{0:T(1024)S(1)} %bitcast.267, bf16[1,4096,1024]{2,1,0:T(8,128)(2,1)} %all-gather.15.cloned.1.call-done, f32[512,4096]{1,0:T(8,128)} %get-tuple-element.63, ...), kind=kOutput, calls=%fused_computation.153 | convolution fusion | flops 8625586176 | bytes 39872512 | tf_op jit(solution)/shard_map/dot_general | solution.py:45
  438.6 12.0 %fusion.36 = f32[4,16,64,448]{3,2,1,0:T(8,128)} fusion(bf16[4,128,16,64]{1,3,2,0:T(8,128)(2,1)S(1)} %copy.58, f32[4,16,448,128]{3,2,1,0:T(8,128)} %get-tuple-element.60, f32[4,16,128]{2,1,0:T(8,128)S(1)} %log_add_fusion.1), kind=kOutput, calls=%fused_computation.75 | convolution fusion | flops 477102080 | bytes 23101440 | tf_op jit(solution)/shard_map/shkq,sqhe->skhe/dot_general | solution.py:178
  450.6 10.3 %multiply_reduce_fusion.1 = (f32[4,16,128]{2,1,0:T(8,128)S(1)}, f32[4,16,448,128]{3,2,1,0:T(8,128)}) fusion(f32[4,16,448,128]{3,2,1,0:T(8,128)} %get-tuple-element.60, f32[4,16,128]{2,1,0:T(8,128)S(1)} %log_add_fusion.1, bf16[4,448,16,64]{1,3,2,0:T(8,128)(2,1)S(1)} %bitcast.230, bf16[4,128,16,64]{1,3,2,0:T(8,128)(2,1)S(1)} %copy.58), kind=kOutput, calls=%fused_computation.10 | convolution fusion | flops 480763904 | bytes 34144256 | tf_op jit(solution)/shard_map/sqhe,skhe->shkq/dot_general | solution.py:165
  461.0 7.9 slice.247
  468.8 6.6 copy.81
  475.4 10.5 %multiply_convert_fusion.1 = bf16[4,16,448,128]{3,2,1,0:T(8,128)(2,1)S(1)} fusion(f32[4,16,448,128]{3,2,1,0:T(8,128)} %get-tuple-element.70, f32[4,16,448,128]{3,2,1,0:T(8,128)} %get-tuple-element.60, f32[4,16,128]{2,1,0:T(8,128)S(1)} %get-tuple-element.69, f32[4,16,128]{2,1,0:T(8,128)S(1)} %log_add_fusion.1), kind=kLoop, calls=%fused_computation.9 | loop fusion | flops 14680064 | bytes 36765696 | tf_op jit(solution)/shard_map/convert_element_type | solution.py:169
  496.8 6.6 copy.80
  503.4 8.2 fusion.3
  529.2 12.6 %collective-permute-done.4 = bf16[4,128,2048]{2,1,0:T(8,128)(2,1)} collective-permute-done((bf16[4,128,2048]{2,1,0:T(8,128)(2,1)}, bf16[4,128,2048]{2,1,0:T(8,128)(2,1)}, u32[]{:S(2)}, u32[]{:S(2)}) %collective-permute-start.4) | collective-permute-done | bytes 2097184 | tf_op jit(solution)/shard_map/ppermute | solution.py:18
  550.2 6.6 multiply_reduce_fusion.3
  558.8 23.9 %multiply_reduce_fusion.2 = (f32[512]{0:T(512)S(1)}, f32[512,1024]{1,0:T(8,128)}) fusion(f32[512,1024]{1,0:T(8,128)S(1)} %copy-done.14, f32[512]{0:T(512)S(1)} %copy-done.35, f32[1024]{0:T(1024)S(1)} %bitcast.261, bf16[1,4096,1024]{2,1,0:T(8,128)(2,1)} %all-gather.11.cloned.1.call-done, f32[512,4096]{1,0:T(8,128)} %get-tuple-element.55, ...), kind=kOutput, calls=%fused_computation.148 | convolution fusion | flops 8625586176 | bytes 39872512 | tf_op jit(solution)/shard_map/dot_general | solution.py:45
  590.8 11.8 %fusion.34 = f32[4,16,64,448]{3,2,1,0:T(8,128)} fusion(bf16[4,128,16,64]{1,3,2,0:T(8,128)(2,1)S(1)} %copy.65, f32[4,16,448,128]{3,2,1,0:T(8,128)} %get-tuple-element.52, f32[4,16,128]{2,1,0:T(8,128)S(1)} %log_add_fusion), kind=kOutput, calls=%fused_computation.74 | convolution fusion | flops 477102080 | bytes 23101440 | tf_op jit(solution)/shard_map/shkq,sqhe->skhe/dot_general | solution.py:178
  602.6 10.1 %multiply_reduce_fusion = (f32[4,16,128]{2,1,0:T(8,128)S(1)}, f32[4,16,448,128]{3,2,1,0:T(8,128)}) fusion(f32[4,16,448,128]{3,2,1,0:T(8,128)} %get-tuple-element.52, f32[4,16,128]{2,1,0:T(8,128)S(1)} %log_add_fusion, bf16[4,448,16,64]{1,3,2,0:T(8,128)(2,1)S(1)} %bitcast.228, bf16[4,128,16,64]{1,3,2,0:T(8,128)(2,1)S(1)} %copy.65), kind=kOutput, calls=%fused_computation.7 | convolution fusion | flops 480763904 | bytes 34144256 | tf_op jit(solution)/shard_map/sqhe,skhe->shkq/dot_general | solution.py:165
  612.7 7.7 slice.253
  627.0 10.7 %multiply_convert_fusion = bf16[4,16,448,128]{3,2,1,0:T(8,128)(2,1)S(1)} fusion(f32[4,16,448,128]{3,2,1,0:T(8,128)} %get-tuple-element.76, f32[4,16,448,128]{3,2,1,0:T(8,128)} %get-tuple-element.52, f32[4,16,128]{2,1,0:T(8,128)S(1)} %get-tuple-element.75, f32[4,16,128]{2,1,0:T(8,128)S(1)} %log_add_fusion), kind=kLoop, calls=%fused_computation.6 | loop fusion | flops 14680064 | bytes 36765696 | tf_op jit(solution)/shard_map/convert_element_type | solution.py:169
  648.5 6.6 copy.82
  655.1 8.2 fusion.2
  690.8 125.5 %all-reduce.4.cloned.1.call-done = f32[2,2,64,1024]{2,3,1,0:T(8,128)} async-done(((f32[2,2,64,1024]{2,3,1,0:T(8,128)}), f32[2,2,64,1024]{2,3,1,0:T(8,128)}) %all-reduce.4.cloned.1.call-update) | async-done | bytes 1048592 | tf_op jit(solution)/shard_map/psum | solution.py:208
  823.5 7.5 add_add_fusion.8
  (264 shorter events, 200.1 us)
Async XLA Ops:
  7.2 169.1 %all-gather.11.cloned.1.call-start = ((), (), s32[]{:S(2)}) async-start(), calls=%async_computation.1 | async-start | bytes 9437184 | tf_op jit(solution)/shard_map/all_gather | solution.py:125
  10.4 193.0 %all-gather.13.cloned.1.call-start = ((), (), s32[]{:S(2)}) async-start(), calls=%async_computation.2 | async-start | bytes 9437184 | tf_op jit(solution)/shard_map/all_gather | solution.py:126
  12.0 353.8 %all-gather.15.cloned.1.call-start = ((), (), s32[]{:S(2)}) async-start(), calls=%async_computation.3 | async-start | bytes 9437184 | tf_op jit(solution)/shard_map/all_gather | solution.py:125
  18.6 101.4 %copy-start.33 = (s32[4,1024]{1,0:T(4,128)S(1)}, s32[4,1024]{1,0:T(4,128)}, u32[]{:S(2)}) copy-start(s32[4,1024]{1,0:T(4,128)} %param.15) | copy-start | bytes 49156
  18.6 101.8 %copy-start.51 = (f32[2,1024]{1,0:T(2,128)S(1)}, f32[2,1024]{1,0:T(2,128)}, u32[]{:S(2)}) copy-start(f32[2,1024]{1,0:T(2,128)} %param.19) | copy-start | bytes 24580
  18.6 102.4 %copy-start.52 = (f32[2,1024]{1,0:T(2,128)S(1)}, f32[2,1024]{1,0:T(2,128)}, u32[]{:S(2)}) copy-start(f32[2,1024]{1,0:T(2,128)} %param.25) | copy-start | bytes 24580
  18.6 103.0 %copy-start.43 = (f32[2,2,1024]{2,1,0:T(2,128)S(1)}, f32[2,2,1024]{2,1,0:T(2,128)}, u32[]{:S(2)}) copy-start(f32[2,2,1024]{2,1,0:T(2,128)} %param.20) | copy-start | bytes 49156
  18.6 103.6 %copy-start.44 = (f32[2,2,1024]{2,1,0:T(2,128)S(1)}, f32[2,2,1024]{2,1,0:T(2,128)}, u32[]{:S(2)}) copy-start(f32[2,2,1024]{2,1,0:T(2,128)} %param.21) | copy-start | bytes 49156
  20.2 104.5 %collective-permute-start.1 = (bf16[4,128,2048]{2,1,0:T(8,128)(2,1)S(1)}, bf16[4,128,2048]{2,1,0:T(8,128)(2,1)}, u32[]{:S(2)}, u32[]{:S(2)}) collective-permute-start(bf16[4,128,2048]{2,1,0:T(8,128)(2,1)S(1)} %slice.238), channel_id=1, source_target_pairs={{1,0},{2,1},{3,2},{4,3},{5,4},{6,5},{7,6},{9,8},{10,9},{11,10},{12... | collective-permute-start | bytes 6291464 | tf_op jit(solution)/shard_map/ppermute | solution.py:21
  22.8 101.9 %collective-permute-start = (bf16[4,128,2048]{2,1,0:T(8,128)(2,1)S(1)}, bf16[4,128,2048]{2,1,0:T(8,128)(2,1)}, u32[]{:S(2)}, u32[]{:S(2)}) collective-permute-start(bf16[4,128,2048]{2,1,0:T(8,128)(2,1)S(1)} %slice.238), channel_id=1, source_target_pairs={{0,1},{1,2},{2,3},{3,4},{4,5},{5,6},{6,7},{8,9},{9,10},{10,11},{11... | collective-permute-start | bytes 6291464 | tf_op jit(solution)/shard_map/ppermute | solution.py:18
  25.9 366.6 %all-gather.17.cloned.1.call-start = ((), (), s32[]{:S(2)}) async-start(), calls=%async_computation.4 | async-start | bytes 9437184 | tf_op jit(solution)/shard_map/all_gather | solution.py:126
  118.4 85.0 %copy-start.45 = (f32[1,4096]{1,0:T(1,128)}, f32[1,4096]{1,0:T(1,128)S(1)}, u32[]{:S(2)}) copy-start(f32[1,4096]{1,0:T(1,128)S(1)} %convert_element_type.132) | copy-start | bytes 49156
  120.0 25.4 %copy-start.5 = (bf16[4,128,1024]{1,2,0:T(8,128)(2,1)}, bf16[4,128,1024]{1,2,0:T(8,128)(2,1)S(1)}, u32[]{:S(2)}) copy-start(bf16[4,128,1024]{1,2,0:T(8,128)(2,1)S(1)} %copy.51) | copy-start | bytes 3145732
  122.2 81.2 %copy-start.56 = (f32[1,1,1024]{2,1,0:T(1,128)}, f32[1,1,1024]{2,1,0:T(1,128)S(1)}, u32[]{:S(2)}) copy-start(f32[1,1,1024]{2,1,0:T(1,128)S(1)} %get-tuple-element.37) | copy-start | bytes 12292
  122.2 241.3 %copy-start.58 = (f32[1,1,1024]{2,1,0:T(1,128)}, f32[1,1,1024]{2,1,0:T(1,128)S(1)}, u32[]{:S(2)}) copy-start(f32[1,1,1024]{2,1,0:T(1,128)S(1)} %get-tuple-element.36) | copy-start | bytes 12292
  175.8 27.6 %copy-start.13 = (f32[512,1024]{1,0:T(8,128)}, f32[512,1024]{1,0:T(8,128)S(1)}, u32[]{:S(2)}) copy-start(f32[512,1024]{1,0:T(8,128)S(1)} %get-tuple-element.54) | copy-start | bytes 6291460
  175.9 27.6 %copy-start.34 = (f32[512]{0:T(512)}, f32[512]{0:T(512)S(1)}, u32[]{:S(2)}) copy-start(f32[512]{0:T(512)S(1)} %broadcast_multiply_fusion.5) | copy-start | bytes 6148
  176.2 27.2 %copy-start.38 = (f32[512]{0:T(512)}, f32[512]{0:T(512)S(1)}, u32[]{:S(2)}) copy-start(f32[512]{0:T(512)S(1)} %multiply_reduce_fusion.8) | copy-start | bytes 6148
  176.2 27.2 %copy-start.47 = (f32[512]{0:T(512)}, f32[512]{0:T(512)S(1)}, u32[]{:S(2)}) copy-start(f32[512]{0:T(512)S(1)} %fusion.163) | copy-start | bytes 6148
  176.3 27.2 %copy-start.63 = (f32[1,1,1024]{2,1,0:T(1,128)S(1)}, f32[1,1,1024]{2,1,0:T(1,128)}, u32[]{:S(2)}) copy-start(f32[1,1,1024]{2,1,0:T(1,128)} %get-tuple-element.41) | copy-start | bytes 12292
  215.8 147.8 %copy-start.36 = (f32[512]{0:T(512)}, f32[512]{0:T(512)S(1)}, u32[]{:S(2)}) copy-start(f32[512]{0:T(512)S(1)} %broadcast_multiply_fusion.4) | copy-start | bytes 6148
  216.2 147.4 %copy-start.49 = (f32[512]{0:T(512)}, f32[512]{0:T(512)S(1)}, u32[]{:S(2)}) copy-start(f32[512]{0:T(512)S(1)} %fusion.164) | copy-start | bytes 6148
  224.8 84.5 %collective-permute-start.3 = (bf16[4,128,2048]{2,1,0:T(8,128)(2,1)S(1)}, bf16[4,128,2048]{2,1,0:T(8,128)(2,1)}, u32[]{:S(2)}, u32[]{:S(2)}) collective-permute-start(bf16[4,128,2048]{2,1,0:T(8,128)(2,1)S(1)} %slice.242), channel_id=1, source_target_pairs={{1,0},{2,1},{3,2},{4,3},{5,4},{6,5},{7,6},{9,8},{10,9},{11,10},{12... | collective-permute-start | bytes 6291464 | tf_op jit(solution)/shard_map/ppermute | solution.py:21
  227.0 82.4 %collective-permute-start.2 = (bf16[4,128,2048]{2,1,0:T(8,128)(2,1)S(1)}, bf16[4,128,2048]{2,1,0:T(8,128)(2,1)}, u32[]{:S(2)}, u32[]{:S(2)}) collective-permute-start(bf16[4,128,2048]{2,1,0:T(8,128)(2,1)S(1)} %slice.242), channel_id=1, source_target_pairs={{0,1},{1,2},{2,3},{3,4},{4,5},{5,6},{6,7},{8,9},{9,10},{10,11},{11... | collective-permute-start | bytes 6291464 | tf_op jit(solution)/shard_map/ppermute | solution.py:18
  230.4 585.8 %all-reduce.4.cloned.1.call-start = ((), (), s32[]{:S(2)}) async-start(), calls=%async_computation | async-start | bytes 4194304 | tf_op jit(solution)/shard_map/psum | solution.py:208
  309.3 25.2 %copy-start.7 = (bf16[4,128,1024]{1,2,0:T(8,128)(2,1)}, bf16[4,128,1024]{1,2,0:T(8,128)(2,1)S(1)}, u32[]{:S(2)}) copy-start(bf16[4,128,1024]{1,2,0:T(8,128)(2,1)S(1)} %copy.55) | copy-start | bytes 3145732
  365.9 26.7 %copy-start.54 = (f32[1,1024]{1,0:T(1,128)S(1)}, f32[1,1024]{1,0:T(1,128)}, u32[]{:S(2)}) copy-start(f32[1,1024]{1,0:T(1,128)} %get-tuple-element.43) | copy-start | bytes 12292
  516.6 25.2 %collective-permute-start.4 = (bf16[4,128,2048]{2,1,0:T(8,128)(2,1)}, bf16[4,128,2048]{2,1,0:T(8,128)(2,1)}, u32[]{:S(2)}, u32[]{:S(2)}) collective-permute-start(bf16[4,128,2048]{2,1,0:T(8,128)(2,1)} %get-tuple-element.18), channel_id=1, source_target_pairs={{0,1},{1,2},{2,3},{3,4},{4,5},{5,6},{6,7},{8,9},{9,10},{10,11},{11... | collective-permute-start | bytes 6291464 | tf_op jit(solution)/shard_map/ppermute | solution.py:18
  518.5 27.7 %collective-permute-start.5 = (bf16[4,128,2048]{2,1,0:T(8,128)(2,1)}, bf16[4,128,2048]{2,1,0:T(8,128)(2,1)}, u32[]{:S(2)}, u32[]{:S(2)}) collective-permute-start(bf16[4,128,2048]{2,1,0:T(8,128)(2,1)} %get-tuple-element.19), channel_id=1, source_target_pairs={{1,0},{2,1},{3,2},{4,3},{5,4},{6,5},{7,6},{9,8},{10,9},{11,10},{12... | collective-permute-start | bytes 6291464 | tf_op jit(solution)/shard_map/ppermute | solution.py:21
  558.8 23.9 %copy-start.48 = (f32[512]{0:T(512)S(1)}, f32[512]{0:T(512)}, u32[]{:S(2)}) copy-start(f32[512]{0:T(512)} %copy-done.47) | copy-start | bytes 6148
  668.2 151.2 %collective-permute-start.6 = (bf16[4,128,2048]{2,1,0:T(8,128)(2,1)}, bf16[4,128,2048]{2,1,0:T(8,128)(2,1)}, u32[]{:S(2)}, u32[]{:S(2)}) collective-permute-start(bf16[4,128,2048]{2,1,0:T(8,128)(2,1)} %get-tuple-element.16), channel_id=1, source_target_pairs={{0,1},{1,2},{2,3},{3,4},{4,5},{5,6},{6,7},{8,9},{9,10},{10,11},{11... | collective-permute-start | bytes 6291464 | tf_op jit(solution)/shard_map/ppermute | solution.py:18
  670.1 149.3 %collective-permute-start.7 = (bf16[4,128,2048]{2,1,0:T(8,128)(2,1)}, bf16[4,128,2048]{2,1,0:T(8,128)(2,1)}, u32[]{:S(2)}, u32[]{:S(2)}) collective-permute-start(bf16[4,128,2048]{2,1,0:T(8,128)(2,1)} %get-tuple-element.17), channel_id=1, source_target_pairs={{1,0},{2,1},{3,2},{4,3},{5,4},{6,5},{7,6},{9,8},{10,9},{11,10},{12... | collective-permute-start | bytes 6291464 | tf_op jit(solution)/shard_map/ppermute | solution.py:21
  (51 other events, 405.9 us)
Sparse Core Ops, SparseCore 0:
  10.6 103.1 all-gather.10
  115.9 80.5 all-gather.12
  198.0 102.4 all-gather.14
  302.6 80.7 all-gather.16
  681.5 134.6 all-reduce.3
where the time goes:
time: 847 us; the launch traced here: 838 us
  matrix products  257 us (30%)
  blocking collectives  165 us (19%)
  waiting for transfers between devices  143 us (17%)
  local copies, waits for them, and re-layouts  136 us (16%)
  other arithmetic  101 us (12%)
  starting transfers between devices  20.1 us (2%)
  between operations  15.4 us (2%)
    all_gather x2, blocking collectives, local(): bias_rows = lax.all_gather(b_up[layer_index], 'wide', axis=0, tiled=True)  165 us
    psum x1, waiting for transfers between devices, local(): grad_prefix = lax.psum(jnp.stack(prefix_grads, axis=0), ('rows', 'wide'))  125 us
    dot_general x8, matrix products, multiply(): return jnp.dot(left, right, preferred_element_type=jnp.float32)  87.2 us
    dot_general x6, matrix products, multiply_back(): lax.dot_general(left, right, (((1,), (1,)), ((), ())), preferred_element_...  70.5 us
    unnamed x145, local copies, waits for them, and re-layouts  41.8 us
    concatenate x4, local copies, waits for them, and re-layouts, with_prefix(): return split_heads(jnp.concatenate([fixed_rows, window_part], axis=1))  24.8 us
    another operation x4, other arithmetic  24.4 us
    dot_general x2, matrix products, local(): jnp.einsum('shkq,sqhe->skhe', probs_low, grad_context, preferred_element_...  23.8 us
  transfers between devices with their start and end apart: 13, of which 3 were waited for; matrix products, arithmetic and copies ran while one was open for 28% of the time, Pallas kernels for 0%

commit v1 on v0

--- a/solution.py
+++ b/solution.py
@@ -3,6 +3,8 @@
 import jax
 import jax.numpy as jnp
 from jax import lax
+from jax.experimental import pallas as pl
+from jax.experimental.pallas import tpu as pltpu
 from jax.sharding import PartitionSpec as P
 
 HEADS = 16
@@ -49,6 +51,205 @@
     return lax.dot_general(
         left, right, (((1,), (1,)), ((), ())), preferred_element_type=jnp.float32
     )
+
+
+MESH = pl.DeviceIdType.MESH
+
+
+class Gather:
+    def __init__(self, shards, full, sems):
+        self.shards = shards
+        self.full = full
+        self.send_sem, self.zs, self.xs, self.ys, self.ds, self.cz, self.cx, self.cy, self.cd, self.cown, self.own = sems
+        self.row = lax.axis_index("rows")
+        wide = lax.axis_index("wide")
+        self.z, self.core = lax.div(wide, 2), lax.rem(wide, 2)
+        self.shard_rows = shards[0].shape[1]
+        self.unit_rows = self.shard_rows // 4
+        self.row_x = self.row + 1 - 2 * lax.rem(self.row, 2)
+        self.row_y = lax.rem(self.row + 2, 4)
+        self.row_d = 3 - self.row
+
+    def peer(self, kind):
+        wide = self.z * 2 + self.core
+        if kind == "x":
+            return (self.row_x, wide)
+        if kind == "y":
+            return (self.row_y, wide)
+        if kind == "core":
+            return (self.row, self.z * 2 + 1 - self.core)
+        if kind == "right":
+            return (self.row, wide + 2)
+        return (self.row, wide - 2)
+
+    def unit(self, layer, member, z, core, quarter):
+        start = (z * 2 + core) * self.shard_rows + quarter * self.unit_rows
+        return self.full.at[layer, member, pl.ds(pl.multiple_of(start, self.unit_rows), self.unit_rows)]
+
+    def shard(self, layer, member, z, core):
+        start = (z * 2 + core) * self.shard_rows
+        return self.full.at[layer, member, pl.ds(pl.multiple_of(start, self.shard_rows), self.shard_rows)]
+
+    def barrier(self):
+        sem = pltpu.get_barrier_semaphore()
+        for kind in ("x", "y", "core"):
+            pl.semaphore_signal(sem, inc=1, device_id=self.peer(kind), device_id_type=MESH)
+
+        @pl.when(self.z < 3)
+        def _():
+            pl.semaphore_signal(sem, inc=1, device_id=self.peer("right"), device_id_type=MESH)
+
+        @pl.when(self.z > 0)
+        def _():
+            pl.semaphore_signal(sem, inc=1, device_id=self.peer("left"), device_id_type=MESH)
+
+        pl.semaphore_wait(sem, 3 + jnp.minimum(self.z, 1) + jnp.minimum(3 - self.z, 1))
+
+    def copy(self, src, dst, recv, kind):
+        return pltpu.make_async_remote_copy(
+            src_ref=src, dst_ref=dst, send_sem=self.send_sem, recv_sem=recv,
+            device_id=self.peer(kind), device_id_type=MESH,
+        )
+
+    def start(self, layer):
+        for member in range(2):
+            shard = self.shards[member].at[layer]
+            mine = shard.at[pl.ds(pl.multiple_of(self.row * self.unit_rows, self.unit_rows), self.unit_rows)]
+            here = self.unit(layer, member, self.z, self.core, self.row)
+
+            @pl.when(self.z < 3)
+            def _():
+                self.copy(mine, here, self.zs.at[layer, member, 0, 0], "right").start()
+
+            @pl.when(self.z > 0)
+            def _():
+                self.copy(mine, here, self.zs.at[layer, member, 0, 1], "left").start()
+
+        for member in range(2):
+            shard = self.shards[member].at[layer]
+            place = self.shard(layer, member, self.z, self.core)
+            pltpu.make_async_copy(shard, place, self.own.at[layer, member]).start()
+            self.copy(shard, place, self.cown.at[layer, member], "core").start()
+
+    def slots(self, body):
+        for step in range(3):
+            for side in range(2):
+                origin = self.z - 1 - step if side == 0 else self.z + 1 + step
+                inside = origin >= 0 if side == 0 else origin < 4
+
+                @pl.when(inside)
+                def _():
+                    body(step, side, origin)
+
+    def on_z(self, layer, step, side, origin):
+        for member in range(2):
+            unit = self.unit(layer, member, origin, self.core, self.row)
+            self.copy(unit, unit, self.zs.at[layer, member, step, side], "x").wait_recv()
+            if step < 2:
+                more = self.z < 3 if side == 0 else self.z > 0
+
+                @pl.when(more)
+                def _():
+                    self.copy(unit, unit, self.zs.at[layer, member, step + 1, side], "right" if side == 0 else "left").start()
+
+            self.copy(unit, unit, self.xs.at[layer, member, step, side], "x").start()
+            self.copy(unit, unit, self.ys.at[layer, member, step, side], "y").start()
+            self.copy(unit, unit, self.cz.at[layer, member, step, side], "core").start()
+
+    def on_xy(self, layer, step, side, origin):
+        for member in range(2):
+            unit = self.unit(layer, member, origin, self.core, self.row_x)
+            self.copy(unit, unit, self.xs.at[layer, member, step, side], "x").wait_recv()
+            if member == 0:
+                self.copy(unit, unit, self.ds.at[layer, member, step, side], "y").start()
+            self.copy(unit, unit, self.cx.at[layer, member, step, side], "core").start()
+            unit = self.unit(layer, member, origin, self.core, self.row_y)
+            self.copy(unit, unit, self.ys.at[layer, member, step, side], "y").wait_recv()
+            if member == 1:
+                self.copy(unit, unit, self.ds.at[layer, member, step, side], "x").start()
+            self.copy(unit, unit, self.cy.at[layer, member, step, side], "core").start()
+
+    def on_d(self, layer, step, side, origin):
+        for member in range(2):
+            unit = self.unit(layer, member, origin, self.core, self.row_d)
+            self.copy(unit, unit, self.ds.at[layer, member, step, side], "x").wait_recv()
+            self.copy(unit, unit, self.cd.at[layer, member, step, side], "core").start()
+
+    def on_core(self, layer, step, side, origin):
+        for member in range(2):
+            for sem, quarter in ((self.cz, self.row), (self.cx, self.row_x), (self.cy, self.row_y), (self.cd, self.row_d)):
+                unit = self.unit(layer, member, origin, 1 - self.core, quarter)
+                self.copy(unit, unit, sem.at[layer, member, step, side], "core").wait_recv()
+
+    def on_own(self, layer):
+        for member in range(2):
+            place = self.shard(layer, member, self.z, self.core)
+            pltpu.make_async_copy(self.shards[member].at[layer], place, self.own.at[layer, member]).wait()
+            place = self.shard(layer, member, self.z, 1 - self.core)
+            self.copy(place, place, self.cown.at[layer, member], "core").wait_recv()
+
+    def drain(self, layer):
+        def wait(units):
+            span = self.full.at[layer, 0, pl.ds(0, units * self.unit_rows)]
+            self.copy(span, span, self.own.at[layer, 0], "core").wait_send()
+
+        for member in range(2):
+            wait(4)
+            @pl.when(self.z < 3)
+            def _():
+                wait(1)
+            @pl.when(self.z > 0)
+            def _():
+                wait(1)
+
+        def slot(step, side, origin):
+            if step < 2:
+                more = self.z < 3 if side == 0 else self.z > 0
+                @pl.when(more)
+                def _():
+                    wait(2)
+            wait(2 * 3 + 2 * 2 + 2 + 2)
+
+        self.slots(slot)
+
+
+GATHER_SEMS = (
+    [pltpu.SemaphoreType.DMA] + [pltpu.SemaphoreType.DMA((2, 2, 3, 2))] * 8 + [pltpu.SemaphoreType.DMA((2, 2))] * 2
+)
+
+
+def gather_kernel(up_ref, down_ref, out_ref, full, out_sem, *sems):
+    g = Gather((up_ref, down_ref), full, sems)
+    g.barrier()
+    layers = up_ref.shape[0]
+    for layer in range(layers):
+        g.start(layer)
+    for layer in range(layers):
+        g.slots(lambda step, side, origin: g.on_z(layer, step, side, origin))
+        g.slots(lambda step, side, origin: g.on_xy(layer, step, side, origin))
+        g.slots(lambda step, side, origin: g.on_d(layer, step, side, origin))
+        g.on_own(layer)
+        g.slots(lambda step, side, origin: g.on_core(layer, step, side, origin))
+        pltpu.make_async_copy(full.at[layer], out_ref.at[layer], out_sem.at[layer]).start()
+        g.drain(layer)
+    for layer in range(layers):
+        pltpu.make_async_copy(full.at[layer], out_ref.at[layer], out_sem.at[layer]).wait()
+
+
+def gathered(w_up, w_down):
+    layers, rows, width = w_up.shape
+    count = lax.axis_size("wide")
+    if count != 8 or lax.axis_size("rows") != 4:
+        both = [lax.all_gather(w, "wide", axis=1, tiled=True) for w in (w_up, w_down)]
+        return jnp.stack(both, axis=1)
+    return pl.pallas_call(
+        gather_kernel,
+        out_shape=jax.ShapeDtypeStruct((layers, 2, count * rows, width), w_up.dtype),
+        in_specs=[pl.BlockSpec(memory_space=pl.ANY)] * 2,
+        out_specs=pl.BlockSpec(memory_space=pl.ANY),
+        scratch_shapes=[pltpu.VMEM((layers, 2, count * rows, width), w_up.dtype), pltpu.SemaphoreType.DMA((2,))] + GATHER_SEMS,
+        compiler_params=pltpu.CompilerParams(collective_id=0, has_side_effects=True, vmem_limit_bytes=48 << 20),
+    )(w_up, w_down)
 
 
 def local(
@@ -101,6 +302,8 @@
 
     hidden = tokens.astype(jnp.float32).reshape(rows_here, model_width)
     stored = []
+    both = gathered(w_up, w_down)
+    bias_all = lax.all_gather(b_up, "wide", axis=1, tiled=True)
     for layer_index in range(LAYERS):
         qkv_all = multiply(hidden.astype(jnp.bfloat16), w_qkv[layer_index]) + b_qkv[layer_index]
         qkv_low = qkv_all.astype(jnp.bfloat16).reshape(seqs_here, tok_here, 3 * model_width)
@@ -122,9 +325,7 @@
         pre_norm = hidden + attention
         normed = normalize(pre_norm, norm_gain[layer_index, 0], norm_bias[layer_index, 0])
         normed_low = normed.astype(jnp.bfloat16)
-        up_rows = lax.all_gather(w_up[layer_index], "wide", axis=0, tiled=True)
-        down_rows = lax.all_gather(w_down[layer_index], "wide", axis=0, tiled=True)
-        bias_rows = lax.all_gather(b_up[layer_index], "wide", axis=0, tiled=True)
+        up_rows, down_rows, bias_rows = both[layer_index, 0], both[layer_index, 1], bias_all[layer_index]
         pre_rows = multiply_back(normed_low, up_rows) + bias_rows.astype(jnp.float32)
         ffn_out = multiply(gelu_exact(pre_rows).astype(jnp.bfloat16), down_rows)
         kept_ffn = ()
@@ -144,9 +345,7 @@
             second_in, norm_gain[layer_index, 1], norm_bias[layer_index, 1], grad_hidden
         )
         grad_ffn_low = grad_sum2.astype(jnp.bfloat16)
-        back_up_rows = lax.all_gather(w_up[layer_index], "wide", axis=0, tiled=True)
-        back_down_rows = lax.all_gather(w_down[layer_index], "wide", axis=0, tiled=True)
-        back_bias_rows = lax.all_gather(b_up[layer_index], "wide", axis=0, tiled=True)
+        back_up_rows, back_down_rows, back_bias_rows = both[layer_index, 0], both[layer_index, 1], bias_all[layer_index]
         back_pre_rows = multiply_back(normed_low, back_up_rows) + back_bias_rows.astype(jnp.float32)
         grad_rows = gelu_back(back_pre_rows, multiply_back(grad_ffn_low, back_down_rows)).astype(
             jnp.bfloat16

time: 847 us -> 871 us (1.028)
  blocking collectives: 165 us -> 21.9 us
  Pallas kernels: 0 us -> 139 us
  waiting for transfers between devices: 143 us -> 163 us
    all_gather x2 -> x1, blocking collectives: 165 us -> 21.9 us  [local(): bias_all = lax.all_gather(b_up, 'wide', axis=1, tiled=True)]
    pallas_call x0 -> x1, Pallas kernels: none -> 139 us  [gathered(): pl.pallas_call(gather_kernel, out_shape=jax.ShapeDtypeStruct((layers, 2,...]
    ppermute x4, waiting for transfers between devices: 12.6 us -> 31 us  [extended(): lax.ppermute(lax.slice_in_dim(block, block.shape[dim] - width, None, axis...]
    dot_general x2, matrix products: 20.5 us -> 30.5 us  [local(): jnp.einsum('sqhe,skhe->shkq', grad_context, value_all, preferred_element_...]
  transfers between devices with their start and end apart: 13 -> 9, of which waited for: 3 -> 5; matrix products, arithmetic and copies ran while one was open for 28% -> 5% of each run, Pallas kernels for 0% -> 16%
where the time goes in v1:
time: 871 us; the launch traced here: 860 us
  matrix products  265 us (30%)
  waiting for transfers between devices  163 us (19%)
  Pallas kernels  139 us (16%)
  local copies, waits for them, and re-layouts  132 us (15%)
  other arithmetic  102 us (12%)
  blocking collectives  21.9 us (3%)
  starting transfers between devices  20.8 us (2%)
  between operations  15.6 us (2%)
    pallas_call x1, Pallas kernels, gathered(): pl.pallas_call(gather_kernel, out_shape=jax.ShapeDtypeStruct((layers, 2,...  139 us
    psum x1, waiting for transfers between devices, local(): grad_prefix = lax.psum(jnp.stack(prefix_grads, axis=0), ('rows', 'wide'))  123 us
    dot_general x8, matrix products, multiply(): return jnp.dot(left, right, preferred_element_type=jnp.float32)  85.4 us
    dot_general x6, matrix products, multiply_back(): lax.dot_general(left, right, (((1,), (1,)), ((), ())), preferred_element_...  71 us
    unnamed x145, local copies, waits for them, and re-layouts  42.9 us
    ppermute x4, waiting for transfers between devices, extended(): lax.ppermute(lax.slice_in_dim(block, block.shape[dim] - width, None, axis...  31 us
    dot_general x2, matrix products, local(): jnp.einsum('sqhe,skhe->shkq', grad_context, value_all, preferred_element_...  30.5 us
    concatenate x4, local copies, waits for them, and re-layouts, with_prefix(): return split_heads(jnp.concatenate([fixed_rows, window_part], axis=1))  24.8 us
  transfers between devices with their start and end apart: 9, of which 5 were waited for; matrix products, arithmetic and copies ran while one was open for 5% of the time, Pallas kernels for 16%

profile of v1, /device:TPU:9, one launch (start us, length us, event | category | flops | bytes accessed | tf_op | source)
XLA Modules:
  0.0 859.8 jit_solution(3242188160123632192)
XLA Ops:
  31.7 138.7 %shard_map.157 = bf16[2,2,4096,1024]{3,2,1,0:T(8,128)(2,1)} custom-call(bf16[2,512,1024]{2,1,0:T(8,128)(2,1)S(1)} %copy-done, bf16[2,512,1024]{2,1,0:T(8,128)(2,1)S(1)} %copy-done.1), custom_call_target="tpu_custom_call" | custom-call | tf_op jit(solution)/shard_map/pallas_call | solution.py:245
  170.5 21.9 %all_gather.3 = bf16[2,4096]{1,0:T(2,128)(2,1)S(1)} all-gather(bf16[2,512]{1,0:T(2,128)(2,1)S(1)} %copy-done.62), channel_id=1, replica_groups=mesh['rows'=4,'wide'=8] {'wide'}, dimensions={1}, use_global_device_ids=true | all-gather | bytes 18432 | tf_op jit(solution)/shard_map/all_gather | solution.py:306
  216.5 10.5 %fusion.198 = (f32[4,16,128]{2,1,0:T(8,128)S(1)}, f32[4,16,448,128]{3,2,1,0:T(8,128)}) fusion(bf16[4,448,16,64]{1,3,2,0:T(8,128)(2,1)} %bitcast.215, bf16[4,128,16,64]{1,3,2,0:T(8,128)(2,1)S(1)} %bitcast.225, pred[4,448,128]{2,1,0:T(8,128)(4,1)S(1)} %concatenate.59), kind=kOutput, calls=%fused_computation.271 | convolution fusion | flops 480763904 | bytes 19660800 | tf_op jit(solution)/shard_map/sqhe,skhe->shkq/dot_general | solution.py:298
  227.0 9.0 %fusion = f32[4,16,128]{2,1,0:T(8,128)S(1)} fusion(f32[4,16,448,128]{3,2,1,0:T(8,128)} %get-tuple-element.48, f32[4,16,128]{2,1,0:T(8,128)S(1)} %get-tuple-element.47), kind=kLoop, calls=%fused_computation.18 | loop fusion | flops 7331840 | bytes 14745600 | tf_op jit(solution)/shard_map/reduce_sum | solution.py:317
  236.1 8.4 fusion.142
  247.2 27.3 %fusion.6 = (f32[512,4096]{1,0:T(8,128)}, f32[512,4096]{1,0:T(8,128)}) fusion(f32[4096]{0:T(1024)S(1)} %bitcast.249, bf16[2,2,4096,1024]{3,2,1,0:T(8,128)(2,1)} %shard_map.157, f32[512,1024]{1,0:T(8,128)S(1)} %get-tuple-element.50, f32[1024]{0:T(1024)S(1)} %bitcast.274, f32[1024]{0:T(1024)S(1)} %bitcast.261, f32[512]{0:T(512)S(1)} %fusion.171, ...), kind=kOutput, calls=%fused_computation.26 | convolution fusion | flops 4429709312 | bytes 27291648 | tf_op jit(solution)/shard_map/dot_general | solution.py:51
  274.5 11.3 %fusion.200 = (f32[512]{0:T(512)S(1)}, f32[512,1024]{1,0:T(8,128)S(1)}) fusion(f32[1024]{0:T(1024)S(1)} %bitcast.259, bf16[2,2,4096,1024]{3,2,1,0:T(8,128)(2,1)} %shard_map.157, f32[512,4096]{1,0:T(8,128)} %get-tuple-element.51, f32[512,4096]{1,0:T(8,128)} %get-tuple-element.52, f32[4096]{0:T(1024)S(1)} %bitcast.250, f32[1024]{0:T(1024)S(1)} %bitcast.275, ...), kind=kOutput, calls=%fused_computation.273 | convolution fusion | flops 4307025408 | bytes 29394944 | tf_op jit(solution)/shard_map/dot_general | solution.py:47
  287.0 6.6 add_convert_fusion.2
  304.3 18.7 %collective-permute-done.2 = bf16[4,128,2048]{2,1,0:T(8,128)(2,1)} collective-permute-done((bf16[4,128,2048]{2,1,0:T(8,128)(2,1)}, bf16[4,128,2048]{2,1,0:T(8,128)(2,1)}, u32[]{:S(2)}, u32[]{:S(2)}) %collective-permute-start.2) | collective-permute-done | bytes 2097184 | tf_op jit(solution)/shard_map/ppermute | solution.py:20
  352.5 10.4 %fusion.201 = (f32[4,16,128]{2,1,0:T(8,128)S(1)}, f32[4,16,448,128]{3,2,1,0:T(8,128)}) fusion(bf16[4,448,16,64]{1,3,2,0:T(8,128)(2,1)} %bitcast.217, bf16[4,128,16,64]{1,3,2,0:T(8,128)(2,1)S(1)} %bitcast.227, pred[4,448,128]{2,1,0:T(8,128)(4,1)S(1)} %concatenate.59), kind=kOutput, calls=%fused_computation.274 | convolution fusion | flops 480763904 | bytes 19660800 | tf_op jit(solution)/shard_map/sqhe,skhe->shkq/dot_general | solution.py:298
  362.9 9.0 %fusion.1 = f32[4,16,128]{2,1,0:T(8,128)S(1)} fusion(f32[4,16,448,128]{3,2,1,0:T(8,128)} %get-tuple-element.56, f32[4,16,128]{2,1,0:T(8,128)S(1)} %get-tuple-element.55), kind=kLoop, calls=%fused_computation.19 | loop fusion | flops 7331840 | bytes 14745600 | tf_op jit(solution)/shard_map/reduce_sum | solution.py:317
  371.9 8.4 fusion.143
  383.6 27.0 %fusion.7 = (f32[512,4096]{1,0:T(8,128)}, f32[512,4096]{1,0:T(8,128)}) fusion(f32[4096]{0:T(1024)S(1)} %bitcast.252, bf16[2,2,4096,1024]{3,2,1,0:T(8,128)(2,1)} %shard_map.157, f32[512,1024]{1,0:T(8,128)S(1)} %get-tuple-element.58, f32[1024]{0:T(1024)S(1)} %bitcast.270, f32[1024]{0:T(1024)S(1)} %bitcast.267, f32[512]{0:T(512)S(1)} %fusion.173, ...), kind=kOutput, calls=%fused_computation.27 | convolution fusion | flops 4429709312 | bytes 27291648 | tf_op jit(solution)/shard_map/dot_general | solution.py:51
  410.6 11.3 %fusion.203 = (f32[512]{0:T(512)S(1)}, f32[512,1024]{1,0:T(8,128)S(1)}) fusion(f32[1024]{0:T(1024)S(1)} %bitcast.257, bf16[2,2,4096,1024]{3,2,1,0:T(8,128)(2,1)} %shard_map.157, f32[512,4096]{1,0:T(8,128)} %get-tuple-element.59, f32[512,4096]{1,0:T(8,128)} %get-tuple-element.60, f32[4096]{0:T(1024)S(1)} %bitcast.253, f32[1024]{0:T(1024)S(1)} %bitcast.271, ...), kind=kOutput, calls=%fused_computation.276 | convolution fusion | flops 4307025408 | bytes 29394944 | tf_op jit(solution)/shard_map/dot_general | solution.py:47
  425.1 23.2 %multiply_reduce_fusion.4 = (f32[512]{0:T(512)S(1)}, f32[512,1024]{1,0:T(8,128)}) fusion(f32[512,1024]{1,0:T(8,128)S(1)} %copy-done.18, f32[512]{0:T(512)S(1)} %broadcast_multiply_fusion.3, f32[1024]{0:T(1024)S(1)} %bitcast.269, bf16[2,2,4096,1024]{3,2,1,0:T(8,128)(2,1)} %shard_map.157, f32[512,4096]{1,0:T(8,128)} %get-tuple-element.59, ...), kind=kOutput, calls=%fused_computation.161 | convolution fusion | flops 8625586176 | bytes 41971712 | tf_op jit(solution)/shard_map/dot_general | solution.py:47
  456.6 15.2 %multiply_reduce_fusion.1 = (f32[4,16,128]{2,1,0:T(8,128)S(1)}, f32[4,16,448,128]{3,2,1,0:T(8,128)}) fusion(f32[4,16,448,128]{3,2,1,0:T(8,128)} %get-tuple-element.56, f32[4,16,128]{2,1,0:T(8,128)S(1)} %log_add_fusion.1, bf16[4,448,16,64]{1,3,2,0:T(8,128)(2,1)} %bitcast.231, bf16[4,128,16,64]{1,3,2,0:T(8,128)(2,1)S(1)} %copy.58), kind=kOutput, calls=%fused_computation.10 | convolution fusion | flops 480763904 | bytes 34144256 | tf_op jit(solution)/shard_map/sqhe,skhe->shkq/dot_general | solution.py:364
  471.8 8.4 fusion.44
  487.9 6.6 copy.81
  494.5 10.7 %multiply_convert_fusion.1 = bf16[4,16,448,128]{3,2,1,0:T(8,128)(2,1)S(1)} fusion(f32[4,16,448,128]{3,2,1,0:T(8,128)} %get-tuple-element.66, f32[4,16,448,128]{3,2,1,0:T(8,128)} %get-tuple-element.56, f32[4,16,128]{2,1,0:T(8,128)S(1)} %get-tuple-element.65, f32[4,16,128]{2,1,0:T(8,128)S(1)} %log_add_fusion.1), kind=kLoop, calls=%fused_computation.9 | loop fusion | flops 14680064 | bytes 36765696 | tf_op jit(solution)/shard_map/convert_element_type | solution.py:368
  516.1 6.6 copy.80
  522.6 8.2 fusion.3
  548.7 12.3 %collective-permute-done.4 = bf16[4,128,2048]{2,1,0:T(8,128)(2,1)} collective-permute-done((bf16[4,128,2048]{2,1,0:T(8,128)(2,1)}, bf16[4,128,2048]{2,1,0:T(8,128)(2,1)}, u32[]{:S(2)}, u32[]{:S(2)}) %collective-permute-start.4) | collective-permute-done | bytes 2097184 | tf_op jit(solution)/shard_map/ppermute | solution.py:20
  569.4 6.6 multiply_reduce_fusion.3
  578.0 23.5 %multiply_reduce_fusion.2 = (f32[512]{0:T(512)S(1)}, f32[512,1024]{1,0:T(8,128)}) fusion(f32[512,1024]{1,0:T(8,128)S(1)} %copy-done.14, f32[512]{0:T(512)S(1)} %copy-done.34, f32[1024]{0:T(1024)S(1)} %bitcast.263, bf16[2,2,4096,1024]{3,2,1,0:T(8,128)(2,1)} %shard_map.157, f32[512,4096]{1,0:T(8,128)} %get-tuple-element.51, ...), kind=kOutput, calls=%fused_computation.156 | convolution fusion | flops 8625586176 | bytes 41971712 | tf_op jit(solution)/shard_map/dot_general | solution.py:47
  609.6 11.7 %fusion.42 = f32[4,16,64,448]{3,2,1,0:T(8,128)} fusion(bf16[4,128,16,64]{1,3,2,0:T(8,128)(2,1)S(1)} %copy.65, f32[4,16,448,128]{3,2,1,0:T(8,128)} %get-tuple-element.48, f32[4,16,128]{2,1,0:T(8,128)S(1)} %log_add_fusion), kind=kOutput, calls=%fused_computation.82 | convolution fusion | flops 477102080 | bytes 23101440 | tf_op jit(solution)/shard_map/shkq,sqhe->skhe/dot_general | solution.py:377
  621.4 15.3 %multiply_reduce_fusion = (f32[4,16,128]{2,1,0:T(8,128)S(1)}, f32[4,16,448,128]{3,2,1,0:T(8,128)}) fusion(f32[4,16,448,128]{3,2,1,0:T(8,128)} %get-tuple-element.48, f32[4,16,128]{2,1,0:T(8,128)S(1)} %log_add_fusion, bf16[4,448,16,64]{1,3,2,0:T(8,128)(2,1)} %bitcast.229, bf16[4,128,16,64]{1,3,2,0:T(8,128)(2,1)S(1)} %copy.65), kind=kOutput, calls=%fused_computation.7 | convolution fusion | flops 480763904 | bytes 34144256 | tf_op jit(solution)/shard_map/sqhe,skhe->shkq/dot_general | solution.py:364
  636.7 10.8 %multiply_convert_fusion = bf16[4,16,448,128]{3,2,1,0:T(8,128)(2,1)S(1)} fusion(f32[4,16,448,128]{3,2,1,0:T(8,128)} %get-tuple-element.72, f32[4,16,448,128]{3,2,1,0:T(8,128)} %get-tuple-element.48, f32[4,16,128]{2,1,0:T(8,128)S(1)} %get-tuple-element.71, f32[4,16,128]{2,1,0:T(8,128)S(1)} %log_add_fusion), kind=kLoop, calls=%fused_computation.6 | loop fusion | flops 14680064 | bytes 36765696 | tf_op jit(solution)/shard_map/convert_element_type | solution.py:368
  658.3 6.6 copy.83
  664.9 7.7 slice.254
  679.1 8.2 fusion.2
  714.9 123.1 %all-reduce.4.cloned.1.call-done = f32[2,2,64,1024]{2,3,1,0:T(8,128)} async-done(((f32[2,2,64,1024]{2,3,1,0:T(8,128)}), f32[2,2,64,1024]{2,3,1,0:T(8,128)}) %all-reduce.4.cloned.1.call-update) | async-done | bytes 1048592 | tf_op jit(solution)/shard_map/psum | solution.py:407
  845.1 7.5 add_add_fusion.8
  (249 shorter events, 213.4 us)
Async XLA Ops:
  7.2 830.8 %all-reduce.4.cloned.1.call-start = ((), (), s32[]{:S(2)}) async-start(), calls=%async_computation | async-start | bytes 4194304 | tf_op jit(solution)/shard_map/psum | solution.py:407
  18.3 177.8 %collective-permute-start = (bf16[4,128,2048]{2,1,0:T(8,128)(2,1)}, bf16[4,128,2048]{2,1,0:T(8,128)(2,1)}, u32[]{:S(2)}, u32[]{:S(2)}) collective-permute-start(bf16[4,128,2048]{2,1,0:T(8,128)(2,1)} %slice.238), channel_id=1, source_target_pairs={{0,1},{1,2},{2,3},{3,4},{4,5},{5,6},{6,7},{8,9},{9,10},{10,11},{11... | collective-permute-start | bytes 6291464 | tf_op jit(solution)/shard_map/ppermute | solution.py:20
  22.1 174.1 %collective-permute-start.1 = (bf16[4,128,2048]{2,1,0:T(8,128)(2,1)}, bf16[4,128,2048]{2,1,0:T(8,128)(2,1)}, u32[]{:S(2)}, u32[]{:S(2)}) collective-permute-start(bf16[4,128,2048]{2,1,0:T(8,128)(2,1)} %slice.238), channel_id=1, source_target_pairs={{1,0},{2,1},{3,2},{4,3},{5,4},{6,5},{7,6},{9,8},{10,9},{11,10},{12... | collective-permute-start | bytes 6291464 | tf_op jit(solution)/shard_map/ppermute | solution.py:23
  28.9 187.6 %copy-start.7 = (bf16[4,128,1024]{1,2,0:T(8,128)(2,1)}, bf16[4,128,1024]{1,2,0:T(8,128)(2,1)S(1)}, u32[]{:S(2)}) copy-start(bf16[4,128,1024]{1,2,0:T(8,128)(2,1)S(1)} %copy.51) | copy-start | bytes 3145732
  31.7 138.8 %copy-start.62 = (bf16[2,512]{1,0:T(2,128)(2,1)S(1)}, bf16[2,512]{1,0:T(2,128)(2,1)}, u32[]{:S(2)}) copy-start(bf16[2,512]{1,0:T(2,128)(2,1)} %param.23) | copy-start | bytes 6148
  31.7 160.7 %copy-start.52 = (f32[2,1024]{1,0:T(2,128)S(1)}, f32[2,1024]{1,0:T(2,128)}, u32[]{:S(2)}) copy-start(f32[2,1024]{1,0:T(2,128)} %param.19) | copy-start | bytes 24580
  31.7 161.3 %copy-start.53 = (f32[2,1024]{1,0:T(2,128)S(1)}, f32[2,1024]{1,0:T(2,128)}, u32[]{:S(2)}) copy-start(f32[2,1024]{1,0:T(2,128)} %param.25) | copy-start | bytes 24580
  31.7 161.9 %copy-start.42 = (f32[2,2,1024]{2,1,0:T(2,128)S(1)}, f32[2,2,1024]{2,1,0:T(2,128)}, u32[]{:S(2)}) copy-start(f32[2,2,1024]{2,1,0:T(2,128)} %param.20) | copy-start | bytes 49156
  31.7 162.5 %copy-start.43 = (f32[2,2,1024]{2,1,0:T(2,128)S(1)}, f32[2,2,1024]{2,1,0:T(2,128)}, u32[]{:S(2)}) copy-start(f32[2,2,1024]{2,1,0:T(2,128)} %param.21) | copy-start | bytes 49156
  31.7 163.1 %copy-start.25 = (bf16[2,2,64,1024]{3,2,1,0:T(8,128)(2,1)S(1)}, bf16[2,2,64,1024]{3,2,1,0:T(8,128)(2,1)}, u32[]{:S(2)}) copy-start(bf16[2,2,64,1024]{3,2,1,0:T(8,128)(2,1)} %param.26) | copy-start | bytes 1572868
  194.2 80.3 %copy-start.56 = (f32[1,1,1024]{2,1,0:T(1,128)}, f32[1,1,1024]{2,1,0:T(1,128)S(1)}, u32[]{:S(2)}) copy-start(f32[1,1,1024]{2,1,0:T(1,128)S(1)} %get-tuple-element.33) | copy-start | bytes 12292
  194.2 187.1 %copy-start.58 = (f32[1,1,1024]{2,1,0:T(1,128)}, f32[1,1,1024]{2,1,0:T(1,128)S(1)}, u32[]{:S(2)}) copy-start(f32[1,1,1024]{2,1,0:T(1,128)S(1)} %get-tuple-element.32) | copy-start | bytes 12292
  196.1 78.4 %copy-start.44 = (f32[1,4096]{1,0:T(1,128)}, f32[1,4096]{1,0:T(1,128)S(1)}, u32[]{:S(2)}) copy-start(f32[1,4096]{1,0:T(1,128)S(1)} %get-tuple-element.40) | copy-start | bytes 49156
  246.8 27.7 %copy-start.13 = (f32[512,1024]{1,0:T(8,128)}, f32[512,1024]{1,0:T(8,128)S(1)}, u32[]{:S(2)}) copy-start(f32[512,1024]{1,0:T(8,128)S(1)} %get-tuple-element.50) | copy-start | bytes 6291460
  246.8 27.7 %copy-start.33 = (f32[512]{0:T(512)}, f32[512]{0:T(512)S(1)}, u32[]{:S(2)}) copy-start(f32[512]{0:T(512)S(1)} %broadcast_multiply_fusion.5) | copy-start | bytes 6148
  247.2 27.3 %copy-start.37 = (f32[512]{0:T(512)}, f32[512]{0:T(512)S(1)}, u32[]{:S(2)}) copy-start(f32[512]{0:T(512)S(1)} %multiply_reduce_fusion.8) | copy-start | bytes 6148
  247.2 27.3 %copy-start.48 = (f32[512]{0:T(512)}, f32[512]{0:T(512)S(1)}, u32[]{:S(2)}) copy-start(f32[512]{0:T(512)S(1)} %fusion.171) | copy-start | bytes 6148
  285.8 95.5 %copy-start.15 = (f32[512,1024]{1,0:T(8,128)}, f32[512,1024]{1,0:T(8,128)S(1)}, u32[]{:S(2)}) copy-start(f32[512,1024]{1,0:T(8,128)S(1)} %get-tuple-element.54) | copy-start | bytes 6291460
  285.8 95.5 %copy-start.35 = (f32[512]{0:T(512)}, f32[512]{0:T(512)S(1)}, u32[]{:S(2)}) copy-start(f32[512]{0:T(512)S(1)} %broadcast_multiply_fusion.4) | copy-start | bytes 6148
  286.2 95.1 %copy-start.50 = (f32[512]{0:T(512)}, f32[512]{0:T(512)S(1)}, u32[]{:S(2)}) copy-start(f32[512]{0:T(512)S(1)} %fusion.172) | copy-start | bytes 6148
  295.2 27.8 %collective-permute-start.2 = (bf16[4,128,2048]{2,1,0:T(8,128)(2,1)}, bf16[4,128,2048]{2,1,0:T(8,128)(2,1)}, u32[]{:S(2)}, u32[]{:S(2)}) collective-permute-start(bf16[4,128,2048]{2,1,0:T(8,128)(2,1)} %slice.243), channel_id=1, source_target_pairs={{0,1},{1,2},{2,3},{3,4},{4,5},{5,6},{6,7},{8,9},{9,10},{10,11},{11... | collective-permute-start | bytes 6291464 | tf_op jit(solution)/shard_map/ppermute | solution.py:20
  299.7 27.7 %collective-permute-start.3 = (bf16[4,128,2048]{2,1,0:T(8,128)(2,1)}, bf16[4,128,2048]{2,1,0:T(8,128)(2,1)}, u32[]{:S(2)}, u32[]{:S(2)}) collective-permute-start(bf16[4,128,2048]{2,1,0:T(8,128)(2,1)} %slice.243), channel_id=1, source_target_pairs={{1,0},{2,1},{3,2},{4,3},{5,4},{6,5},{7,6},{9,8},{10,9},{11,10},{12... | collective-permute-start | bytes 6291464 | tf_op jit(solution)/shard_map/ppermute | solution.py:23
  304.3 48.2 %copy-start.9 = (bf16[4,128,1024]{1,2,0:T(8,128)(2,1)}, bf16[4,128,1024]{1,2,0:T(8,128)(2,1)S(1)}, u32[]{:S(2)}) copy-start(bf16[4,128,1024]{1,2,0:T(8,128)(2,1)S(1)} %copy.55) | copy-start | bytes 3145732
  382.9 27.6 %copy-start.17 = (f32[512,1024]{1,0:T(8,128)}, f32[512,1024]{1,0:T(8,128)S(1)}, u32[]{:S(2)}) copy-start(f32[512,1024]{1,0:T(8,128)S(1)} %get-tuple-element.58) | copy-start | bytes 6291460
  383.5 27.0 %copy-start.54 = (f32[1,1024]{1,0:T(1,128)S(1)}, f32[1,1024]{1,0:T(1,128)}, u32[]{:S(2)}) copy-start(f32[1,1024]{1,0:T(1,128)} %get-tuple-element.41) | copy-start | bytes 12292
  535.9 25.2 %collective-permute-start.4 = (bf16[4,128,2048]{2,1,0:T(8,128)(2,1)}, bf16[4,128,2048]{2,1,0:T(8,128)(2,1)}, u32[]{:S(2)}, u32[]{:S(2)}) collective-permute-start(bf16[4,128,2048]{2,1,0:T(8,128)(2,1)} %get-tuple-element.18), channel_id=1, source_target_pairs={{0,1},{1,2},{2,3},{3,4},{4,5},{5,6},{6,7},{8,9},{9,10},{10,11},{11... | collective-permute-start | bytes 6291464 | tf_op jit(solution)/shard_map/ppermute | solution.py:20
  537.8 27.7 %collective-permute-start.5 = (bf16[4,128,2048]{2,1,0:T(8,128)(2,1)}, bf16[4,128,2048]{2,1,0:T(8,128)(2,1)}, u32[]{:S(2)}, u32[]{:S(2)}) collective-permute-start(bf16[4,128,2048]{2,1,0:T(8,128)(2,1)} %get-tuple-element.19), channel_id=1, source_target_pairs={{1,0},{2,1},{3,2},{4,3},{5,4},{6,5},{7,6},{9,8},{10,9},{11,10},{12... | collective-permute-start | bytes 6291464 | tf_op jit(solution)/shard_map/ppermute | solution.py:23
  578.0 23.5 %copy-start.38 = (f32[512]{0:T(512)S(1)}, f32[512]{0:T(512)}, u32[]{:S(2)}) copy-start(f32[512]{0:T(512)} %copy-done.37) | copy-start | bytes 6148
  578.0 23.5 %copy-start.49 = (f32[512]{0:T(512)S(1)}, f32[512]{0:T(512)}, u32[]{:S(2)}) copy-start(f32[512]{0:T(512)} %copy-done.48) | copy-start | bytes 6148
  621.3 32.6 %slice-start = ((s8[8388608]{0:T(1024)(128)(4,1)}), s8[4194304]{0:T(1024)(128)(4,1)S(1)}, s32[]{:S(2)}) async-start(s8[8388608]{0:T(1024)(128)(4,1)} %bitcast.222), calls=%async_computation.1 | async-start | bytes 8388608
  692.2 148.9 %collective-permute-start.6 = (bf16[4,128,2048]{2,1,0:T(8,128)(2,1)}, bf16[4,128,2048]{2,1,0:T(8,128)(2,1)}, u32[]{:S(2)}, u32[]{:S(2)}) collective-permute-start(bf16[4,128,2048]{2,1,0:T(8,128)(2,1)} %get-tuple-element.16), channel_id=1, source_target_pairs={{0,1},{1,2},{2,3},{3,4},{4,5},{5,6},{6,7},{8,9},{9,10},{10,11},{11... | collective-permute-start | bytes 6291464 | tf_op jit(solution)/shard_map/ppermute | solution.py:20
  694.1 146.9 %collective-permute-start.7 = (bf16[4,128,2048]{2,1,0:T(8,128)(2,1)}, bf16[4,128,2048]{2,1,0:T(8,128)(2,1)}, u32[]{:S(2)}, u32[]{:S(2)}) collective-permute-start(bf16[4,128,2048]{2,1,0:T(8,128)(2,1)} %get-tuple-element.17), channel_id=1, source_target_pairs={{1,0},{2,1},{3,2},{4,3},{5,4},{6,5},{7,6},{9,8},{10,9},{11,10},{12... | collective-permute-start | bytes 6291464 | tf_op jit(solution)/shard_map/ppermute | solution.py:23
  (47 other events, 368.1 us)
Sparse Core Ops, SparseCore 0:
  705.6 132.2 all-reduce.3

commit v2 on v0

v2 whole, which is shorter than its diff:
```python
import functools
import math

import jax
import jax.numpy as jnp
from jax import lax
from jax.experimental import pallas as pl
from jax.experimental.pallas import tpu as pltpu
from jax.sharding import PartitionSpec as P

HEADS = 16
PAIR_MAX = 128
MESH = pl.DeviceIdType.MESH
LANES = 128
SPAN = 1024
ROOT_HALF = math.sqrt(0.5)


def multiply(left, right):
    return jnp.dot(left, right, preferred_element_type=jnp.float32)


def multiply_back(left, right):
    return lax.dot_general(left, right, (((1,), (1,)), ((), ())), preferred_element_type=jnp.float32)


def multiply_first(left, right):
    return lax.dot_general(left, right, (((0,), (0,)), ((), ())), preferred_element_type=jnp.float32)


def two_heads(rows):
    half = rows.shape[1] // 2
    lane = lax.broadcasted_iota(jnp.int32, rows.shape, 1)
    nothing = jnp.zeros_like(rows)
    return jnp.concatenate([jnp.where(lane < half, rows, nothing), jnp.where(lane >= half, rows, nothing)], axis=0)


def own_heads(columns):
    half, count = columns.shape[0] // 2, columns.shape[1] // 2
    place = lax.broadcasted_iota(jnp.int32, (columns.shape[0], count), 0)
    return jnp.where(place < half, columns[:, :count], columns[:, count:]).T


def attend(blocks, rows, rim, pair, q_ref, k_ref, v_ref, prefix_ref, hide_ref, context_ref, lse_ref):
    lanes = pl.ds(pl.multiple_of(pair * 128, 128), 128)
    prefix_keys, prefix_values = prefix_ref[0, :, lanes], prefix_ref[1, :, lanes]
    for block in range(blocks):
        here = pl.ds(block * rows, rows)
        window = pl.ds(block * rows, rows + 2 * rim)
        queries = two_heads(q_ref[here, lanes])
        hide = hide_ref[block]
        fixed = multiply_back(prefix_keys, queries)
        near = multiply_back(k_ref[window, lanes], queries) + jnp.concatenate([hide, hide], axis=1)
        top = jnp.maximum(jnp.max(fixed, axis=0, keepdims=True), jnp.max(near, axis=0, keepdims=True))
        fixed, near = jnp.exp(fixed - top), jnp.exp(near - top)
        total = jnp.sum(fixed, axis=0, keepdims=True) + jnp.sum(near, axis=0, keepdims=True)
        share = 1.0 / total
        columns = multiply_first(prefix_values, fixed.astype(jnp.bfloat16)) + multiply_first(
            v_ref[window, lanes], near.astype(jnp.bfloat16)
        )
        context_ref[here, lanes] = own_heads(columns * share).astype(jnp.bfloat16)
        lse_ref[pair * blocks + block] = top + jnp.log(total)


def attend_back(blocks, rows, rim, pair, q_ref, k_ref, v_ref, prefix_ref, hide_ref, lse_ref, grad_ref, dq_ref, dk_ref, dv_ref, dp_ref, scale):
    lanes = pl.ds(pl.multiple_of(pair * 128, 128), 128)
    prefix_keys, prefix_values = prefix_ref[0, :, lanes], prefix_ref[1, :, lanes]
    for block in range(blocks):
        here = pl.ds(block * rows, rows)
        window = pl.ds(block * rows, rows + 2 * rim)
        queries = two_heads(q_ref[here, lanes])
        grads = two_heads(grad_ref[here, lanes])
        hide = hide_ref[block]
        keys, values = k_ref[window, lanes], v_ref[window, lanes]
        lse = lse_ref[pair * blocks + block]
        fixed = jnp.exp(multiply_back(prefix_keys, queries) - lse)
        near = jnp.exp(multiply_back(keys, queries) + jnp.concatenate([hide, hide], axis=1) - lse)
        grad_fixed = multiply_back(prefix_values, grads)
        grad_near = multiply_back(values, grads)
        dots = jnp.sum(fixed * grad_fixed, axis=0, keepdims=True) + jnp.sum(near * grad_near, axis=0, keepdims=True)
        grad_fixed = (fixed * (grad_fixed - dots)).astype(jnp.bfloat16)
        grad_near = (near * (grad_near - dots)).astype(jnp.bfloat16)
        fixed, near = fixed.astype(jnp.bfloat16), near.astype(jnp.bfloat16)
        columns = multiply_first(prefix_keys, grad_fixed) + multiply_first(keys, grad_near)
        dq_ref[here, lanes] = (own_heads(columns) * scale).astype(jnp.bfloat16)
        new_keys, new_values = multiply(grad_near, queries), multiply(near, grads)
        fixed_keys, fixed_values = multiply(grad_fixed, queries), multiply(fixed, grads)
        old = pl.ds(block * rows, 2 * rim)
        fresh = pl.ds(block * rows + 2 * rim, rows)
        if block == 0:
            dk_ref[window, lanes], dv_ref[window, lanes] = new_keys, new_values
            dp_ref[0, :, lanes], dp_ref[1, :, lanes] = fixed_keys, fixed_values
        else:
            dk_ref[old, lanes] += new_keys[: 2 * rim]
            dv_ref[old, lanes] += new_values[: 2 * rim]
            dk_ref[fresh, lanes], dv_ref[fresh, lanes] = new_keys[2 * rim :], new_values[2 * rim :]
            dp_ref[0, :, lanes] += fixed_keys
            dp_ref[1, :, lanes] += fixed_values


def gelu_pair(values):
    size = jnp.abs(values) * ROOT_HALF
    bell = jnp.exp(values * values * -0.5)
    t = 1.0 / (1.0 + 0.3275911 * size)
    series = ((((1.061405429 * t - 1.453152027) * t + 1.421413741) * t - 0.284496736) * t + 0.254829592) * t
    tail = 0.5 * series * bell
    below = jnp.where(values < 0, tail, 1.0 - tail)
    return values * below, below + values * bell * (1.0 / math.sqrt(2.0 * math.pi))


def normalize(values):
    center = values - jnp.mean(values, axis=-1, keepdims=True)
    scale = lax.rsqrt(jnp.mean(center * center, axis=-1, keepdims=True) + 1e-05)
    return center * scale, scale


def norm_grad(grad, unit, scale, gain):
    inner = grad * gain
    first = jnp.mean(inner, axis=-1, keepdims=True)
    second = jnp.mean(inner * unit, axis=-1, keepdims=True)
    return scale * (inner - first - unit * second)


def each(count, step, body):
    @pl.loop(0, count)
    def _(i):
        body(pl.ds(pl.multiple_of(i * step, step), step))


class Place:
    def __init__(self, seqs, tok):
        self.seqs, self.tok, self.rows = seqs, tok, seqs * tok
        self.wide_size = lax.axis_size("wide")
        self.parts = self.wide_size // seqs
        self.row, self.wide = lax.axis_index("rows"), lax.axis_index("wide")
        self.seq, self.part = lax.div(self.wide, self.parts), lax.rem(self.wide, self.parts)

    def others(self, body):
        @pl.loop(1, self.wide_size)
        def _(step):
            body(lax.rem(self.wide + step, self.wide_size))

    def barrier(self, more):
        sem = pltpu.get_barrier_semaphore()
        self.others(lambda other: pl.semaphore_signal(sem, inc=1, device_id=(self.row, other), device_id_type=MESH))
        for row in more:
            pl.semaphore_signal(sem, inc=1, device_id=(row, self.wide), device_id_type=MESH)
        pl.semaphore_wait(sem, self.wide_size - 1 + len(more))

    def remote(self, src, dst, send, recv, device):
        return pltpu.make_async_remote_copy(
            src_ref=src, dst_ref=dst, send_sem=send, recv_sem=recv, device_id=device, device_id_type=MESH
        )

    def send_out(self, parts, target, send, recv, own):
        block = lax.rem(self.wide, self.seqs)
        for s in range(self.seqs):
            goal = s * self.parts + lax.div(self.wide, self.seqs)

            @pl.when(goal != self.wide)
            def _():
                self.remote(parts(s), target(block), send, recv.at[block], (self.row, goal)).start()

            @pl.when(goal == self.wide)
            def _():
                pltpu.make_async_copy(parts(s), target(block), own).start()

    def sent_out(self, parts, target, send, recv, own):
        block = lax.rem(self.wide, self.seqs)
        for s in range(self.seqs):
            goal = s * self.parts + lax.div(self.wide, self.seqs)

            @pl.when(goal != self.wide)
            def _():
                self.remote(parts(s), target(block), send, recv.at[block], (self.row, goal)).wait_send()

    def got_out(self, parts, target, send, recv, own):
        for b in range(self.seqs):
            source = self.part * self.seqs + b

            @pl.when(source != self.wide)
            def _():
                self.remote(parts(0), target(b), send, recv.at[b], (self.row, self.wide)).wait_recv()

            @pl.when(source == self.wide)
            def _():
                pltpu.make_async_copy(parts(0), target(b), own).wait()

    def send_home_block(self, b, part, target, send, recv, own):
        goal = self.part * self.seqs + b

        @pl.when(goal != self.wide)
        def _():
            self.remote(part, target(self.seq), send, recv.at[self.seq], (self.row, goal)).start()

        @pl.when(goal == self.wide)
        def _():
            pltpu.make_async_copy(part, target(self.seq), own).start()

    def sent_home(self, part, target, send, recv):
        for b in range(self.seqs):
            goal = self.part * self.seqs + b

            @pl.when(goal != self.wide)
            def _():
                self.remote(part, target(self.seq), send, recv.at[self.seq], (self.row, goal)).wait_send()

    def got_home(self, s, part, target, send, recv, own):
        source = s * self.parts + lax.div(self.wide, self.seqs)

        @pl.when(source != self.wide)
        def _():
            self.remote(part, target(s), send, recv.at[s], (self.row, self.wide)).wait_recv()

        @pl.when(source == self.wide)
        def _():
            pltpu.make_async_copy(part, target(s), own).wait()


class Gather:
    def __init__(self, shards, full, sems):
        self.shards = shards
        self.full = full
        self.send_sem, self.zs, self.xs, self.ys, self.ds, self.cz, self.cx, self.cy, self.cd, self.cown, self.own = sems
        self.row = lax.axis_index("rows")
        self.wide = lax.axis_index("wide")
        self.z, self.core = lax.div(self.wide, 2), lax.rem(self.wide, 2)
        self.shard_rows = shards[0].shape[1]
        self.unit_rows = self.shard_rows // 4
        self.row_x = self.row + 1 - 2 * lax.rem(self.row, 2)
        self.row_y = lax.rem(self.row + 2, 4)
        self.row_d = 3 - self.row

    def unit(self, layer, member, z, core, quarter):
        start = (z * 2 + core) * self.shard_rows + quarter * self.unit_rows
        return self.full.at[layer, member, pl.ds(pl.multiple_of(start, self.unit_rows), self.unit_rows)]

    def shard(self, layer, member, z, core):
        start = (z * 2 + core) * self.shard_rows
        return self.full.at[layer, member, pl.ds(pl.multiple_of(start, self.shard_rows), self.shard_rows)]

    def copy(self, src, dst, recv, kind):
        if kind == "x":
            device = (self.row_x, self.wide)
        elif kind == "y":
            device = (self.row_y, self.wide)
        elif kind == "core":
            device = (self.row, self.z * 2 + 1 - self.core)
        else:
            device = (self.row, self.wide + 2 - 4 * kind)
        return pltpu.make_async_remote_copy(
            src_ref=src, dst_ref=dst, send_sem=self.send_sem, recv_sem=recv, device_id=device, device_id_type=MESH
        )

    def start_z(self, layer):
        for member in range(2):
            start = pl.multiple_of(self.row * self.unit_rows, self.unit_rows)
            mine = self.shards[member].at[layer, pl.ds(start, self.unit_rows)]
            here = self.unit(layer, member, self.z, self.core, self.row)

            @pl.when(self.z < 3)
            def _():
                self.copy(mine, here, self.zs.at[layer, member, 0, 0], 0).start()

            @pl.when(self.z > 0)
            def _():
                self.copy(mine, here, self.zs.at[layer, member, 0, 1], 1).start()

    def start_core(self, layer):
        for member in range(2):
            place = self.shard(layer, member, self.z, self.core)
            pltpu.make_async_copy(self.shards[member].at[layer], place, self.own.at[layer, member]).start()
            self.copy(self.shards[member].at[layer], place, self.cown.at[layer, member], "core").start()

    def slot(self, i):
        near = jnp.minimum(self.z, 3 - self.z)
        far_side = 1 - lax.div(self.z, 2)
        both = jnp.minimum(lax.div(i, jnp.maximum(2 * near, 1)), 1) + (1 - jnp.minimum(near, 1))
        both = 1 - jnp.minimum(both, 1)
        step = both * lax.div(i, 2) + (1 - both) * (i - near)
        side = both * lax.rem(i, 2) + (1 - both) * far_side
        return step, side, self.z + (1 + step) * (2 * side - 1)

    def on_z(self, layer, i):
        step, side, origin = self.slot(i)
        for member in range(2):
            unit = self.unit(layer, member, origin, self.core, self.row)
            self.copy(unit, unit, self.zs.at[layer, member, step, side], "x").wait_recv()
            target = self.z + 1 - 2 * side

            @pl.when((target >= 0) & (target < 4))
            def _():
                self.copy(unit, unit, self.zs.at[layer, member, step + 1, side], side).start()

            self.copy(unit, unit, self.xs.at[layer, member, step, side], "x").start()
            self.copy(unit, unit, self.ys.at[layer, member, step, side], "y").start()
            self.copy(unit, unit, self.cz.at[layer, member, step, side], "core").start()

    def on_xy(self, layer, i):
        step, side, origin = self.slot(i)
        for member in range(2):
            unit = self.unit(layer, member, origin, self.core, self.row_x)
            self.copy(unit, unit, self.xs.at[layer, member, step, side], "x").wait_recv()
            if member == 0:
                self.copy(unit, unit, self.ds.at[layer, member, step, side], "y").start()
            self.copy(unit, unit, self.cx.at[layer, member, step, side], "core").start()
            unit = self.unit(layer, member, origin, self.core, self.row_y)
            self.copy(unit, unit, self.ys.at[layer, member, step, side], "y").wait_recv()
            if member == 1:
                self.copy(unit, unit, self.ds.at[layer, member, step, side], "x").start()
            self.copy(unit, unit, self.cy.at[layer, member, step, side], "core").start()

    def on_d(self, layer, i):
        step, side, origin = self.slot(i)
        for member in range(2):
            unit = self.unit(layer, member, origin, self.core, self.row_d)
            self.copy(unit, unit, self.ds.at[layer, member, step, side], "x").wait_recv()
            self.copy(unit, unit, self.cd.at[layer, member, step, side], "core").start()

    def on_core(self, layer, i):
        step, side, origin = self.slot(i)
        for member in range(2):
            for sem, quarter in ((self.cz, self.row), (self.cx, self.row_x), (self.cy, self.row_y), (self.cd, self.row_d)):
                unit = self.unit(layer, member, origin, 1 - self.core, quarter)
                self.copy(unit, unit, sem.at[layer, member, step, side], "core").wait_recv()

    def on_own(self, layer):
        for member in range(2):
            place = self.shard(layer, member, self.z, self.core)
            pltpu.make_async_copy(self.shards[member].at[layer], place, self.own.at[layer, member]).wait()
            place = self.shard(layer, member, self.z, 1 - self.core)
            self.copy(place, place, self.cown.at[layer, member], "core").wait_recv()

    def drain(self, layers):
        def wait(units):
            span = self.full.at[0, 0, pl.ds(0, units * self.unit_rows)]
            self.copy(span, span, self.own.at[0, 0], "core").wait_send()

        @pl.loop(0, layers)
        def _(layer):
            wait(8)

            @pl.when(self.z < 3)
            def _():
                wait(2)

            @pl.when(self.z > 0)
            def _():
                wait(2)

            @pl.loop(0, 3)
            def _(i):
                step, side, origin = self.slot(i)
                target = self.z + 1 - 2 * side

                @pl.when((target >= 0) & (target < 4))
                def _():
                    wait(2)

                wait(14)


def gather_sems(layers):
    return (
        [pltpu.SemaphoreType.DMA]
        + [pltpu.SemaphoreType.DMA((layers, 2, 3, 2))] * 8
        + [pltpu.SemaphoreType.DMA((layers, 2))] * 2
    )


def forward_kernel(
    fast, seqs, tok, rim,
    tokens, cotangent, w_qkv, w_out, w_up, w_down, full_in,
    hide, b_qkv, b_out, gains, shifts, b_up, b_down, prefix,
    y_low, cot_out, full_out, q_out, k_out, v_out, unit_out, scale_out, slope_out, lse_out,
    full, wqkv, wout, x, low, acc, q, k, v, halo, context, slope, unit1, unit2, scale1, scale2, lse, bias,
    load_sem, store_sem, slope_sem, full_sem, tok_send, tok_recv, tok_own, cot_send, cot_recv, cot_own,
    halo_send, halo_recv, bias_send, bias_recv, bias_own,
    *gather_sem,
):
    layers, width = w_qkv.shape[0], tokens.shape[2]
    place = Place(seqs, tok)
    rows = place.rows
    gather = Gather((w_up, w_down), full, gather_sem) if fast else None
    place.barrier((gather.row_x, gather.row_y) if fast else ())
    own_bias = bias.at[place.wide]

    def load(layer):
        return (
            pltpu.make_async_copy(w_qkv.at[layer], wqkv, load_sem.at[0]),
            pltpu.make_async_copy(w_out.at[layer], wout, load_sem.at[1]),
        )

    def put_bias(other):
        return place.remote(b_up, own_bias, bias_send, bias_recv.at[place.wide], (place.row, other))

    def got_bias(other):
        return place.remote(b_up, bias.at[other], bias_send, bias_recv.at[other], (place.row, other))

    if fast:
        gather.start_z(0)
        gather.start_core(0)
    else:
        pltpu.make_async_copy(full_in, full, full_sem.at[0]).start()
    for copy in load(0):
        copy.start()
    place.others(lambda other: put_bias(other).start())
    pltpu.make_async_copy(b_up, own_bias, bias_own).start()

    tok_args = (lambda s: tokens.at[s], lambda b: low.at[pl.ds(pl.multiple_of(b * tok, tok), tok)], tok_send, tok_recv, tok_own)
    cot_args = (lambda s: cotangent.at[s], lambda b: cot_out.at[pl.ds(pl.multiple_of(b * tok, tok), tok)], cot_send, cot_recv, cot_own)
    events = []
    if fast:
        gather.on_z(0, 0)
        place.send_out(*tok_args)
        gather.on_z(0, 1)
        gather.on_xy(0, 0)
        gather.start_z(1)
        gather.start_core(1)
        gather.on_z(0, 2)
        gather.on_xy(0, 1)
        events = [
            (gather.on_d, 0, 0), (gather.on_xy, 0, 2), (gather.on_z, 1, 0), (gather.on_d, 0, 1), (gather.on_d, 0, 2),
            (gather.on_z, 1, 1), (gather.on_z, 1, 2), (gather.on_xy, 1, 0),
        ]
    else:
        place.send_out(*tok_args)

    def tick(count=1):
        for _ in range(min(count, len(events))):
            event, layer, i = events.pop(0)
            event(layer, i)

    blank = jnp.zeros((rim, width), jnp.bfloat16)

    @pl.when(place.part == 0)
    def _():
        k[pl.ds(0, rim)] = blank
        v[pl.ds(0, rim)] = blank

    @pl.when(place.part == place.parts - 1)
    def _():
        k[pl.ds(rim + rows, rim)] = blank
        v[pl.ds(rim + rows, rim)] = blank

    place.got_out(*tok_args)

    def halo_copy(layer, member, side, wide):
        ref = (k, v)[member]
        return place.remote(
            ref.at[pl.ds((rows, rim)[side], rim)], halo.at[layer, member, side],
            halo_send.at[member, side], halo_recv.at[layer, member, side], (place.row, wide),
        )

    def halos(body, to):
        for side in range(2):
            @pl.when(place.part < place.parts - 1 if (side == 0) == to else place.part > 0)
            def _():
                for member in range(2):
                    body(member, side, jnp.clip(place.wide + (1 - 2 * side), 0, place.wide_size - 1))

    def got_halo(layer, member, side, wide):
        halo_copy(layer, member, side, place.wide).wait_recv()
        (k, v)[member][pl.ds((0, rim + rows)[side], rim)] = halo[layer, member, side]

    def kept(layer):
        return [
            pltpu.make_async_copy(src, dst.at[layer], store_sem.at[i])
            for i, (src, dst) in enumerate(((q, q_out), (k, k_out), (v, v_out)))
        ]

    def kept_norm(layer, which):
        unit, scale = ((unit1, scale1), (unit2, scale2))[which]
        return [
            pltpu.make_async_copy(unit, unit_out.at[layer, which], store_sem.at[3 + which]),
            pltpu.make_async_copy(scale, scale_out.at[layer, which], store_sem.at[5 + which]),
        ]

    half = width // 2
    for layer in range(layers):
        if layer > 0:
            for copy in kept(layer - 1) + kept_norm(layer - 1, 0) + kept_norm(layer - 1, 1):
                copy.wait()
        load(layer)[0].wait()
        for part in (2, 3, 4, 5, 0, 1):
            lanes = pl.ds(part * half, half)
            made = multiply(low[...], wqkv[:, lanes]) + b_qkv[layer, :, lanes]
            kind, side = part // 2, pl.ds((part % 2) * half, half)
            if kind == 0:
                q[:, side] = made.astype(jnp.bfloat16) * (1.0 / math.sqrt(width // HEADS))
            else:
                (k, v)[kind - 1][pl.ds(rim, rows), side] = made.astype(jnp.bfloat16)
            if part == 5:
                tick()
                halos(lambda *at: halo_copy(layer, *at).start(), True)
        if layer + 1 < layers:
            load(layer + 1)[0].start()
        tick()
        halos(lambda *at: got_halo(layer, *at), False)
        halos(lambda *at: halo_copy(layer, *at).wait_send(), True)
        for copy in kept(layer):
            copy.start()

        for first in (0, 4):
            @pl.loop(first, first + 4)
            def _(pair):
                attend(seqs, tok, rim, pair, q, k, v, prefix.at[layer], hide, context, lse.at[layer])

            tick()
        load(layer)[1].wait()
        for part in range(2):
            lanes = pl.ds(part * half, half)
            acc[:, lanes] = multiply(context[...], wout[:, lanes])
        if layer + 1 < layers:
            load(layer + 1)[1].start()
        tick()

        def first_norm(at):
            before = low[at].astype(jnp.float32) if layer == 0 else x[at]
            unit, scale = normalize(before + acc[at] + b_out[layer])
            unit1[at] = unit.astype(jnp.bfloat16)
            scale1[at] = jnp.broadcast_to(scale, (scale.shape[0], LANES))
            normed = unit * gains[layer, 0] + shifts[layer, 0]
            low[at] = normed.astype(jnp.bfloat16)
            acc[at] = normed + b_down[layer]

        each(rows // 64, 64, first_norm)
        for copy in kept_norm(layer, 0):
            copy.start()
        tick()
        if layer == 0:
            pltpu.make_async_copy(b_up, own_bias, bias_own).wait()
            place.others(lambda other: got_bias(other).wait_recv())

            place.others(lambda other: put_bias(other).wait_send())
            if not fast:
                pltpu.make_async_copy(full_in, full, full_sem.at[0]).wait()

        hidden = b_up.shape[1] // layers

        @pl.loop(0, full.shape[2] // SPAN)
        def _(i):
            spot = i
            if fast:
                @pl.when(i == 0)
                def _():
                    gather.on_own(layer)

                @pl.when(i > 0)
                def _():
                    if layer == 1:
                        @pl.when(i > 1)
                        def _():
                            gather.on_xy(1, i - 1)

                        gather.on_d(1, i - 1)
                    gather.on_core(layer, i - 1)

                origin = gather.slot(jnp.maximum(i - 1, 0))[2]
                started = jnp.minimum(i, 1)
                spot = started * origin + (1 - started) * gather.z
            units = pl.ds(pl.multiple_of(spot * SPAN, SPAN), SPAN)
            slot = lax.rem(i, 2)
            step_bias = jnp.concatenate(
                [bias[spot * (SPAN // hidden) + n, :, pl.ds(layer * hidden, hidden)] for n in range(SPAN // hidden)], axis=1
            )

            @pl.when(i > 1)
            def _():
                pltpu.make_async_copy(slope.at[slot], slope_out.at[layer, spot], slope_sem.at[slot]).wait()

            for part in range(2):
                at = pl.ds(part * (rows // 2), rows // 2)
                act, rise = gelu_pair(multiply_back(low[at], full[layer, 0, units]) + step_bias)
                slope[slot, at] = rise.astype(jnp.bfloat16)
                acc[at] += multiply(act.astype(jnp.bfloat16), full[layer, 1, units])
            pltpu.make_async_copy(slope.at[slot], slope_out.at[layer, spot], slope_sem.at[slot]).start()
            if fast:
                pltpu.make_async_copy(full.at[layer, :, units], full_out.at[layer, :, units], full_sem.at[layer]).start()

        for slot in range(2):
            pltpu.make_async_copy(slope.at[slot], slope_out.at[layer, 0], slope_sem.at[slot]).wait()

        def second_norm(at):
            unit, scale = normalize(acc[at])
            unit2[at] = unit.astype(jnp.bfloat16)
            scale2[at] = jnp.broadcast_to(scale, (scale.shape[0], LANES))
            after = unit * gains[layer, 1] + shifts[layer, 1]
            low[at] = after.astype(jnp.bfloat16)
            if layer + 1 < layers:
                x[at] = after

        each(rows // 64, 64, second_norm)
        for copy in kept_norm(layer, 1):
            copy.start()
        if layer == 0:
            place.send_out(*cot_args)
            tick(2)
    last = [pltpu.make_async_copy(low, y_low, store_sem.at[7]), pltpu.make_async_copy(lse, lse_out, store_sem.at[8])]
    for copy in last:
        copy.start()
    place.sent_out(*tok_args)
    place.got_out(*cot_args)
    place.sent_out(*cot_args)
    for copy in last + kept(layers - 1) + kept_norm(layers - 1, 0) + kept_norm(layers - 1, 1):
        copy.wait()
    if fast:
        gather.drain(layers)
        for layer in range(layers):
            pltpu.make_async_copy(full.at[layer], full_out.at[layer], full_sem.at[layer]).wait()


def forward(fast, tokens, cotangent, w_qkv, w_out, w_up, w_down, full_in, hide, b_qkv, b_out, gains, shifts, b_up, b_down, prefix):
    seqs, tok, width = tokens.shape
    layers, rim, rows = w_qkv.shape[0], PAIR_MAX, seqs * tok
    wides = lax.axis_size("wide")
    units = w_up.shape[1] * wides
    low, full_type = jnp.bfloat16, jnp.float32
    spans = units // SPAN
    shape = jax.ShapeDtypeStruct
    dma = pltpu.SemaphoreType.DMA
    scores = (layers, width // LANES * seqs, 1, 2 * tok)
    return pl.pallas_call(
        functools.partial(forward_kernel, fast, seqs, tok, rim),
        out_shape=(
            shape((rows, width), low), shape((rows, width), low), shape((layers, 2, units, width), low),
            shape((layers, rows, width), low), shape((layers, rows + 2 * rim, width), low),
            shape((layers, rows + 2 * rim, width), low), shape((layers, 2, rows, width), low),
            shape((layers, 2, rows, LANES), full_type), shape((layers, spans, rows, SPAN), low), shape(scores, full_type),
        ),
        in_specs=[pl.BlockSpec(memory_space=pl.ANY)] * 7 + [pl.BlockSpec(memory_space=pltpu.VMEM)] * 8,
        out_specs=(pl.BlockSpec(memory_space=pl.ANY),) * 10,
        scratch_shapes=[
            pltpu.VMEM((layers, 2, units, width), low), pltpu.VMEM(w_qkv.shape[1:], low), pltpu.VMEM(w_out.shape[1:], low),
            pltpu.VMEM((rows, width), full_type), pltpu.VMEM((rows, width), low), pltpu.VMEM((rows, width), full_type),
            pltpu.VMEM((rows, width), low), pltpu.VMEM((rows + 2 * rim, width), low), pltpu.VMEM((rows + 2 * rim, width), low),
            pltpu.VMEM((layers, 2, 2, rim, width), low), pltpu.VMEM((rows, width), low), pltpu.VMEM((2, rows, SPAN), low),
            pltpu.VMEM((rows, width), low), pltpu.VMEM((rows, width), low),
            pltpu.VMEM((rows, LANES), full_type), pltpu.VMEM((rows, LANES), full_type),
            pltpu.VMEM(scores, full_type), pltpu.VMEM((wides,) + b_up.shape, full_type),
            dma((2,)), dma((9,)), dma((2,)), dma((layers,)), dma, dma((seqs,)), dma, dma, dma((seqs,)), dma,
            dma((2, 2)), dma((layers, 2, 2)), dma, dma((wides,)), dma,
        ] + (gather_sems(layers) if fast else []),
        compiler_params=pltpu.CompilerParams(collective_id=0, has_side_effects=True, vmem_limit_bytes=67043328),
    )(tokens, cotangent, w_qkv, w_out, w_up, w_down, full_in, hide, b_qkv, b_out, gains, shifts, b_up, b_down, prefix)


def backward_kernel(
    seqs, tok, rim,
    y_low, cot_in, full, w_qkv, w_out, q_in, k_in, v_in, unit_in, scale_in, slope_in,
    lse, hide, gains, prefix,
    out, grads, prefix_grads,
    wqkv, wout, q, k, v, unit1, unit2, scale1, scale2, up, down, slope, cot, acc, low, context, made, dk, dv, edge, edge_in, home,
    load_sem, ffn_sem, out_send, out_recv, out_own, home_send, home_recv, home_own, edge_send, edge_recv, store_sem,
):
    layers, width = w_qkv.shape[0], w_qkv.shape[1]
    place = Place(seqs, tok)
    rows = place.rows
    place.barrier(())
    spans = slope_in.shape[1]

    def out_rows(b):
        return y_low.at[pl.ds(b * tok, tok)]

    out_args = (lambda s: out.at[s], out_send, out_recv)
    for b in range(seqs):
        place.send_home_block(b, out_rows(b), *out_args, out_own)

    cot_copy = pltpu.make_async_copy(cot_in, cot, load_sem.at[layers, 0])
    cot_copy.start()

    def loads(layer):
        pairs = (
            (unit_in.at[layer, 1], unit2), (scale_in.at[layer, 1], scale2), (unit_in.at[layer, 0], unit1),
            (scale_in.at[layer, 0], scale1), (w_out.at[layer], wout), (q_in.at[layer], q), (k_in.at[layer], k),
            (v_in.at[layer], v), (w_qkv.at[layer], wqkv),
        )
        return [pltpu.make_async_copy(src, dst.at[layer % 2], load_sem.at[layer, i]) for i, (src, dst) in enumerate(pairs)]

    def ffn_loads(layer, i):
        slot = lax.rem(i, 2)
        units = pl.ds(pl.multiple_of(i * SPAN, SPAN), SPAN)
        return [
            pltpu.make_async_copy(full.at[layer, 1, units], down.at[slot], ffn_sem.at[slot, 0]),
            pltpu.make_async_copy(slope_in.at[layer, i], slope.at[slot], ffn_sem.at[slot, 1]),
            pltpu.make_async_copy(full.at[layer, 0, units], up.at[slot], ffn_sem.at[slot, 2]),
        ]

    order = list(reversed(range(layers)))
    for copy in loads(order[0])[:2]:
        copy.start()
    for i in range(2):
        for copy in ffn_loads(order[0], i):
            copy.start()
    for copy in loads(order[0])[2:]:
        copy.start()
    half = width // 2
    for layer in order:
        here = layer % 2
        mine = loads(layer)
        if layer == order[0]:
            cot_copy.wait()
        if layer > 0:
            for copy in loads(layer - 1):
                copy.start()
        mine[0].wait()
        mine[1].wait()

        def second_norm(at):
            grad = cot[at].astype(jnp.float32) if layer == order[0] else acc[at]
            grad = norm_grad(grad, unit2[here, at].astype(jnp.float32), scale2[here, at, :1], gains[layer, 1])
            acc[at] = grad
            low[at] = grad.astype(jnp.bfloat16)

        each(rows // 64, 64, second_norm)

        @pl.loop(0, spans)
        def _(i):
            slot = lax.rem(i, 2)
            for copy in ffn_loads(layer, i):
                copy.wait()
            for part in range(2):
                at = pl.ds(part * (rows // 2), rows // 2)
                grad = multiply_back(low[at], down[slot]) * slope[slot, at].astype(jnp.float32)
                acc[at] += multiply(grad.astype(jnp.bfloat16), up[slot])

            @pl.when(i + 2 < spans)
            def _():
                for copy in ffn_loads(layer, i + 2):
                    copy.start()

        if layer > 0:
            for i in range(2):
                for copy in ffn_loads(layer - 1, i):
                    copy.start()
        mine[2].wait()
        mine[3].wait()

        def first_norm(at):
            grad = norm_grad(acc[at], unit1[here, at].astype(jnp.float32), scale1[here, at, :1], gains[layer, 0])
            acc[at] = grad
            low[at] = grad.astype(jnp.bfloat16)

        each(rows // 64, 64, first_norm)
        mine[4].wait()
        for part in range(2):
            span = pl.ds(part * half, half)
            context[:, span] = multiply_back(low[...], wout[here, span]).astype(jnp.bfloat16)
        for copy in mine[5:8]:
            copy.wait()

        @pl.loop(0, width // LANES)
        def _(pair):
            attend_back(
                seqs, tok, rim, pair, q.at[here], k.at[here], v.at[here], prefix.at[layer], hide, lse.at[layer], context,
                made, dk, dv, prefix_grads.at[layer], 1.0 / math.sqrt(width // HEADS),
            )

        low_edge, high_edge, own_rows = pl.ds(0, rim), pl.ds(rim + rows, rim), pl.ds(rim, rows)
        for member, ref in enumerate((dk, dv)):
            lanes = pl.ds(member * width, width)
            edge[layer, 0, :, lanes] = ref[low_edge].astype(jnp.bfloat16)
            edge[layer, 1, :, lanes] = ref[high_edge].astype(jnp.bfloat16)

        def edge_copy(side, wide):
            return place.remote(
                edge.at[layer, side], edge_in.at[layer, side], edge_send.at[layer, side], edge_recv.at[layer, side], (place.row, wide)
            )

        mine[8].wait()
        for part in range(2):
            span = pl.ds(part * half, half)
            acc[:, span] += multiply_back(made[:, pl.ds(0, width)], wqkv[here, span, pl.ds(0, width)])
            if part == 0:
                @pl.when(place.part > 0)
                def _():
                    edge_copy(0, place.wide - 1).start()

                @pl.when(place.part < place.parts - 1)
                def _():
                    edge_copy(1, place.wide + 1).start()

        @pl.when(place.part < place.parts - 1)
        def _():
            edge_copy(0, place.wide).wait_recv()
            for member, ref in enumerate((dk, dv)):
                ref[pl.ds(rows, rim)] += edge_in[layer, 0, :, pl.ds(member * width, width)].astype(jnp.float32)

        @pl.when(place.part > 0)
        def _():
            edge_copy(1, place.wide).wait_recv()
            for member, ref in enumerate((dk, dv)):
                ref[pl.ds(rim, rim)] += edge_in[layer, 1, :, pl.ds(member * width, width)].astype(jnp.float32)

        for member, ref in enumerate((dk, dv)):
            def lower(at):
                made[at, pl.ds((1 + member) * width, width)] = ref[pl.ds(pl.multiple_of(at.start + rim, 64), 64)].astype(jnp.bfloat16)

            each(rows // 64, 64, lower)

        @pl.when(place.part > 0)
        def _():
            edge_copy(0, place.wide).wait_send()

        @pl.when(place.part < place.parts - 1)
        def _():
            edge_copy(1, place.wide).wait_send()

        others = pl.ds(width, 2 * width)
        for part in range(2):
            span = pl.ds(part * half, half)
            acc[:, span] += multiply_back(made[:, others], wqkv[here, span, others])

    low[...] = acc[...].astype(jnp.bfloat16)
    home_args = (lambda s: home.at[s], home_send, home_recv)
    for b in range(seqs):
        place.send_home_block(b, low.at[pl.ds(b * tok, tok)], *home_args, home_own)
    for s in range(seqs):
        place.got_home(s, low.at[pl.ds(0, tok)], *home_args, home_own)
        acc[pl.ds(s * tok, tok)] = home[s].astype(jnp.float32)
        pltpu.make_async_copy(acc.at[pl.ds(s * tok, tok)], grads.at[s], store_sem.at[s]).start()
    place.sent_home(low.at[pl.ds(0, tok)], *home_args)
    place.sent_home(out_rows(0), *out_args)
    for s in range(seqs):
        place.got_home(s, out_rows(0), *out_args, out_own)
        pltpu.make_async_copy(acc.at[pl.ds(s * tok, tok)], grads.at[s], store_sem.at[s]).wait()


def backward(y_low, cot, full, w_qkv, w_out, q, k, v, unit, scale, slope, lse, hide, gains, prefix, seqs):
    rows, width = y_low.shape
    layers, rim, tok = w_qkv.shape[0], PAIR_MAX, rows // seqs
    low, full_type = jnp.bfloat16, jnp.float32
    shape = jax.ShapeDtypeStruct
    dma = pltpu.SemaphoreType.DMA
    vmem = pltpu.VMEM
    return pl.pallas_call(
        functools.partial(backward_kernel, seqs, tok, rim),
        out_shape=(shape((seqs, tok, width), low), shape((seqs, tok, width), full_type), shape(prefix.shape, full_type)),
        in_specs=[pl.BlockSpec(memory_space=pl.ANY)] * 11 + [pl.BlockSpec(memory_space=pltpu.VMEM)] * 4,
        out_specs=(pl.BlockSpec(memory_space=pl.ANY),) * 2 + (pl.BlockSpec(memory_space=pltpu.VMEM),),
        scratch_shapes=[
            vmem((2,) + w_qkv.shape[1:], low), vmem((2,) + w_out.shape[1:], low), vmem((2, rows, width), low),
            vmem((2, rows + 2 * rim, width), low), vmem((2, rows + 2 * rim, width), low),
            vmem((2, rows, width), low), vmem((2, rows, width), low), vmem((2, rows, LANES), full_type), vmem((2, rows, LANES), full_type),
            vmem((2, SPAN, width), low), vmem((2, SPAN, width), low), vmem((2, rows, SPAN), low),
            vmem((rows, width), low), vmem((rows, width), full_type), vmem((rows, width), low), vmem((rows, width), low),
            vmem((rows, 3 * width), low), vmem((rows + 2 * rim, width), full_type), vmem((rows + 2 * rim, width), full_type),
            vmem((layers, 2, rim, 2 * width), low), vmem((layers, 2, rim, 2 * width), low), vmem((seqs, tok, width), low),
            dma((layers + 1, 9)), dma((2, 3)), dma, dma((seqs,)), dma, dma, dma((seqs,)), dma, dma((layers, 2)), dma((layers, 2)), dma((seqs,)),
        ],
        compiler_params=pltpu.CompilerParams(collective_id=1, has_side_effects=True, vmem_limit_bytes=67043328),
    )(y_low, cot, full, w_qkv, w_out, q, k, v, unit, scale, slope, lse, hide, gains, prefix)


def local(
    tokens,
    segments,
    w_qkv,
    b_qkv,
    w_out,
    b_out,
    norm_gain,
    norm_bias,
    w_up,
    b_up,
    w_down,
    b_down,
    prefix,
    cotangent,
):
    seqs, tok, width = tokens.shape
    layers, rim, rows = w_qkv.shape[0], PAIR_MAX, seqs * tok
    wides = lax.axis_size("wide")
    fast = wides == 8 and lax.axis_size("rows") == 4
    parts = wides // seqs
    wide = lax.axis_index("wide")
    ids = jnp.pad(segments, ((0, 0), (rim, rim)), constant_values=-1)
    ids = lax.dynamic_slice(ids, (lax.div(wide, parts), lax.rem(wide, parts) * rows), (1, rows + 2 * rim))[0]
    hide = jnp.stack(
        [
            jnp.where(ids[b * tok : b * tok + tok + 2 * rim, None] == ids[None, b * tok + rim : b * tok + rim + tok], 0.0, -1e30)
            for b in range(seqs)
        ]
    )
    full_in = w_up
    if not fast:
        full_in = jnp.stack([lax.all_gather(w, "wide", axis=1, tiled=True) for w in (w_up, w_down)], axis=1)
    gains, shifts = norm_gain[:, :, None], norm_bias[:, :, None]
    y_low, cot, full, q, k, v, unit, scale, slope, lse = forward(
        fast, tokens, cotangent, w_qkv, w_out, w_up, w_down, full_in, hide, b_qkv[:, None], b_out[:, None], gains, shifts,
        b_up.astype(jnp.float32).reshape(1, -1), b_down[:, None], prefix,
    )
    output, grads, prefix_grads = backward(
        y_low, cot, full if fast else full_in, w_qkv, w_out, q, k, v, unit, scale, slope, lse, hide, gains, prefix, seqs
    )
    return output, grads, lax.psum(prefix_grads, ("rows", "wide"))


def solution(mesh):
    return jax.shard_map(
        local,
        mesh=mesh,
        in_specs=(
            P("rows", "wide", None),
            P("rows", None),
            P(),
            P(),
            P(),
            P(),
            P(),
            P(),
            P(None, "wide", None),
            P(None, "wide"),
            P(None, "wide", None),
            P(),
            P(),
            P("rows", "wide", None),
        ),
        out_specs=(P("rows", "wide", None), P("rows", "wide", None), P()),
        check_vma=False,
    )
```

time: 847 us -> 464 us (0.55)
  Pallas kernels: 0 us -> 300 us
  matrix products: 257 us -> 0 us
  blocking collectives: 165 us -> 0 us
  local copies, waits for them, and re-layouts: 136 us -> 13.6 us
  other arithmetic: 101 us -> 1.95 us
  starting transfers between devices: 20.1 us -> 0.04 us
  waiting for transfers between devices: 143 us -> 127 us
    pallas_call x0 -> x2, Pallas kernels: none -> 300 us  [the longest x1 162 us: forward(): pl.pallas_call(functools.partial(forward_kernel, fast, seqs, tok, rim), o...]
    dot_general x26 -> x0, matrix products: 257 us -> none  [the longest x8 87.2 us: multiply(): return jnp.dot(left, right, preferred_element_type=jnp.float32)]
    all_gather x2 -> x0, blocking collectives: 165 us -> none  [local(): bias_rows = lax.all_gather(b_up[layer_index], 'wide', axis=0, tiled=True)]
    slice x22 -> x1, local copies, waits for them, and re-layouts: 52.7 us -> 0.93 us  [local(): ids[b * tok:b * tok + tok + 2 * rim, None]]
    unnamed x145 -> x8, local copies, waits for them, and re-layouts: 41.8 us -> 5.24 us
    reduce_sum x14 -> x0, other arithmetic: 36.2 us -> none  [the longest x2 18 us: local(): denominator = jnp.sum(exp_scores, axis=2, keepdims=True)]
    concatenate x9 -> x0, local copies, waits for them, and re-layouts: 31.6 us -> none  [the longest x4 24.8 us: with_prefix(): return split_heads(jnp.concatenate([fixed_rows, window_part], axis=1))]
    another operation x7 -> x1, other arithmetic: 26 us -> 0.93 us  [local(): jnp.stack([jnp.where(ids[b * tok:b * tok + tok + 2 * rim, None] == ids[No...]
  transfers between devices with their start and end apart: 13 -> 1, of which waited for: 3 -> 1; matrix products, arithmetic and copies ran while one was open for 28% -> 0% of each run, Pallas kernels for 0% -> 0%
where the time goes in v2:
time: 464 us; the launch traced here: 457 us
  Pallas kernels  300 us (65%)
  waiting for transfers between devices  127 us (27%)
  between operations  14.5 us (3%)
  local copies, waits for them, and re-layouts  13.6 us (3%)
    pallas_call x1, Pallas kernels, forward(): pl.pallas_call(functools.partial(forward_kernel, fast, seqs, tok, rim), o...  162 us
    pallas_call x1, Pallas kernels, backward(): pl.pallas_call(functools.partial(backward_kernel, seqs, tok, rim), out_sh...  138 us
    psum x1, waiting for transfers between devices, local(): return (output, grads, lax.psum(prefix_grads, ('rows', 'wide')))  127 us
  transfers between devices with their start and end apart: 1, of which 1 were waited for; matrix products, arithmetic and copies ran while one was open for 0% of the time, Pallas kernels for 0%

profile of v2, /device:TPU:9, one launch (start us, length us, event | category | flops | bytes accessed | tf_op | source)
XLA Modules:
  0.0 457.2 jit_solution(2443948107720229060)
XLA Ops:
  7.2 0.0 all-reduce.3.cloned.1.call-start
  7.2 0.9 fusion
  8.2 0.8 fusion.5
  9.0 0.7 convert_bitcast_fusion
  9.7 0.6 copy.17
  10.3 1.3 broadcast_in_dim.40.b_out
  11.6 1.3 broadcast_in_dim.43.b_down
  12.9 1.3 broadcast_in_dim.41.gains
  14.2 1.3 broadcast_in_dim.42.shifts
  15.5 1.4 broadcast_in_dim.39.b_qkv
  16.9 0.2 compare_select_fusion.2
  17.1 0.2 compare_select_fusion
  17.2 0.9 pad_maximum_fusion.hide
  18.2 162.2 %shard_map.157 = (bf16[512,1024]{1,0:T(8,128)(2,1)}, bf16[512,1024]{1,0:T(8,128)(2,1)}, bf16[2,2,4096,1024]{3,2,1,0:T(8,128)(2,1)}, bf16[2,512,1024]{2,1,0:T(8,1...) custom-call(bf16[4,128,1024]{2,1,0:T(8,128)(2,1)} %tokens.1, ...), custom_call_target="tpu_custom_call" | custom-call | tf_op jit(solution)/shard_map/pallas_call | solution.py:623
  180.4 137.9 %shard_map.158 = (bf16[4,128,1024]{2,1,0:T(8,128)(2,1)}, f32[4,128,1024]{2,1,0:T(8,128)}, f32[2,2,64,1024]{3,2,1,0:T(8,128)}) custom-call(bf16[512,1024]{1,0:T(8,128)(2,1)} %get-tuple-element.16.y_low, bf16[512,1024]{1,0:T(8,128)(2,1)} %get-tuple-element.17.cot_in, bf16[2,2,4096,1024]{3,2,1,0:T(8,128)(2,1)} %get-tuple-element.18.full, ...), custom_call_target="tpu_custom_call" | custom-call | tf_op jit(solution)/shard_map/pallas_call | solution.py:836
  318.3 0.0 copy-start
  318.3 0.0 all-reduce.3.cloned.1.call-update
  318.3 126.9 %all-reduce.3.cloned.1.call-done = f32[2,2,64,1024]{3,2,1,0:T(8,128)} async-done(((f32[2,2,64,1024]{3,2,1,0:T(8,128)}), f32[2,2,64,1024]{3,2,1,0:T(8,128)}) %all-reduce.3.cloned.1.call-update) | async-done | bytes 1048592 | tf_op jit(solution)/shard_map/psum | solution.py:896
  445.2 0.0 copy-start.1
  445.2 2.4 copy.22
  447.6 0.0 copy-done
  447.6 1.3 copy.23
  448.9 0.0 copy-done.1
  448.9 1.0 copy.24
Async XLA Ops:
  7.2 438.1 %all-reduce.3.cloned.1.call-start = ((), (), s32[]{:S(2)}) async-start(), calls=%async_computation | async-start | bytes 2097152 | tf_op jit(solution)/shard_map/psum | solution.py:896
  318.3 129.3 %copy-start = (f32[4,128,1024]{2,1,0:T(8,128)S(1)}, f32[4,128,1024]{2,1,0:T(8,128)}, u32[]{:S(2)}) copy-start(f32[4,128,1024]{2,1,0:T(8,128)} %get-tuple-element.45) | copy-start | bytes 6291460
  445.2 3.7 copy-start.1
Sparse Core Ops, SparseCore 0:
  318.5 126.7 all-reduce.2

commit v3 on v2

--- a/solution.py
+++ b/solution.py
@@ -143,8 +143,8 @@
     def barrier(self, more):
         sem = pltpu.get_barrier_semaphore()
         self.others(lambda other: pl.semaphore_signal(sem, inc=1, device_id=(self.row, other), device_id_type=MESH))
-        for row in more:
-            pl.semaphore_signal(sem, inc=1, device_id=(row, self.wide), device_id_type=MESH)
+        for device in more:
+            pl.semaphore_signal(sem, inc=1, device_id=device, device_id_type=MESH)
         pl.semaphore_wait(sem, self.wide_size - 1 + len(more))
 
     def remote(self, src, dst, send, recv, device):
@@ -358,6 +358,87 @@
                     wait(2)
 
                 wait(14)
+
+
+class PrefixSum:
+    def __init__(self, place, parts, inbox, planes, total, sems):
+        self.parts, self.inbox, self.planes, self.total = parts, inbox, planes, total
+        self.send_sem, self.in_sem, self.plane_sem, self.total_sem = sems
+        self.row = place.row
+        self.z, self.core = lax.div(place.wide, 2), lax.rem(place.wide, 2)
+        self.me = self.row * 2 + self.core
+        self.size = inbox.shape[2]
+
+    def peers(self, body):
+        @pl.loop(1, 8)
+        def _(step):
+            body(lax.rem(self.me + step, 8))
+
+    def others(self):
+        return [(lax.rem(self.row + step, 4), self.z * 2 + core) for step in range(1, 4) for core in range(2)]
+
+    def piece(self, ref, layer, index):
+        start = lax.rem(index, 4) * self.size
+        return ref.at[layer, lax.div(index, 4), pl.ds(pl.multiple_of(start, self.size), self.size)]
+
+    def copy(self, src, dst, recv, row, wide):
+        return pltpu.make_async_remote_copy(
+            src_ref=src, dst_ref=dst, send_sem=self.send_sem, recv_sem=recv, device_id=(row, wide), device_id_type=MESH
+        )
+
+    def in_copy(self, layer, peer, origin):
+        return self.copy(
+            self.piece(self.parts, layer, peer), self.inbox.at[layer, origin], self.in_sem.at[layer, origin],
+            lax.div(peer, 2), self.z * 2 + lax.rem(peer, 2),
+        )
+
+    def plane_copy(self, layer, z, origin):
+        place = self.planes.at[layer, origin]
+        return self.copy(place, place, self.plane_sem.at[layer, origin], self.row, z * 2 + self.core)
+
+    def total_copy(self, layer, peer, origin):
+        place = self.piece(self.total, layer, origin)
+        return self.copy(place, place, self.total_sem.at[layer, origin], lax.div(peer, 2), self.z * 2 + lax.rem(peer, 2))
+
+    def planes_others(self, body):
+        @pl.loop(1, 4)
+        def _(step):
+            body(lax.rem(self.z + step, 4))
+
+    def start(self, layer):
+        self.peers(lambda peer: self.in_copy(layer, peer, self.me).start())
+
+    def middle(self, layer):
+        self.peers(lambda peer: self.in_copy(layer, self.me, peer).wait_recv())
+        value = self.piece(self.parts, layer, self.me)[...]
+        for step in range(1, 8):
+            value += self.inbox[layer, lax.rem(self.me + step, 8)]
+        self.planes[layer, self.z] = value
+        self.planes_others(lambda z: self.plane_copy(layer, z, self.z).start())
+
+    def last(self, layer):
+        self.planes_others(lambda z: self.plane_copy(layer, self.z, z).wait_recv())
+        value = self.planes[layer, 0]
+        for z in range(1, 4):
+            value += self.planes[layer, z]
+        self.piece(self.total, layer, self.me)[...] = value
+        self.peers(lambda peer: self.total_copy(layer, peer, self.me).start())
+
+    def finish(self, layer):
+        self.peers(lambda peer: self.total_copy(layer, self.me, peer).wait_recv())
+        self.peers(lambda peer: self.in_copy(layer, peer, self.me).wait_send())
+        self.planes_others(lambda z: self.plane_copy(layer, z, self.z).wait_send())
+        self.peers(lambda peer: self.total_copy(layer, peer, self.me).wait_send())
+
+
+def prefix_scratch(shape):
+    layers, members, count, width = shape
+    size = members * count // 8
+    dma = pltpu.SemaphoreType.DMA
+    return [
+        pltpu.VMEM(shape, jnp.float32), pltpu.VMEM((layers, 8, size, width), jnp.float32),
+        pltpu.VMEM((layers, 4, size, width), jnp.float32), dma, dma((layers, 8)), dma((layers, 4)), dma((layers, 8)),
+    ]
 
 
 def gather_sems(layers):
@@ -382,7 +463,7 @@
     place = Place(seqs, tok)
     rows = place.rows
     gather = Gather((w_up, w_down), full, gather_sem) if fast else None
-    place.barrier((gather.row_x, gather.row_y) if fast else ())
+    place.barrier(((gather.row_x, place.wide), (gather.row_y, place.wide)) if fast else ())
     own_bias = bias.at[place.wide]
 
     def load(layer):
@@ -484,7 +565,7 @@
         load(layer)[0].wait()
         for part in (2, 3, 4, 5, 0, 1):
             lanes = pl.ds(part * half, half)
-            made = multiply(low[...], wqkv[:, lanes]) + b_qkv[layer, :, lanes]
+            made = multiply(low[...], wqkv[:, lanes]) + b_qkv[layer : layer + 1, lanes]
             kind, side = part // 2, pl.ds((part % 2) * half, half)
             if kind == 0:
                 q[:, side] = made.astype(jnp.bfloat16) * (1.0 / math.sqrt(width // HEADS))
@@ -517,12 +598,12 @@
 
         def first_norm(at):
             before = low[at].astype(jnp.float32) if layer == 0 else x[at]
-            unit, scale = normalize(before + acc[at] + b_out[layer])
+            unit, scale = normalize(before + acc[at] + b_out[layer : layer + 1])
             unit1[at] = unit.astype(jnp.bfloat16)
             scale1[at] = jnp.broadcast_to(scale, (scale.shape[0], LANES))
-            normed = unit * gains[layer, 0] + shifts[layer, 0]
+            normed = unit * gains[layer, :1] + shifts[layer, :1]
             low[at] = normed.astype(jnp.bfloat16)
-            acc[at] = normed + b_down[layer]
+            acc[at] = normed + b_down[layer : layer + 1]
 
         each(rows // 64, 64, first_norm)
         for copy in kept_norm(layer, 0):
@@ -585,7 +666,7 @@
             unit, scale = normalize(acc[at])
             unit2[at] = unit.astype(jnp.bfloat16)
             scale2[at] = jnp.broadcast_to(scale, (scale.shape[0], LANES))
-            after = unit * gains[layer, 1] + shifts[layer, 1]
+            after = unit * gains[layer, 1:] + shifts[layer, 1:]
             low[at] = after.astype(jnp.bfloat16)
             if layer + 1 < layers:
                 x[at] = after
@@ -646,17 +727,22 @@
 
 
 def backward_kernel(
-    seqs, tok, rim,
+    fast, seqs, tok, rim,
     y_low, cot_in, full, w_qkv, w_out, q_in, k_in, v_in, unit_in, scale_in, slope_in,
     lse, hide, gains, prefix,
     out, grads, prefix_grads,
-    wqkv, wout, q, k, v, unit1, unit2, scale1, scale2, up, down, slope, cot, acc, low, context, made, dk, dv, edge, edge_in, home,
-    load_sem, ffn_sem, out_send, out_recv, out_own, home_send, home_recv, home_own, edge_send, edge_recv, store_sem,
+    wqkv, wout, q, k, v, unit1, unit2, scale1, scale2, up, down, slope, cot, acc, low, context, made, dk, dv, edge, edge_in,
+    load_sem, ffn_sem, out_send, out_recv, out_own, home_send, home_recv, home_own, edge_send, edge_recv,
+    *sums,
 ):
     layers, width = w_qkv.shape[0], w_qkv.shape[1]
     place = Place(seqs, tok)
     rows = place.rows
-    place.barrier(())
+    prefix_sum, prefix_parts = None, prefix_grads
+    if fast:
+        prefix_parts = sums[0]
+        prefix_sum = PrefixSum(place, *sums[:3], prefix_grads, sums[3:])
+    place.barrier(prefix_sum.others() if fast else ())
     spans = slope_in.shape[1]
 
     def out_rows(b):
@@ -673,9 +759,10 @@
         pairs = (
             (unit_in.at[layer, 1], unit2), (scale_in.at[layer, 1], scale2), (unit_in.at[layer, 0], unit1),
             (scale_in.at[layer, 0], scale1), (w_out.at[layer], wout), (q_in.at[layer], q), (k_in.at[layer], k),
-            (v_in.at[layer], v), (w_qkv.at[layer], wqkv),
+            (v_in.at[layer], v),
         )
-        return [pltpu.make_async_copy(src, dst.at[layer % 2], load_sem.at[layer, i]) for i, (src, dst) in enumerate(pairs)]
+        copies = [pltpu.make_async_copy(src, dst.at[layer % 2], load_sem.at[layer, i]) for i, (src, dst) in enumerate(pairs)]
+        return copies + [pltpu.make_async_copy(w_qkv.at[layer], wqkv, load_sem.at[layer, 8])]
 
     def ffn_loads(layer, i):
         slot = lax.rem(i, 2)
@@ -701,14 +788,16 @@
         if layer == order[0]:
             cot_copy.wait()
         if layer > 0:
-            for copy in loads(layer - 1):
+            for copy in loads(layer - 1)[:8]:
                 copy.start()
+        if layer < order[0]:
+            mine[8].start()
         mine[0].wait()
         mine[1].wait()
 
         def second_norm(at):
             grad = cot[at].astype(jnp.float32) if layer == order[0] else acc[at]
-            grad = norm_grad(grad, unit2[here, at].astype(jnp.float32), scale2[here, at, :1], gains[layer, 1])
+            grad = norm_grad(grad, unit2[here, at].astype(jnp.float32), scale2[here, at, :1], gains[layer, 1:])
             acc[at] = grad
             low[at] = grad.astype(jnp.bfloat16)
 
@@ -737,11 +826,13 @@
         mine[3].wait()
 
         def first_norm(at):
-            grad = norm_grad(acc[at], unit1[here, at].astype(jnp.float32), scale1[here, at, :1], gains[layer, 0])
+            grad = norm_grad(acc[at], unit1[here, at].astype(jnp.float32), scale1[here, at, :1], gains[layer, :1])
             acc[at] = grad
             low[at] = grad.astype(jnp.bfloat16)
 
         each(rows // 64, 64, first_norm)
+        if fast and layer + 1 < layers:
+            prefix_sum.last(layer + 1)
         mine[4].wait()
         for part in range(2):
             span = pl.ds(part * half, half)
@@ -753,8 +844,11 @@
         def _(pair):
             attend_back(
                 seqs, tok, rim, pair, q.at[here], k.at[here], v.at[here], prefix.at[layer], hide, lse.at[layer], context,
-                made, dk, dv, prefix_grads.at[layer], 1.0 / math.sqrt(width // HEADS),
+                made, dk, dv, prefix_parts.at[layer], 1.0 / math.sqrt(width // HEADS),
             )
+
+        if fast:
+            prefix_sum.start(layer)
 
         low_edge, high_edge, own_rows = pl.ds(0, rim), pl.ds(rim + rows, rim), pl.ds(rim, rows)
         for member, ref in enumerate((dk, dv)):
@@ -770,7 +864,7 @@
         mine[8].wait()
         for part in range(2):
             span = pl.ds(part * half, half)
-            acc[:, span] += multiply_back(made[:, pl.ds(0, width)], wqkv[here, span, pl.ds(0, width)])
+            acc[:, span] += multiply_back(made[:, pl.ds(0, width)], wqkv[span, pl.ds(0, width)])
             if part == 0:
                 @pl.when(place.part > 0)
                 def _():
@@ -806,27 +900,30 @@
         def _():
             edge_copy(1, place.wide).wait_send()
 
+        if fast:
+            prefix_sum.middle(layer)
         others = pl.ds(width, 2 * width)
         for part in range(2):
             span = pl.ds(part * half, half)
-            acc[:, span] += multiply_back(made[:, others], wqkv[here, span, others])
+            acc[:, span] += multiply_back(made[:, others], wqkv[span, others])
 
     low[...] = acc[...].astype(jnp.bfloat16)
-    home_args = (lambda s: home.at[s], home_send, home_recv)
+    home_args = (lambda s: grads.at[s], home_send, home_recv)
     for b in range(seqs):
         place.send_home_block(b, low.at[pl.ds(b * tok, tok)], *home_args, home_own)
+    if fast:
+        prefix_sum.last(0)
     for s in range(seqs):
         place.got_home(s, low.at[pl.ds(0, tok)], *home_args, home_own)
-        acc[pl.ds(s * tok, tok)] = home[s].astype(jnp.float32)
-        pltpu.make_async_copy(acc.at[pl.ds(s * tok, tok)], grads.at[s], store_sem.at[s]).start()
+        place.got_home(s, out_rows(0), *out_args, out_own)
     place.sent_home(low.at[pl.ds(0, tok)], *home_args)
     place.sent_home(out_rows(0), *out_args)
-    for s in range(seqs):
-        place.got_home(s, out_rows(0), *out_args, out_own)
-        pltpu.make_async_copy(acc.at[pl.ds(s * tok, tok)], grads.at[s], store_sem.at[s]).wait()
-
-
-def backward(y_low, cot, full, w_qkv, w_out, q, k, v, unit, scale, slope, lse, hide, gains, prefix, seqs):
+    if fast:
+        for layer in order:
+            prefix_sum.finish(layer)
+
+
+def backward(fast, y_low, cot, full, w_qkv, w_out, q, k, v, unit, scale, slope, lse, hide, gains, prefix, seqs):
     rows, width = y_low.shape
     layers, rim, tok = w_qkv.shape[0], PAIR_MAX, rows // seqs
     low, full_type = jnp.bfloat16, jnp.float32
@@ -834,20 +931,20 @@
     dma = pltpu.SemaphoreType.DMA
     vmem = pltpu.VMEM
     return pl.pallas_call(
-        functools.partial(backward_kernel, seqs, tok, rim),
-        out_shape=(shape((seqs, tok, width), low), shape((seqs, tok, width), full_type), shape(prefix.shape, full_type)),
+        functools.partial(backward_kernel, fast, seqs, tok, rim),
+        out_shape=(shape((seqs, tok, width), low), shape((seqs, tok, width), low), shape(prefix.shape, full_type)),
         in_specs=[pl.BlockSpec(memory_space=pl.ANY)] * 11 + [pl.BlockSpec(memory_space=pltpu.VMEM)] * 4,
         out_specs=(pl.BlockSpec(memory_space=pl.ANY),) * 2 + (pl.BlockSpec(memory_space=pltpu.VMEM),),
         scratch_shapes=[
-            vmem((2,) + w_qkv.shape[1:], low), vmem((2,) + w_out.shape[1:], low), vmem((2, rows, width), low),
+            vmem(w_qkv.shape[1:], low), vmem((2,) + w_out.shape[1:], low), vmem((2, rows, width), low),
             vmem((2, rows + 2 * rim, width), low), vmem((2, rows + 2 * rim, width), low),
             vmem((2, rows, width), low), vmem((2, rows, width), low), vmem((2, rows, LANES), full_type), vmem((2, rows, LANES), full_type),
             vmem((2, SPAN, width), low), vmem((2, SPAN, width), low), vmem((2, rows, SPAN), low),
             vmem((rows, width), low), vmem((rows, width), full_type), vmem((rows, width), low), vmem((rows, width), low),
             vmem((rows, 3 * width), low), vmem((rows + 2 * rim, width), full_type), vmem((rows + 2 * rim, width), full_type),
-            vmem((layers, 2, rim, 2 * width), low), vmem((layers, 2, rim, 2 * width), low), vmem((seqs, tok, width), low),
-            dma((layers + 1, 9)), dma((2, 3)), dma, dma((seqs,)), dma, dma, dma((seqs,)), dma, dma((layers, 2)), dma((layers, 2)), dma((seqs,)),
-        ],
+            vmem((layers, 2, rim, 2 * width), low), vmem((layers, 2, rim, 2 * width), low),
+            dma((layers + 1, 9)), dma((2, 3)), dma, dma((seqs,)), dma, dma, dma((seqs,)), dma, dma((layers, 2)), dma((layers, 2)),
+        ] + (prefix_scratch(prefix.shape) if fast else []),
         compiler_params=pltpu.CompilerParams(collective_id=1, has_side_effects=True, vmem_limit_bytes=67043328),
     )(y_low, cot, full, w_qkv, w_out, q, k, v, unit, scale, slope, lse, hide, gains, prefix)
 
@@ -885,15 +982,16 @@
     full_in = w_up
     if not fast:
         full_in = jnp.stack([lax.all_gather(w, "wide", axis=1, tiled=True) for w in (w_up, w_down)], axis=1)
-    gains, shifts = norm_gain[:, :, None], norm_bias[:, :, None]
     y_low, cot, full, q, k, v, unit, scale, slope, lse = forward(
-        fast, tokens, cotangent, w_qkv, w_out, w_up, w_down, full_in, hide, b_qkv[:, None], b_out[:, None], gains, shifts,
-        b_up.astype(jnp.float32).reshape(1, -1), b_down[:, None], prefix,
+        fast, tokens, cotangent, w_qkv, w_out, w_up, w_down, full_in, hide, b_qkv, b_out, norm_gain, norm_bias,
+        b_up.astype(jnp.float32).reshape(1, -1), b_down, prefix,
     )
     output, grads, prefix_grads = backward(
-        y_low, cot, full if fast else full_in, w_qkv, w_out, q, k, v, unit, scale, slope, lse, hide, gains, prefix, seqs
+        fast, y_low, cot, full if fast else full_in, w_qkv, w_out, q, k, v, unit, scale, slope, lse, hide, norm_gain, prefix, seqs
     )
-    return output, grads, lax.psum(prefix_grads, ("rows", "wide"))
+    if not fast:
+        prefix_grads = lax.psum(prefix_grads, ("rows", "wide"))
+    return output, grads.astype(jnp.float32), prefix_grads
 
 
 def solution(mesh):

time: 464 us -> 324 us (0.70)
  waiting for transfers between devices: 127 us -> 0 us
  between operations: 14.5 us -> 1.14 us
  Pallas kernels: 300 us -> 310 us
  local copies, waits for them, and re-layouts: 13.6 us -> 4.28 us
    psum x1 -> x0, waiting for transfers between devices: 127 us -> none  [local(): return (output, grads, lax.psum(prefix_grads, ('rows', 'wide')))]
    pallas_call x1, Pallas kernels: 138 us -> 148 us  [backward(): pl.pallas_call(functools.partial(backward_kernel, fast, seqs, tok, rim),...]
    broadcast_in_dim x5 -> x0, local copies, waits for them, and re-layouts: 6.61 us -> none  [the longest x2 2.66 us: local(): gains, shifts = (norm_gain[:, :, None], norm_bias[:, :, None])]
  transfers between devices with their start and end apart: 1 -> 0, of which waited for: 1 -> 0; matrix products, arithmetic and copies ran while one was open for 0% -> 0% of each run, Pallas kernels for 0% -> 0%
where the time goes in v3:
time: 324 us; the launch traced here: 321 us
  Pallas kernels  310 us (96%)
  other arithmetic  4.89 us (2%)
  local copies, waits for them, and re-layouts  4.28 us (1%)
    pallas_call x1, Pallas kernels, forward(): pl.pallas_call(functools.partial(forward_kernel, fast, seqs, tok, rim), o...  162 us
    pallas_call x1, Pallas kernels, backward(): pl.pallas_call(functools.partial(backward_kernel, fast, seqs, tok, rim),...  148 us

profile of v3, /device:TPU:9, one launch (start us, length us, event | category | flops | bytes accessed | tf_op | source)
XLA Modules:
  0.0 320.7 jit_solution(13617732392435481304)
XLA Ops:
  0.6 0.8 fusion.5
  1.5 0.7 convert_bitcast_fusion
  2.2 0.6 copy.17
  2.8 0.9 fusion
  3.7 0.2 compare_select_fusion.2
  3.8 0.2 compare_select_fusion
  4.0 0.9 pad_maximum_fusion.hide
  4.9 162.2 %shard_map.157 = (bf16[512,1024]{1,0:T(8,128)(2,1)}, bf16[512,1024]{1,0:T(8,128)(2,1)}, bf16[2,2,4096,1024]{3,2,1,0:T(8,128)(2,1)}, bf16[2,512,1024]{2,1,0:T(8,1...) custom-call(bf16[4,128,1024]{2,1,0:T(8,128)(2,1)} %tokens.1, ...), custom_call_target="tpu_custom_call" | custom-call | tf_op jit(solution)/shard_map/pallas_call | solution.py:704
  167.2 148.2 %shard_map.158 = (bf16[4,128,1024]{2,1,0:T(8,128)(2,1)}, bf16[4,128,1024]{2,1,0:T(8,128)(2,1)}, f32[2,2,64,1024]{3,2,1,0:T(8,128)}) custom-call(bf16[512,1024]{1,0:T(8,128)(2,1)} %get-tuple-element.16.y_low, bf16[512,1024]{1,0:T(8,128)(2,1)} %get-tuple-element.17.cot_in, bf16[2,2,4096,1024]{3,2,1,0:T(8,128)(2,1)} %get-tuple-element.18.full, ...), custom_call_target="tpu_custom_call" | custom-call | tf_op jit(solution)/shard_map/pallas_call | solution.py:933
  315.4 0.0 copy-start.1
  315.4 0.0 copy-start
  315.4 2.9 convert_element_type.4
  318.3 0.0 copy-done.1
  318.3 1.0 copy.20
  319.3 0.0 copy-done
  319.3 1.0 copy.21
Async XLA Ops:
  315.4 3.0 copy-start.1
  315.4 3.9 %copy-start = (f32[2,2,64,1024]{3,2,1,0:T(8,128)S(1)}, f32[2,2,64,1024]{3,2,1,0:T(8,128)}, u32[]{:S(2)}) copy-start(f32[2,2,64,1024]{3,2,1,0:T(8,128)} %get-tuple-element.46) | copy-start | bytes 3145732

commit v4 on v3

--- a/solution.py
+++ b/solution.py
@@ -296,6 +296,21 @@
             self.copy(unit, unit, self.ys.at[layer, member, step, side], "y").start()
             self.copy(unit, unit, self.cz.at[layer, member, step, side], "core").start()
 
+    def on_first(self, layer, _):
+        self.on_z(layer, 0)
+
+        @pl.when((self.z > 0) & (self.z < 3))
+        def _():
+            self.on_z(layer, 1)
+
+    def on_second(self, layer, _):
+        self.on_z(layer, 1 + jnp.minimum(self.z, 1) * jnp.minimum(3 - self.z, 1))
+
+    def on_third(self, layer, _):
+        @pl.when((self.z == 0) | (self.z == 3))
+        def _():
+            self.on_z(layer, 2)
+
     def on_xy(self, layer, i):
         step, side, origin = self.slot(i)
         for member in range(2):
@@ -490,27 +505,42 @@
 
     tok_args = (lambda s: tokens.at[s], lambda b: low.at[pl.ds(pl.multiple_of(b * tok, tok), tok)], tok_send, tok_recv, tok_own)
     cot_args = (lambda s: cotangent.at[s], lambda b: cot_out.at[pl.ds(pl.multiple_of(b * tok, tok), tok)], cot_send, cot_recv, cot_own)
-    events = []
+    events = {}
     if fast:
-        gather.on_z(0, 0)
+        gather.on_first(0, 0)
         place.send_out(*tok_args)
-        gather.on_z(0, 1)
+        gather.on_second(0, 0)
         gather.on_xy(0, 0)
-        gather.start_z(1)
-        gather.start_core(1)
-        gather.on_z(0, 2)
-        gather.on_xy(0, 1)
-        events = [
-            (gather.on_d, 0, 0), (gather.on_xy, 0, 2), (gather.on_z, 1, 0), (gather.on_d, 0, 1), (gather.on_d, 0, 2),
-            (gather.on_z, 1, 1), (gather.on_z, 1, 2), (gather.on_xy, 1, 0),
-        ]
+        events = {
+            (0, "queries"): [(gather.on_xy, 0, 1)],
+            (0, "pair", 1): [(gather.on_third, 0, 0)],
+            (0, "pair", 4): [(gather.on_first, 1, 0), (gather.on_d, 0, 0)],
+            (0, "projected"): [(gather.on_d, 0, 1)],
+            (0, "normed"): [(gather.on_xy, 0, 2)],
+            (0, "step", 1): [(gather.on_core, 0, 0)],
+            (0, "step", 2): [(gather.on_second, 1, 0), (gather.on_core, 0, 1), (gather.on_d, 0, 2)],
+            (0, "step", 3): [(gather.on_core, 0, 2)],
+            (0, "done"): [(gather.on_xy, 1, 0), (gather.on_third, 1, 0)],
+            (1, "pair", 4): [(gather.on_xy, 1, 1)],
+            (1, "projected"): [(gather.on_d, 1, 0)],
+            (1, "normed"): [(gather.on_d, 1, 1)],
+            (1, "step", 1): [(gather.on_xy, 1, 2), (gather.on_core, 1, 0)],
+            (1, "step", 2): [(gather.on_d, 1, 2), (gather.on_core, 1, 1)],
+            (1, "step", 3): [(gather.on_core, 1, 2)],
+        }
     else:
         place.send_out(*tok_args)
 
-    def tick(count=1):
-        for _ in range(min(count, len(events))):
-            event, layer, i = events.pop(0)
+    def tick(*when):
+        for event, layer, i in events.get(when, ()):
             event(layer, i)
+
+    def loop_tick(layer, kind, index, count):
+        for n in range(count):
+            if (layer, kind, n) in events:
+                @pl.when(index == n)
+                def _():
+                    tick(layer, kind, n)
 
     blank = jnp.zeros((rim, width), jnp.bfloat16)
 
@@ -525,6 +555,9 @@
         v[pl.ds(rim + rows, rim)] = blank
 
     place.got_out(*tok_args)
+    if fast:
+        gather.start_z(1)
+        gather.start_core(1)
 
     def halo_copy(layer, member, side, wide):
         ref = (k, v)[member]
@@ -572,29 +605,27 @@
             else:
                 (k, v)[kind - 1][pl.ds(rim, rows), side] = made.astype(jnp.bfloat16)
             if part == 5:
-                tick()
                 halos(lambda *at: halo_copy(layer, *at).start(), True)
         if layer + 1 < layers:
             load(layer + 1)[0].start()
-        tick()
+        tick(layer, "queries")
         halos(lambda *at: got_halo(layer, *at), False)
         halos(lambda *at: halo_copy(layer, *at).wait_send(), True)
         for copy in kept(layer):
             copy.start()
 
-        for first in (0, 4):
-            @pl.loop(first, first + 4)
-            def _(pair):
-                attend(seqs, tok, rim, pair, q, k, v, prefix.at[layer], hide, context, lse.at[layer])
-
-            tick()
+        @pl.loop(0, width // LANES)
+        def _(pair):
+            attend(seqs, tok, rim, pair, q, k, v, prefix.at[layer], hide, context, lse.at[layer])
+            loop_tick(layer, "pair", pair, width // LANES)
+
         load(layer)[1].wait()
         for part in range(2):
             lanes = pl.ds(part * half, half)
             acc[:, lanes] = multiply(context[...], wout[:, lanes])
         if layer + 1 < layers:
             load(layer + 1)[1].start()
-        tick()
+        tick(layer, "projected")
 
         def first_norm(at):
             before = low[at].astype(jnp.float32) if layer == 0 else x[at]
@@ -608,7 +639,7 @@
         each(rows // 64, 64, first_norm)
         for copy in kept_norm(layer, 0):
             copy.start()
-        tick()
+        tick(layer, "normed")
         if layer == 0:
             pltpu.make_async_copy(b_up, own_bias, bias_own).wait()
             place.others(lambda other: got_bias(other).wait_recv())
@@ -627,16 +658,7 @@
                 def _():
                     gather.on_own(layer)
 
-                @pl.when(i > 0)
-                def _():
-                    if layer == 1:
-                        @pl.when(i > 1)
-                        def _():
-                            gather.on_xy(1, i - 1)
-
-                        gather.on_d(1, i - 1)
-                    gather.on_core(layer, i - 1)
-
+                loop_tick(layer, "step", i, full.shape[2] // SPAN)
                 origin = gather.slot(jnp.maximum(i - 1, 0))[2]
                 started = jnp.minimum(i, 1)
                 spot = started * origin + (1 - started) * gather.z
@@ -676,7 +698,7 @@
             copy.start()
         if layer == 0:
             place.send_out(*cot_args)
-            tick(2)
+            tick(0, "done")
     last = [pltpu.make_async_copy(low, y_low, store_sem.at[7]), pltpu.make_async_copy(lse, lse_out, store_sem.at[8])]
     for copy in last:
         copy.start()

time: 324 us -> 292 us (0.901)
  Pallas kernels: 310 us -> 282 us
    pallas_call x1, Pallas kernels: 148 us -> 124 us  [backward(): pl.pallas_call(functools.partial(backward_kernel, fast, seqs, tok, rim),...]
    pallas_call x1, Pallas kernels: 162 us -> 158 us  [forward(): pl.pallas_call(functools.partial(forward_kernel, fast, seqs, tok, rim), o...]
where the time goes in v4:
time: 292 us
  Pallas kernels  282 us (97%)
  other arithmetic  4.89 us (2%)
  local copies, waits for them, and re-layouts  4.28 us (1%)
    pallas_call x1, Pallas kernels, forward(): pl.pallas_call(functools.partial(forward_kernel, fast, seqs, tok, rim), o...  158 us
    pallas_call x1, Pallas kernels, backward(): pl.pallas_call(functools.partial(backward_kernel, fast, seqs, tok, rim),...  124 us

profile of v4, /device:TPU:9, one launch (start us, length us, event | category | flops | bytes accessed | tf_op | source)
XLA Modules:
  0.0 291.7 jit_solution(14764578830645438326)
XLA Ops:
  0.6 0.8 fusion.5
  1.5 0.7 convert_bitcast_fusion
  2.2 0.6 copy.17
  2.8 0.9 fusion
  3.7 0.2 compare_select_fusion.2
  3.8 0.2 compare_select_fusion
  4.0 0.9 pad_maximum_fusion.hide
  4.9 157.6 %shard_map.157 = (bf16[512,1024]{1,0:T(8,128)(2,1)}, bf16[512,1024]{1,0:T(8,128)(2,1)}, bf16[2,2,4096,1024]{3,2,1,0:T(8,128)(2,1)}, bf16[2,512,1024]{2,1,0:T(8,1...) custom-call(bf16[4,128,1024]{2,1,0:T(8,128)(2,1)} %tokens.1, ...), custom_call_target="tpu_custom_call" | custom-call | tf_op jit(solution)/shard_map/pallas_call | solution.py:726
  162.5 124.3 %shard_map.158 = (bf16[4,128,1024]{2,1,0:T(8,128)(2,1)}, bf16[4,128,1024]{2,1,0:T(8,128)(2,1)}, f32[2,2,64,1024]{3,2,1,0:T(8,128)}) custom-call(bf16[512,1024]{1,0:T(8,128)(2,1)} %get-tuple-element.16.y_low, bf16[512,1024]{1,0:T(8,128)(2,1)} %get-tuple-element.17.cot_in, bf16[2,2,4096,1024]{3,2,1,0:T(8,128)(2,1)} %get-tuple-element.18.full, ...), custom_call_target="tpu_custom_call" | custom-call | tf_op jit(solution)/shard_map/pallas_call | solution.py:955
  286.8 0.0 copy-start.1
  286.8 0.0 copy-start
  286.8 2.9 %convert_element_type.4 = f32[4,128,1024]{2,1,0:T(8,128)} convert(bf16[4,128,1024]{2,1,0:T(8,128)(2,1)} %get-tuple-element.27) | non-fusion elementwise | flops 524288 | bytes 3145728 | tf_op jit(solution)/shard_map/convert_element_type | solution.py:1016
  289.7 0.0 copy-done.1
  289.7 1.0 copy.20
  290.7 0.0 copy-done
  290.7 1.0 copy.21
Async XLA Ops:
  286.8 3.0 %copy-start.1 = (bf16[4,128,1024]{2,1,0:T(8,128)(2,1)S(1)}, bf16[4,128,1024]{2,1,0:T(8,128)(2,1)}, u32[]{:S(2)}) copy-start(bf16[4,128,1024]{2,1,0:T(8,128)(2,1)} %get-tuple-element.44) | copy-start | bytes 3145732
  286.8 3.9 %copy-start = (f32[2,2,64,1024]{3,2,1,0:T(8,128)S(1)}, f32[2,2,64,1024]{3,2,1,0:T(8,128)}, u32[]{:S(2)}) copy-start(f32[2,2,64,1024]{3,2,1,0:T(8,128)} %get-tuple-element.46) | copy-start | bytes 3145732

commit v5 on v4

--- a/solution.py
+++ b/solution.py
@@ -43,59 +43,58 @@
 
 def attend(blocks, rows, rim, pair, q_ref, k_ref, v_ref, prefix_ref, hide_ref, context_ref, lse_ref):
     lanes = pl.ds(pl.multiple_of(pair * 128, 128), 128)
-    prefix_keys, prefix_values = prefix_ref[0, :, lanes], prefix_ref[1, :, lanes]
     for block in range(blocks):
         here = pl.ds(block * rows, rows)
         window = pl.ds(block * rows, rows + 2 * rim)
         queries = two_heads(q_ref[here, lanes])
         hide = hide_ref[block]
-        fixed = multiply_back(prefix_keys, queries)
-        near = multiply_back(k_ref[window, lanes], queries) + jnp.concatenate([hide, hide], axis=1)
-        top = jnp.maximum(jnp.max(fixed, axis=0, keepdims=True), jnp.max(near, axis=0, keepdims=True))
-        fixed, near = jnp.exp(fixed - top), jnp.exp(near - top)
-        total = jnp.sum(fixed, axis=0, keepdims=True) + jnp.sum(near, axis=0, keepdims=True)
+        keys = jnp.concatenate([prefix_ref[0, :, lanes], k_ref[window, lanes]], axis=0)
+        values = jnp.concatenate([prefix_ref[1, :, lanes], v_ref[window, lanes]], axis=0)
+        scores = multiply_back(keys, queries) + jnp.concatenate([hide, hide], axis=1)
+        top = jnp.max(scores, axis=0, keepdims=True)
+        scores = jnp.exp(scores - top)
+        total = jnp.sum(scores, axis=0, keepdims=True)
         share = 1.0 / total
-        columns = multiply_first(prefix_values, fixed.astype(jnp.bfloat16)) + multiply_first(
-            v_ref[window, lanes], near.astype(jnp.bfloat16)
-        )
+        columns = multiply_first(values, scores.astype(jnp.bfloat16))
         context_ref[here, lanes] = own_heads(columns * share).astype(jnp.bfloat16)
         lse_ref[pair * blocks + block] = top + jnp.log(total)
 
 
-def attend_back(blocks, rows, rim, pair, q_ref, k_ref, v_ref, prefix_ref, hide_ref, lse_ref, grad_ref, dq_ref, dk_ref, dv_ref, dp_ref, scale):
+def attend_back(
+    blocks, rows, rim, pair, q_ref, k_ref, v_ref, prefix_ref, hide_ref, lse_ref, context_ref, grad_ref, dq_ref, dk_ref, dv_ref, dp_ref, scale
+):
     lanes = pl.ds(pl.multiple_of(pair * 128, 128), 128)
-    prefix_keys, prefix_values = prefix_ref[0, :, lanes], prefix_ref[1, :, lanes]
     for block in range(blocks):
         here = pl.ds(block * rows, rows)
+        grad = grad_ref[here, lanes]
+        queries, grads = two_heads(q_ref[here, lanes]), two_heads(grad)
+        shared = (grad.astype(jnp.float32) * context_ref[here, lanes].astype(jnp.float32)).T
+        half = shared.shape[0] // 2
+        dots = jnp.concatenate(
+            [jnp.sum(shared[:half], axis=0, keepdims=True), jnp.sum(shared[half:], axis=0, keepdims=True)], axis=1
+        )
+        lse = lse_ref[pair * blocks + block]
         window = pl.ds(block * rows, rows + 2 * rim)
-        queries = two_heads(q_ref[here, lanes])
-        grads = two_heads(grad_ref[here, lanes])
+        keys = jnp.concatenate([prefix_ref[0, :, lanes], k_ref[window, lanes]], axis=0)
+        values = jnp.concatenate([prefix_ref[1, :, lanes], v_ref[window, lanes]], axis=0)
         hide = hide_ref[block]
-        keys, values = k_ref[window, lanes], v_ref[window, lanes]
-        lse = lse_ref[pair * blocks + block]
-        fixed = jnp.exp(multiply_back(prefix_keys, queries) - lse)
-        near = jnp.exp(multiply_back(keys, queries) + jnp.concatenate([hide, hide], axis=1) - lse)
-        grad_fixed = multiply_back(prefix_values, grads)
-        grad_near = multiply_back(values, grads)
-        dots = jnp.sum(fixed * grad_fixed, axis=0, keepdims=True) + jnp.sum(near * grad_near, axis=0, keepdims=True)
-        grad_fixed = (fixed * (grad_fixed - dots)).astype(jnp.bfloat16)
-        grad_near = (near * (grad_near - dots)).astype(jnp.bfloat16)
-        fixed, near = fixed.astype(jnp.bfloat16), near.astype(jnp.bfloat16)
-        columns = multiply_first(prefix_keys, grad_fixed) + multiply_first(keys, grad_near)
+        probs = jnp.exp(multiply_back(keys, queries) + (jnp.concatenate([hide, hide], axis=1) - lse))
+        grad_scores = (probs * (multiply_back(values, grads) - dots)).astype(jnp.bfloat16)
+        new_values = multiply(probs.astype(jnp.bfloat16), grads)
+        new_keys = multiply(grad_scores, queries)
+        columns = multiply_first(keys, grad_scores)
+        count = prefix_ref.shape[1]
+        old, fresh = pl.ds(block * rows, 2 * rim), pl.ds(block * rows + 2 * rim, rows)
+        if block == 0:
+            dk_ref[window, lanes], dv_ref[window, lanes] = new_keys[count:], new_values[count:]
+            dp_ref[0, :, lanes], dp_ref[1, :, lanes] = new_keys[:count], new_values[:count]
+        else:
+            dk_ref[old, lanes] += new_keys[count : count + 2 * rim]
+            dv_ref[old, lanes] += new_values[count : count + 2 * rim]
+            dk_ref[fresh, lanes], dv_ref[fresh, lanes] = new_keys[count + 2 * rim :], new_values[count + 2 * rim :]
+            dp_ref[0, :, lanes] += new_keys[:count]
+            dp_ref[1, :, lanes] += new_values[:count]
         dq_ref[here, lanes] = (own_heads(columns) * scale).astype(jnp.bfloat16)
-        new_keys, new_values = multiply(grad_near, queries), multiply(near, grads)
-        fixed_keys, fixed_values = multiply(grad_fixed, queries), multiply(fixed, grads)
-        old = pl.ds(block * rows, 2 * rim)
-        fresh = pl.ds(block * rows + 2 * rim, rows)
-        if block == 0:
-            dk_ref[window, lanes], dv_ref[window, lanes] = new_keys, new_values
-            dp_ref[0, :, lanes], dp_ref[1, :, lanes] = fixed_keys, fixed_values
-        else:
-            dk_ref[old, lanes] += new_keys[: 2 * rim]
-            dv_ref[old, lanes] += new_values[: 2 * rim]
-            dk_ref[fresh, lanes], dv_ref[fresh, lanes] = new_keys[2 * rim :], new_values[2 * rim :]
-            dp_ref[0, :, lanes] += fixed_keys
-            dp_ref[1, :, lanes] += fixed_values
 
 
 def gelu_pair(values):
@@ -468,7 +467,7 @@
     fast, seqs, tok, rim,
     tokens, cotangent, w_qkv, w_out, w_up, w_down, full_in,
     hide, b_qkv, b_out, gains, shifts, b_up, b_down, prefix,
-    y_low, cot_out, full_out, q_out, k_out, v_out, unit_out, scale_out, slope_out, lse_out,
+    y_low, cot_out, full_out, q_out, k_out, v_out, unit_out, scale_out, slope_out, lse_out, context_out,
     full, wqkv, wout, x, low, acc, q, k, v, halo, context, slope, unit1, unit2, scale1, scale2, lse, bias,
     load_sem, store_sem, slope_sem, full_sem, tok_send, tok_recv, tok_own, cot_send, cot_recv, cot_own,
     halo_send, halo_recv, bias_send, bias_recv, bias_own,
@@ -512,19 +511,19 @@
         gather.on_second(0, 0)
         gather.on_xy(0, 0)
         events = {
-            (0, "queries"): [(gather.on_xy, 0, 1)],
-            (0, "pair", 1): [(gather.on_third, 0, 0)],
+            (0, "queries"): [(gather.on_third, 0, 0)],
+            (0, "pair", 1): [(gather.on_xy, 0, 1)],
             (0, "pair", 4): [(gather.on_first, 1, 0), (gather.on_d, 0, 0)],
+            (0, "pair", 7): [(gather.on_xy, 0, 2)],
             (0, "projected"): [(gather.on_d, 0, 1)],
-            (0, "normed"): [(gather.on_xy, 0, 2)],
+            (0, "normed"): [(gather.on_second, 1, 0)],
             (0, "step", 1): [(gather.on_core, 0, 0)],
-            (0, "step", 2): [(gather.on_second, 1, 0), (gather.on_core, 0, 1), (gather.on_d, 0, 2)],
-            (0, "step", 3): [(gather.on_core, 0, 2)],
-            (0, "done"): [(gather.on_xy, 1, 0), (gather.on_third, 1, 0)],
-            (1, "pair", 4): [(gather.on_xy, 1, 1)],
+            (0, "step", 2): [(gather.on_xy, 1, 0), (gather.on_core, 0, 1), (gather.on_d, 0, 2)],
+            (0, "step", 3): [(gather.on_core, 0, 2), (gather.on_third, 1, 0)],
+            (1, "pair", 2): [(gather.on_xy, 1, 1)],
             (1, "projected"): [(gather.on_d, 1, 0)],
-            (1, "normed"): [(gather.on_d, 1, 1)],
-            (1, "step", 1): [(gather.on_xy, 1, 2), (gather.on_core, 1, 0)],
+            (1, "normed"): [(gather.on_d, 1, 1), (gather.on_xy, 1, 2)],
+            (1, "step", 1): [(gather.on_core, 1, 0)],
             (1, "step", 2): [(gather.on_d, 1, 2), (gather.on_core, 1, 1)],
             (1, "step", 3): [(gather.on_core, 1, 2)],
         }
@@ -583,6 +582,9 @@
             for i, (src, dst) in enumerate(((q, q_out), (k, k_out), (v, v_out)))
         ]
 
+    def kept_context(layer):
+        return [pltpu.make_async_copy(context, context_out.at[layer], store_sem.at[9])]
+
     def kept_norm(layer, which):
         unit, scale = ((unit1, scale1), (unit2, scale2))[which]
         return [
@@ -593,7 +595,7 @@
     half = width // 2
     for layer in range(layers):
         if layer > 0:
-            for copy in kept(layer - 1) + kept_norm(layer - 1, 0) + kept_norm(layer - 1, 1):
+            for copy in kept(layer - 1) + kept_context(layer - 1) + kept_norm(layer - 1, 0) + kept_norm(layer - 1, 1):
                 copy.wait()
         load(layer)[0].wait()
         for part in (2, 3, 4, 5, 0, 1):
@@ -619,6 +621,8 @@
             attend(seqs, tok, rim, pair, q, k, v, prefix.at[layer], hide, context, lse.at[layer])
             loop_tick(layer, "pair", pair, width // LANES)
 
+        for copy in kept_context(layer):
+            copy.start()
         load(layer)[1].wait()
         for part in range(2):
             lanes = pl.ds(part * half, half)
@@ -705,7 +709,7 @@
     place.sent_out(*tok_args)
     place.got_out(*cot_args)
     place.sent_out(*cot_args)
-    for copy in last + kept(layers - 1) + kept_norm(layers - 1, 0) + kept_norm(layers - 1, 1):
+    for copy in last + kept(layers - 1) + kept_context(layers - 1) + kept_norm(layers - 1, 0) + kept_norm(layers - 1, 1):
         copy.wait()
     if fast:
         gather.drain(layers)
@@ -730,9 +734,10 @@
             shape((layers, rows, width), low), shape((layers, rows + 2 * rim, width), low),
             shape((layers, rows + 2 * rim, width), low), shape((layers, 2, rows, width), low),
             shape((layers, 2, rows, LANES), full_type), shape((layers, spans, rows, SPAN), low), shape(scores, full_type),
+            shape((layers, rows, width), low),
         ),
         in_specs=[pl.BlockSpec(memory_space=pl.ANY)] * 7 + [pl.BlockSpec(memory_space=pltpu.VMEM)] * 8,
-        out_specs=(pl.BlockSpec(memory_space=pl.ANY),) * 10,
+        out_specs=(pl.BlockSpec(memory_space=pl.ANY),) * 11,
         scratch_shapes=[
             pltpu.VMEM((layers, 2, units, width), low), pltpu.VMEM(w_qkv.shape[1:], low), pltpu.VMEM(w_out.shape[1:], low),
             pltpu.VMEM((rows, width), full_type), pltpu.VMEM((rows, width), low), pltpu.VMEM((rows, width), full_type),
@@ -741,7 +746,7 @@
             pltpu.VMEM((rows, width), low), pltpu.VMEM((rows, width), low),
             pltpu.VMEM((rows, LANES), full_type), pltpu.VMEM((rows, LANES), full_type),
             pltpu.VMEM(scores, full_type), pltpu.VMEM((wides,) + b_up.shape, full_type),
-            dma((2,)), dma((9,)), dma((2,)), dma((layers,)), dma, dma((seqs,)), dma, dma, dma((seqs,)), dma,
+            dma((2,)), dma((10,)), dma((2,)), dma((layers,)), dma, dma((seqs,)), dma, dma, dma((seqs,)), dma,
             dma((2, 2)), dma((layers, 2, 2)), dma, dma((wides,)), dma,
         ] + (gather_sems(layers) if fast else []),
         compiler_params=pltpu.CompilerParams(collective_id=0, has_side_effects=True, vmem_limit_bytes=67043328),
@@ -750,10 +755,10 @@
 
 def backward_kernel(
     fast, seqs, tok, rim,
-    y_low, cot_in, full, w_qkv, w_out, q_in, k_in, v_in, unit_in, scale_in, slope_in,
+    y_low, cot_in, full, w_qkv, w_out, q_in, k_in, v_in, unit_in, scale_in, slope_in, context_in,
     lse, hide, gains, prefix,
     out, grads, prefix_grads,
-    wqkv, wout, q, k, v, unit1, unit2, scale1, scale2, up, down, slope, cot, acc, low, context, made, dk, dv, edge, edge_in,
+    wqkv, wout, q, k, v, unit1, unit2, scale1, scale2, up, down, slope, cot, acc, low, context, made, dk, dv, edge, edge_in, saved,
     load_sem, ffn_sem, out_send, out_recv, out_own, home_send, home_recv, home_own, edge_send, edge_recv,
     *sums,
 ):
@@ -784,7 +789,10 @@
             (v_in.at[layer], v),
         )
         copies = [pltpu.make_async_copy(src, dst.at[layer % 2], load_sem.at[layer, i]) for i, (src, dst) in enumerate(pairs)]
-        return copies + [pltpu.make_async_copy(w_qkv.at[layer], wqkv, load_sem.at[layer, 8])]
+        return copies + [
+            pltpu.make_async_copy(w_qkv.at[layer], wqkv, load_sem.at[layer, 8]),
+            pltpu.make_async_copy(context_in.at[layer], saved, load_sem.at[layer, 9]),
+        ]
 
     def ffn_loads(layer, i):
         slot = lax.rem(i, 2)
@@ -814,6 +822,7 @@
                 copy.start()
         if layer < order[0]:
             mine[8].start()
+            mine[9].start()
         mine[0].wait()
         mine[1].wait()
 
@@ -824,6 +833,8 @@
             low[at] = grad.astype(jnp.bfloat16)
 
         each(rows // 64, 64, second_norm)
+        if fast and layer + 1 < layers:
+            prefix_sum.middle(layer + 1)
 
         @pl.loop(0, spans)
         def _(i):
@@ -859,13 +870,13 @@
         for part in range(2):
             span = pl.ds(part * half, half)
             context[:, span] = multiply_back(low[...], wout[here, span]).astype(jnp.bfloat16)
-        for copy in mine[5:8]:
+        for copy in mine[5:8] + mine[9:]:
             copy.wait()
 
         @pl.loop(0, width // LANES)
         def _(pair):
             attend_back(
-                seqs, tok, rim, pair, q.at[here], k.at[here], v.at[here], prefix.at[layer], hide, lse.at[layer], context,
+                seqs, tok, rim, pair, q.at[here], k.at[here], v.at[here], prefix.at[layer], hide, lse.at[layer], saved, context,
                 made, dk, dv, prefix_parts.at[layer], 1.0 / math.sqrt(width // HEADS),
             )
 
@@ -922,17 +933,20 @@
         def _():
             edge_copy(1, place.wide).wait_send()
 
-        if fast:
-            prefix_sum.middle(layer)
         others = pl.ds(width, 2 * width)
-        for part in range(2):
-            span = pl.ds(part * half, half)
-            acc[:, span] += multiply_back(made[:, others], wqkv[span, others])
-
-    low[...] = acc[...].astype(jnp.bfloat16)
+        if layer > 0:
+            for part in range(2):
+                span = pl.ds(part * half, half)
+                acc[:, span] += multiply_back(made[:, others], wqkv[span, others])
+
     home_args = (lambda s: grads.at[s], home_send, home_recv)
-    for b in range(seqs):
-        place.send_home_block(b, low.at[pl.ds(b * tok, tok)], *home_args, home_own)
+    for part in range(2):
+        at = pl.ds(part * (rows // 2), rows // 2)
+        low[at] = (acc[at] + multiply_back(made[at, others], wqkv[:, others])).astype(jnp.bfloat16)
+        for b in range(part * (seqs // 2), (part + 1) * (seqs // 2)):
+            place.send_home_block(b, low.at[pl.ds(b * tok, tok)], *home_args, home_own)
+        if fast and part == 0:
+            prefix_sum.middle(0)
     if fast:
         prefix_sum.last(0)
     for s in range(seqs):
@@ -945,7 +959,7 @@
             prefix_sum.finish(layer)
 
 
-def backward(fast, y_low, cot, full, w_qkv, w_out, q, k, v, unit, scale, slope, lse, hide, gains, prefix, seqs):
+def backward(fast, y_low, cot, full, w_qkv, w_out, q, k, v, unit, scale, slope, context, lse, hide, gains, prefix, seqs):
     rows, width = y_low.shape
     layers, rim, tok = w_qkv.shape[0], PAIR_MAX, rows // seqs
     low, full_type = jnp.bfloat16, jnp.float32
@@ -955,7 +969,7 @@
     return pl.pallas_call(
         functools.partial(backward_kernel, fast, seqs, tok, rim),
         out_shape=(shape((seqs, tok, width), low), shape((seqs, tok, width), low), shape(prefix.shape, full_type)),
-        in_specs=[pl.BlockSpec(memory_space=pl.ANY)] * 11 + [pl.BlockSpec(memory_space=pltpu.VMEM)] * 4,
+        in_specs=[pl.BlockSpec(memory_space=pl.ANY)] * 12 + [pl.BlockSpec(memory_space=pltpu.VMEM)] * 4,
         out_specs=(pl.BlockSpec(memory_space=pl.ANY),) * 2 + (pl.BlockSpec(memory_space=pltpu.VMEM),),
         scratch_shapes=[
             vmem(w_qkv.shape[1:], low), vmem((2,) + w_out.shape[1:], low), vmem((2, rows, width), low),
@@ -964,11 +978,11 @@
             vmem((2, SPAN, width), low), vmem((2, SPAN, width), low), vmem((2, rows, SPAN), low),
             vmem((rows, width), low), vmem((rows, width), full_type), vmem((rows, width), low), vmem((rows, width), low),
             vmem((rows, 3 * width), low), vmem((rows + 2 * rim, width), full_type), vmem((rows + 2 * rim, width), full_type),
-            vmem((layers, 2, rim, 2 * width), low), vmem((layers, 2, rim, 2 * width), low),
-            dma((layers + 1, 9)), dma((2, 3)), dma, dma((seqs,)), dma, dma, dma((seqs,)), dma, dma((layers, 2)), dma((layers, 2)),
+            vmem((layers, 2, rim, 2 * width), low), vmem((layers, 2, rim, 2 * width), low), vmem((rows, width), low),
+            dma((layers + 1, 10)), dma((2, 3)), dma, dma((seqs,)), dma, dma, dma((seqs,)), dma, dma((layers, 2)), dma((layers, 2)),
         ] + (prefix_scratch(prefix.shape) if fast else []),
         compiler_params=pltpu.CompilerParams(collective_id=1, has_side_effects=True, vmem_limit_bytes=67043328),
-    )(y_low, cot, full, w_qkv, w_out, q, k, v, unit, scale, slope, lse, hide, gains, prefix)
+    )(y_low, cot, full, w_qkv, w_out, q, k, v, unit, scale, slope, context, lse, hide, gains, prefix)
 
 
 def local(
@@ -1001,15 +1015,16 @@
             for b in range(seqs)
         ]
     )
+    hide = jnp.pad(hide, ((0, 0), (prefix.shape[2], 0), (0, 0)))
     full_in = w_up
     if not fast:
         full_in = jnp.stack([lax.all_gather(w, "wide", axis=1, tiled=True) for w in (w_up, w_down)], axis=1)
-    y_low, cot, full, q, k, v, unit, scale, slope, lse = forward(
+    y_low, cot, full, q, k, v, unit, scale, slope, lse, context = forward(
         fast, tokens, cotangent, w_qkv, w_out, w_up, w_down, full_in, hide, b_qkv, b_out, norm_gain, norm_bias,
         b_up.astype(jnp.float32).reshape(1, -1), b_down, prefix,
     )
     output, grads, prefix_grads = backward(
-        fast, y_low, cot, full if fast else full_in, w_qkv, w_out, q, k, v, unit, scale, slope, lse, hide, norm_gain, prefix, seqs
+        fast, y_low, cot, full if fast else full_in, w_qkv, w_out, q, k, v, unit, scale, slope, context, lse, hide, norm_gain, prefix, seqs
     )
     if not fast:
         prefix_grads = lax.psum(prefix_grads, ("rows", "wide"))

time: 292 us -> 267 us (0.914)
  Pallas kernels: 282 us -> 256 us
    pallas_call x1, Pallas kernels: 124 us -> 103 us  [backward(): pl.pallas_call(functools.partial(backward_kernel, fast, seqs, tok, rim),...]
    pallas_call x1, Pallas kernels: 158 us -> 153 us  [forward(): pl.pallas_call(functools.partial(forward_kernel, fast, seqs, tok, rim), o...]
where the time goes in v5:
time: 267 us; the launch traced here: 266 us
  Pallas kernels  256 us (96%)
  other arithmetic  4.94 us (2%)
  local copies, waits for them, and re-layouts  4.28 us (2%)
    pallas_call x1, Pallas kernels, forward(): pl.pallas_call(functools.partial(forward_kernel, fast, seqs, tok, rim), o...  153 us
    pallas_call x1, Pallas kernels, backward(): pl.pallas_call(functools.partial(backward_kernel, fast, seqs, tok, rim),...  103 us

profile of v5, /device:TPU:9, one launch (start us, length us, event | category | flops | bytes accessed | tf_op | source)
XLA Modules:
  0.0 265.8 jit_solution(5890460748566508310)
XLA Ops:
  0.6 0.8 fusion.5
  1.5 0.7 convert_bitcast_fusion
  2.2 0.6 copy.17
  2.8 0.9 fusion
  3.7 0.2 compare_select_fusion.2
  3.8 0.2 compare_select_fusion
  4.0 1.0 select_maximum_fusion.hide
  5.0 153.0 %shard_map.157 = (bf16[512,1024]{1,0:T(8,128)(2,1)}, bf16[512,1024]{1,0:T(8,128)(2,1)}, bf16[2,2,4096,1024]{3,2,1,0:T(8,128)(2,1)}, bf16[2,512,1024]{2,1,0:T(8,1...) custom-call(bf16[4,128,1024]{2,1,0:T(8,128)(2,1)} %tokens.1, ...), custom_call_target="tpu_custom_call" | custom-call | tf_op jit(solution)/shard_map/pallas_call | solution.py:730
  158.0 102.8 %shard_map.158 = (bf16[4,128,1024]{2,1,0:T(8,128)(2,1)}, bf16[4,128,1024]{2,1,0:T(8,128)(2,1)}, f32[2,2,64,1024]{3,2,1,0:T(8,128)}) custom-call(bf16[512,1024]{1,0:T(8,128)(2,1)} %get-tuple-element.17.y_low, bf16[512,1024]{1,0:T(8,128)(2,1)} %get-tuple-element.18.cot_in, bf16[2,2,4096,1024]{3,2,1,0:T(8,128)(2,1)} %get-tuple-element.19.full, ...), custom_call_target="tpu_custom_call" | custom-call | tf_op jit(solution)/shard_map/pallas_call | solution.py:969
  260.9 0.0 copy-start.1
  260.9 0.0 copy-start
  260.9 2.9 %convert_element_type.6 = f32[4,128,1024]{2,1,0:T(8,128)} convert(bf16[4,128,1024]{2,1,0:T(8,128)(2,1)} %get-tuple-element.29) | non-fusion elementwise | flops 524288 | bytes 3145728 | tf_op jit(solution)/shard_map/convert_element_type | solution.py:1031
  263.8 0.0 copy-done.1
  263.8 1.0 copy.20
  264.8 0.0 copy-done
  264.8 1.0 copy.21
Async XLA Ops:
  260.9 3.0 %copy-start.1 = (bf16[4,128,1024]{2,1,0:T(8,128)(2,1)S(1)}, bf16[4,128,1024]{2,1,0:T(8,128)(2,1)}, u32[]{:S(2)}) copy-start(bf16[4,128,1024]{2,1,0:T(8,128)(2,1)} %get-tuple-element.46) | copy-start | bytes 3145732
  260.9 3.9 %copy-start = (f32[2,2,64,1024]{3,2,1,0:T(8,128)S(1)}, f32[2,2,64,1024]{3,2,1,0:T(8,128)}, u32[]{:S(2)}) copy-start(f32[2,2,64,1024]{3,2,1,0:T(8,128)} %get-tuple-element.48) | copy-start | bytes 3145732

commit v6 on v5

--- a/solution.py
+++ b/solution.py
@@ -216,6 +216,27 @@
             pltpu.make_async_copy(part, target(s), own).wait()
 
 
+def fill_hide(place, rim, segments, hide):
+    count = hide.shape[1] - place.tok - 2 * rim
+    base = place.part * place.rows
+
+    def ids(start):
+        start = pl.multiple_of(start, LANES)
+        rows = segments[:, pl.ds(start, LANES)].astype(jnp.float32)
+        here = lax.broadcasted_iota(jnp.int32, rows.shape, 0) == place.seq
+        return jnp.sum(jnp.where(here, rows, 0.0), axis=0, keepdims=True)
+
+    for b in range(place.seqs):
+        hide[b, pl.ds(0, count)] = jnp.zeros((count, place.tok), jnp.float32)
+        own = ids(base + b * place.tok)
+        for chunk in range((place.tok + 2 * rim) // LANES):
+            start = base + b * place.tok - rim + chunk * LANES
+            safe = jnp.clip(start, 0, segments.shape[1] - LANES)
+            keys = jnp.where(start == safe, ids(safe), -1.0)
+            keys = jnp.broadcast_to(keys, (LANES, LANES)).T
+            hide[b, pl.ds(count + chunk * LANES, LANES)] = jnp.where(keys == own, 0.0, -1e30)
+
+
 class Gather:
     def __init__(self, shards, full, sems):
         self.shards = shards
@@ -466,9 +487,9 @@
 def forward_kernel(
     fast, seqs, tok, rim,
     tokens, cotangent, w_qkv, w_out, w_up, w_down, full_in,
-    hide, b_qkv, b_out, gains, shifts, b_up, b_down, prefix,
+    segments, b_qkv, b_out, gains, shifts, b_up, b_down, prefix,
     y_low, cot_out, full_out, q_out, k_out, v_out, unit_out, scale_out, slope_out, lse_out, context_out,
-    full, wqkv, wout, x, low, acc, q, k, v, halo, context, slope, unit1, unit2, scale1, scale2, lse, bias,
+    full, wqkv, wout, x, low, acc, q, k, v, halo, context, slope, unit1, unit2, scale1, scale2, lse, bias, hide,
     load_sem, store_sem, slope_sem, full_sem, tok_send, tok_recv, tok_own, cot_send, cot_recv, cot_own,
     halo_send, halo_recv, bias_send, bias_recv, bias_own,
     *gather_sem,
@@ -520,9 +541,10 @@
             (0, "step", 1): [(gather.on_core, 0, 0)],
             (0, "step", 2): [(gather.on_xy, 1, 0), (gather.on_core, 0, 1), (gather.on_d, 0, 2)],
             (0, "step", 3): [(gather.on_core, 0, 2), (gather.on_third, 1, 0)],
-            (1, "pair", 2): [(gather.on_xy, 1, 1)],
+            (1, "queries"): [(gather.on_xy, 1, 1)],
+            (1, "pair", 7): [(gather.on_xy, 1, 2)],
             (1, "projected"): [(gather.on_d, 1, 0)],
-            (1, "normed"): [(gather.on_d, 1, 1), (gather.on_xy, 1, 2)],
+            (1, "normed"): [(gather.on_d, 1, 1)],
             (1, "step", 1): [(gather.on_core, 1, 0)],
             (1, "step", 2): [(gather.on_d, 1, 2), (gather.on_core, 1, 1)],
             (1, "step", 3): [(gather.on_core, 1, 2)],
@@ -553,6 +575,7 @@
         k[pl.ds(rim + rows, rim)] = blank
         v[pl.ds(rim + rows, rim)] = blank
 
+    fill_hide(place, rim, segments, hide)
     place.got_out(*tok_args)
     if fast:
         gather.start_z(1)
@@ -717,7 +740,7 @@
             pltpu.make_async_copy(full.at[layer], full_out.at[layer], full_sem.at[layer]).wait()
 
 
-def forward(fast, tokens, cotangent, w_qkv, w_out, w_up, w_down, full_in, hide, b_qkv, b_out, gains, shifts, b_up, b_down, prefix):
+def forward(fast, tokens, cotangent, w_qkv, w_out, w_up, w_down, full_in, segments, b_qkv, b_out, gains, shifts, b_up, b_down, prefix):
     seqs, tok, width = tokens.shape
     layers, rim, rows = w_qkv.shape[0], PAIR_MAX, seqs * tok
     wides = lax.axis_size("wide")
@@ -746,19 +769,20 @@
             pltpu.VMEM((rows, width), low), pltpu.VMEM((rows, width), low),
             pltpu.VMEM((rows, LANES), full_type), pltpu.VMEM((rows, LANES), full_type),
             pltpu.VMEM(scores, full_type), pltpu.VMEM((wides,) + b_up.shape, full_type),
+            pltpu.VMEM((seqs, prefix.shape[2] + tok + 2 * rim, tok), full_type),
             dma((2,)), dma((10,)), dma((2,)), dma((layers,)), dma, dma((seqs,)), dma, dma, dma((seqs,)), dma,
             dma((2, 2)), dma((layers, 2, 2)), dma, dma((wides,)), dma,
         ] + (gather_sems(layers) if fast else []),
         compiler_params=pltpu.CompilerParams(collective_id=0, has_side_effects=True, vmem_limit_bytes=67043328),
-    )(tokens, cotangent, w_qkv, w_out, w_up, w_down, full_in, hide, b_qkv, b_out, gains, shifts, b_up, b_down, prefix)
+    )(tokens, cotangent, w_qkv, w_out, w_up, w_down, full_in, segments, b_qkv, b_out, gains, shifts, b_up, b_down, prefix)
 
 
 def backward_kernel(
     fast, seqs, tok, rim,
     y_low, cot_in, full, w_qkv, w_out, q_in, k_in, v_in, unit_in, scale_in, slope_in, context_in,
-    lse, hide, gains, prefix,
+    lse, segments, gains, prefix,
     out, grads, prefix_grads,
-    wqkv, wout, q, k, v, unit1, unit2, scale1, scale2, up, down, slope, cot, acc, low, context, made, dk, dv, edge, edge_in, saved,
+    wqkv, wout, q, k, v, unit1, unit2, scale1, scale2, up, down, slope, cot, acc, low, context, made, dk, dv, edge, edge_in, saved, hide,
     load_sem, ffn_sem, out_send, out_recv, out_own, home_send, home_recv, home_own, edge_send, edge_recv,
     *sums,
 ):
@@ -812,6 +836,7 @@
     for copy in loads(order[0])[2:]:
         copy.start()
     half = width // 2
+    fill_hide(place, rim, segments, hide)
     for layer in order:
         here = layer % 2
         mine = loads(layer)
@@ -959,7 +984,7 @@
             prefix_sum.finish(layer)
 
 
-def backward(fast, y_low, cot, full, w_qkv, w_out, q, k, v, unit, scale, slope, context, lse, hide, gains, prefix, seqs):
+def backward(fast, y_low, cot, full, w_qkv, w_out, q, k, v, unit, scale, slope, context, lse, segments, gains, prefix, seqs):
     rows, width = y_low.shape
     layers, rim, tok = w_qkv.shape[0], PAIR_MAX, rows // seqs
     low, full_type = jnp.bfloat16, jnp.float32
@@ -979,10 +1004,11 @@
             vmem((rows, width), low), vmem((rows, width), full_type), vmem((rows, width), low), vmem((rows, width), low),
             vmem((rows, 3 * width), low), vmem((rows + 2 * rim, width), full_type), vmem((rows + 2 * rim, width), full_type),
             vmem((layers, 2, rim, 2 * width), low), vmem((layers, 2, rim, 2 * width), low), vmem((rows, width), low),
+            vmem((seqs, prefix.shape[2] + tok + 2 * rim, tok), full_type),
             dma((layers + 1, 10)), dma((2, 3)), dma, dma((seqs,)), dma, dma, dma((seqs,)), dma, dma((layers, 2)), dma((layers, 2)),
         ] + (prefix_scratch(prefix.shape) if fast else []),
         compiler_params=pltpu.CompilerParams(collective_id=1, has_side_effects=True, vmem_limit_bytes=67043328),
-    )(y_low, cot, full, w_qkv, w_out, q, k, v, unit, scale, slope, context, lse, hide, gains, prefix)
+    )(y_low, cot, full, w_qkv, w_out, q, k, v, unit, scale, slope, context, lse, segments, gains, prefix)
 
 
 def local(
@@ -1001,30 +1027,17 @@
     prefix,
     cotangent,
 ):
-    seqs, tok, width = tokens.shape
-    layers, rim, rows = w_qkv.shape[0], PAIR_MAX, seqs * tok
-    wides = lax.axis_size("wide")
-    fast = wides == 8 and lax.axis_size("rows") == 4
-    parts = wides // seqs
-    wide = lax.axis_index("wide")
-    ids = jnp.pad(segments, ((0, 0), (rim, rim)), constant_values=-1)
-    ids = lax.dynamic_slice(ids, (lax.div(wide, parts), lax.rem(wide, parts) * rows), (1, rows + 2 * rim))[0]
-    hide = jnp.stack(
-        [
-            jnp.where(ids[b * tok : b * tok + tok + 2 * rim, None] == ids[None, b * tok + rim : b * tok + rim + tok], 0.0, -1e30)
-            for b in range(seqs)
-        ]
-    )
-    hide = jnp.pad(hide, ((0, 0), (prefix.shape[2], 0), (0, 0)))
+    seqs = tokens.shape[0]
+    fast = lax.axis_size("wide") == 8 and lax.axis_size("rows") == 4
     full_in = w_up
     if not fast:
         full_in = jnp.stack([lax.all_gather(w, "wide", axis=1, tiled=True) for w in (w_up, w_down)], axis=1)
     y_low, cot, full, q, k, v, unit, scale, slope, lse, context = forward(
-        fast, tokens, cotangent, w_qkv, w_out, w_up, w_down, full_in, hide, b_qkv, b_out, norm_gain, norm_bias,
+        fast, tokens, cotangent, w_qkv, w_out, w_up, w_down, full_in, segments, b_qkv, b_out, norm_gain, norm_bias,
         b_up.astype(jnp.float32).reshape(1, -1), b_down, prefix,
     )
     output, grads, prefix_grads = backward(
-        fast, y_low, cot, full if fast else full_in, w_qkv, w_out, q, k, v, unit, scale, slope, context, lse, hide, norm_gain, prefix, seqs
+        fast, y_low, cot, full if fast else full_in, w_qkv, w_out, q, k, v, unit, scale, slope, context, lse, segments, norm_gain, prefix, seqs
     )
     if not fast:
         prefix_grads = lax.psum(prefix_grads, ("rows", "wide"))

time: 267 us -> 263 us (0.985)
  no operation moved by 1% of the time
where the time goes in v6:
time: 263 us; the launch traced here: 262 us
  Pallas kernels  255 us (97%)
  other arithmetic  3.62 us (1%)
    pallas_call x1, Pallas kernels, forward(): pl.pallas_call(functools.partial(forward_kernel, fast, seqs, tok, rim), o...  152 us
    pallas_call x1, Pallas kernels, backward(): pl.pallas_call(functools.partial(backward_kernel, fast, seqs, tok, rim),...  103 us

profile of v6, /device:TPU:9, one launch (start us, length us, event | category | flops | bytes accessed | tf_op | source)
XLA Modules:
  0.0 262.0 jit_solution(730807281992086686)
XLA Ops:
  0.6 0.7 convert_bitcast_fusion
  1.3 0.6 copy.17
  1.9 152.1 %shard_map.157 = (bf16[512,1024]{1,0:T(8,128)(2,1)}, bf16[512,1024]{1,0:T(8,128)(2,1)}, bf16[2,2,4096,1024]{3,2,1,0:T(8,128)(2,1)}, bf16[2,512,1024]{2,1,0:T(8,1...) custom-call(bf16[4,128,1024]{2,1,0:T(8,128)(2,1)} %tokens.1, ...), custom_call_target="tpu_custom_call" | custom-call | tf_op jit(solution)/shard_map/pallas_call | solution.py:753
  154.1 103.0 %shard_map.158 = (bf16[4,128,1024]{2,1,0:T(8,128)(2,1)}, bf16[4,128,1024]{2,1,0:T(8,128)(2,1)}, f32[2,2,64,1024]{3,2,1,0:T(8,128)}) custom-call(bf16[512,1024]{1,0:T(8,128)(2,1)} %get-tuple-element.17.y_low, bf16[512,1024]{1,0:T(8,128)(2,1)} %get-tuple-element.18.cot_in, bf16[2,2,4096,1024]{3,2,1,0:T(8,128)(2,1)} %get-tuple-element.19.full, ...), custom_call_target="tpu_custom_call" | custom-call | tf_op jit(solution)/shard_map/pallas_call | solution.py:994
  257.1 0.0 copy-start.1
  257.1 0.0 copy-start
  257.1 2.9 %convert_element_type.4 = f32[4,128,1024]{2,1,0:T(8,128)} convert(bf16[4,128,1024]{2,1,0:T(8,128)(2,1)} %get-tuple-element.29) | non-fusion elementwise | flops 524288 | bytes 3145728 | tf_op jit(solution)/shard_map/convert_element_type | solution.py:1044
  260.0 0.0 copy-done.1
  260.0 1.0 copy.20
  261.0 0.0 copy-done
  261.0 1.0 copy.21
Async XLA Ops:
  257.1 3.0 %copy-start.1 = (bf16[4,128,1024]{2,1,0:T(8,128)(2,1)S(1)}, bf16[4,128,1024]{2,1,0:T(8,128)(2,1)}, u32[]{:S(2)}) copy-start(bf16[4,128,1024]{2,1,0:T(8,128)(2,1)} %get-tuple-element.34) | copy-start | bytes 3145732
  257.1 3.9 %copy-start = (f32[2,2,64,1024]{3,2,1,0:T(8,128)S(1)}, f32[2,2,64,1024]{3,2,1,0:T(8,128)}, u32[]{:S(2)}) copy-start(f32[2,2,64,1024]{3,2,1,0:T(8,128)} %get-tuple-element.36) | copy-start | bytes 3145732

commit v7 on v6

--- a/solution.py
+++ b/solution.py
@@ -396,8 +396,8 @@
 
 
 class PrefixSum:
-    def __init__(self, place, parts, inbox, planes, total, sems):
-        self.parts, self.inbox, self.planes, self.total = parts, inbox, planes, total
+    def __init__(self, place, parts, rounded, inbox, planes, total, sems):
+        self.parts, self.rounded, self.inbox, self.planes, self.total = parts, rounded, inbox, planes, total
         self.send_sem, self.in_sem, self.plane_sem, self.total_sem = sems
         self.row = place.row
         self.z, self.core = lax.div(place.wide, 2), lax.rem(place.wide, 2)
@@ -423,7 +423,7 @@
 
     def in_copy(self, layer, peer, origin):
         return self.copy(
-            self.piece(self.parts, layer, peer), self.inbox.at[layer, origin], self.in_sem.at[layer, origin],
+            self.piece(self.rounded, layer, peer), self.inbox.at[layer, origin], self.in_sem.at[layer, origin],
             lax.div(peer, 2), self.z * 2 + lax.rem(peer, 2),
         )
 
@@ -441,13 +441,14 @@
             body(lax.rem(self.z + step, 4))
 
     def start(self, layer):
+        self.rounded[layer] = self.parts[layer].astype(jnp.bfloat16)
         self.peers(lambda peer: self.in_copy(layer, peer, self.me).start())
 
     def middle(self, layer):
         self.peers(lambda peer: self.in_copy(layer, self.me, peer).wait_recv())
         value = self.piece(self.parts, layer, self.me)[...]
         for step in range(1, 8):
-            value += self.inbox[layer, lax.rem(self.me + step, 8)]
+            value += self.inbox[layer, lax.rem(self.me + step, 8)].astype(jnp.float32)
         self.planes[layer, self.z] = value
         self.planes_others(lambda z: self.plane_copy(layer, z, self.z).start())
 
@@ -471,7 +472,7 @@
     size = members * count // 8
     dma = pltpu.SemaphoreType.DMA
     return [
-        pltpu.VMEM(shape, jnp.float32), pltpu.VMEM((layers, 8, size, width), jnp.float32),
+        pltpu.VMEM(shape, jnp.float32), pltpu.VMEM(shape, jnp.bfloat16), pltpu.VMEM((layers, 8, size, width), jnp.bfloat16),
         pltpu.VMEM((layers, 4, size, width), jnp.float32), dma, dma((layers, 8)), dma((layers, 4)), dma((layers, 8)),
     ]
 
@@ -792,7 +793,7 @@
     prefix_sum, prefix_parts = None, prefix_grads
     if fast:
         prefix_parts = sums[0]
-        prefix_sum = PrefixSum(place, *sums[:3], prefix_grads, sums[3:])
+        prefix_sum = PrefixSum(place, *sums[:4], prefix_grads, sums[4:])
     place.barrier(prefix_sum.others() if fast else ())
     spans = slope_in.shape[1]
 

time: 263 us -> 262 us (level)
  no operation moved by 1% of the time
where the time goes in v7:
time: 262 us; the launch traced here: 261 us
  Pallas kernels  254 us (97%)
  other arithmetic  3.62 us (1%)
    pallas_call x1, Pallas kernels, forward(): pl.pallas_call(functools.partial(forward_kernel, fast, seqs, tok, rim), o...  152 us
    pallas_call x1, Pallas kernels, backward(): pl.pallas_call(functools.partial(backward_kernel, fast, seqs, tok, rim),...  102 us

profile of v7, /device:TPU:9, one launch (start us, length us, event | category | flops | bytes accessed | tf_op | source)
XLA Modules:
  0.0 261.0 jit_solution(14137689673959994356)
XLA Ops:
  0.6 0.7 convert_bitcast_fusion
  1.3 0.6 copy.17
  1.9 152.1 %shard_map.157 = (bf16[512,1024]{1,0:T(8,128)(2,1)}, bf16[512,1024]{1,0:T(8,128)(2,1)}, bf16[2,2,4096,1024]{3,2,1,0:T(8,128)(2,1)}, bf16[2,512,1024]{2,1,0:T(8,1...) custom-call(bf16[4,128,1024]{2,1,0:T(8,128)(2,1)} %tokens.1, ...), custom_call_target="tpu_custom_call" | custom-call | tf_op jit(solution)/shard_map/pallas_call | solution.py:754
  154.1 102.0 %shard_map.158 = (bf16[4,128,1024]{2,1,0:T(8,128)(2,1)}, bf16[4,128,1024]{2,1,0:T(8,128)(2,1)}, f32[2,2,64,1024]{3,2,1,0:T(8,128)}) custom-call(bf16[512,1024]{1,0:T(8,128)(2,1)} %get-tuple-element.17.y_low, bf16[512,1024]{1,0:T(8,128)(2,1)} %get-tuple-element.18.cot_in, bf16[2,2,4096,1024]{3,2,1,0:T(8,128)(2,1)} %get-tuple-element.19.full, ...), custom_call_target="tpu_custom_call" | custom-call | tf_op jit(solution)/shard_map/pallas_call | solution.py:995
  256.1 0.0 copy-start.1
  256.1 0.0 copy-start
  256.1 2.9 %convert_element_type.4 = f32[4,128,1024]{2,1,0:T(8,128)} convert(bf16[4,128,1024]{2,1,0:T(8,128)(2,1)} %get-tuple-element.29) | non-fusion elementwise | flops 524288 | bytes 3145728 | tf_op jit(solution)/shard_map/convert_element_type | solution.py:1045
  259.0 0.0 copy-done.1
  259.0 1.0 copy.20
  260.0 0.0 copy-done
  260.0 1.0 copy.21
Async XLA Ops:
  256.1 3.0 %copy-start.1 = (bf16[4,128,1024]{2,1,0:T(8,128)(2,1)S(1)}, bf16[4,128,1024]{2,1,0:T(8,128)(2,1)}, u32[]{:S(2)}) copy-start(bf16[4,128,1024]{2,1,0:T(8,128)(2,1)} %get-tuple-element.34) | copy-start | bytes 3145732
  256.1 3.9 %copy-start = (f32[2,2,64,1024]{3,2,1,0:T(8,128)S(1)}, f32[2,2,64,1024]{3,2,1,0:T(8,128)}, u32[]{:S(2)}) copy-start(f32[2,2,64,1024]{3,2,1,0:T(8,128)} %get-tuple-element.36) | copy-start | bytes 3145732
